TPU v7x, 128 devices: a whole 4x4x4 slice. The times are simulated.
128 devices in a mesh: gx: 8 (over z_lo, y), gy: 16 (over z_hi, x, core).
Axes of the slice: x: 4, y: 4, z: 4 (z_hi: 2, z_lo: 2; z = z_hi * 2 + z_lo), core: 2. Of those that a mesh axis runs over, the one named last changes fastest.
Arguments:
- u_wind: float32 [60, 512, 2048], P(None, 'gx', 'gy'), may hold values from -6 to 6
- v_wind: float32 [60, 512, 2048], P(None, 'gx', 'gy'), may hold values from -6 to 6
- w_wind: float32 [60, 512, 2048], P(None, 'gx', 'gy'), may hold values from -3 to 3
- pressure: float32 [60, 512, 2048], P(None, 'gx', 'gy'), may hold values from -6 to 6
- vert_coef: float32 [512, 2048], P('gx', 'gy'), may hold values from 0.2 to 5
- we_slab: float32 [2, 3, 60, 5, 2048], P(None, None, None, None, ('gy', 'gx')), may hold values from -8 to 8
- sn_slab: float32 [2, 3, 60, 5, 512], P(None, None, None, None, ('gx', 'gy')), may hold values from -8 to 8
- relax_width: int32 [512, 2048], P('gx', 'gy'), may hold values from 2 to 5
Outputs:
- u_out: float32 [60, 512, 2048], P(None, 'gx', 'gy')
- v_out: float32 [60, 512, 2048], P(None, 'gx', 'gy')
- w_out: float32 [60, 512, 2048], P(None, 'gx', 'gy')
- p_out: float32 [60, 512, 2048], P(None, 'gx', 'gy')
All inputs are finite; a program needn't handle non-finite values.
Results may differ from a plain program's by a relative error of at most 0.0001.
Values sent between devices are 32-bit elements; how exact they have to be, the bound alone decides.
No kernel may reach another device: no remote copies, remote signals or barrier semaphores. Data moves between devices by JAX's collectives and lax.ppermute only.
A program may use at most 192 MiB of HBM per device.

v0:
```python
import jax
import jax.numpy as jnp
from jax import lax
from jax.sharding import PartitionSpec as P

SUBSTEPS = 6


accel = 0.3
spread = 0.3
buoyancy = 0.5


def in_order(pieces, dim):
    pieces = jnp.moveaxis(pieces, 0, dim)
    dims = pieces.shape
    return pieces.reshape(*dims[:dim], dims[dim] * dims[dim + 1], *dims[dim + 2 :])


def sent_to_all(value, axis):
    size = lax.axis_size(axis)
    return lax.all_to_all(
        jnp.broadcast_to(value[None], (size, *value.shape)), axis, 0, 0, tiled=True
    )


def gather_directly(value, axis, dim):
    return in_order(sent_to_all(value, axis), dim)


def passed_along(block, axis, distance):
    devices = range(lax.axis_size(axis))
    route = [(i - distance, i) for i in devices if i - distance in devices]
    return lax.ppermute(block, axis, route)


def factorize(coef, levels):
    cees = []
    denoms = []
    prev_c = jnp.zeros_like(coef)
    for level in range(levels):
        denom = 1.0 + 2.0 * coef + coef * prev_c
        next_c = -coef / denom
        cees.append(next_c)
        denoms.append(denom)
        prev_c = next_c
    return (cees, denoms)


def tri_solve(coef, factors, rhs):
    cees, denoms = factors
    levels = rhs.shape[0]
    dees = []
    prev_d = jnp.zeros_like(coef)
    for level in range(levels):
        next_d = (rhs[level] + coef * prev_d) / denoms[level]
        dees.append(next_d)
        prev_d = next_d
    solved = [None] * levels
    above = jnp.zeros_like(coef)
    for level in range(levels - 1, -1, -1):
        above = dees[level] - cees[level] * above
        solved[level] = above
    return jnp.stack(solved, axis=0)


def blend(field, rows_k, cols_k, xpos, ypos, nx_total, ny_total, rate):
    band = rows_k.shape[2]
    size_x = field.shape[1]
    size_y = field.shape[2]
    west = jnp.pad(rows_k[0], ((0, 0), (0, size_x - band), (0, 0)))
    east = jnp.pad(rows_k[1][:, ::-1, :], ((0, 0), (size_x - band, 0), (0, 0)))
    south = jnp.pad(jnp.transpose(cols_k[0], (0, 2, 1)), ((0, 0), (0, 0), (0, size_y - band)))
    north = jnp.pad(
        jnp.transpose(cols_k[1][:, ::-1, :], (0, 2, 1)), ((0, 0), (0, 0), (size_y - band, 0))
    )
    weight_w = jnp.maximum(rate - xpos[:, None], 0.0) / rate
    weight_e = jnp.maximum(rate - (nx_total - 1.0 - xpos)[:, None], 0.0) / rate
    weight_s = jnp.maximum(rate - ypos[None, :], 0.0) / rate
    weight_n = jnp.maximum(rate - (ny_total - 1.0 - ypos)[None, :], 0.0) / rate
    field = field + weight_w[None] * (west - field)
    field = field + weight_e[None] * (east - field)
    field = field + weight_s[None] * (south - field)
    field = field + weight_n[None] * (north - field)
    return field


def column_part(u_new, v_new, west_u, south_v, w_old, p_old, coef, factors):
    diverge = u_new - west_u + (v_new - south_v)
    sectioned = p_old - spread * diverge
    above_q = jnp.concatenate([sectioned[1:], jnp.zeros_like(sectioned[:1])], axis=0)
    rhs = w_old + buoyancy * (sectioned - above_q)
    w_new = tri_solve(coef, factors, rhs)
    below_w = jnp.concatenate([jnp.zeros_like(w_new[:1]), w_new[:-1]], axis=0)
    p_new = sectioned - buoyancy * (w_new - below_w)
    return (w_new, p_new)


def per_device(u_wind, v_wind, w_wind, pressure, vert_coef, we_slab, sn_slab, relax_width):
    edge_vals = gather_directly(we_slab, "gx", 4)
    side_vals = lax.all_gather(sn_slab, "gy", axis=4, tiled=True)
    size_x = pressure.shape[1]
    size_y = pressure.shape[2]
    levels = pressure.shape[0]
    col_index = lax.axis_index("gx")
    row_index = lax.axis_index("gy")
    xpos = (col_index * size_x + jnp.arange(size_x, dtype=jnp.int32)).astype(jnp.float32)
    ypos = (row_index * size_y + jnp.arange(size_y, dtype=jnp.int32)).astype(jnp.float32)
    nx_total = float(size_x * lax.axis_size("gx"))
    ny_total = float(size_y * lax.axis_size("gy"))
    rate = relax_width.astype(jnp.float32)
    fields = []
    for index, field in enumerate((u_wind, v_wind, pressure)):
        fields.append(
            blend(
                field,
                edge_vals[:, index],
                side_vals[:, index],
                xpos,
                ypos,
                nx_total,
                ny_total,
                rate,
            )
        )
    u_now, v_now, p_now = fields
    w_now = w_wind
    factors = factorize(vert_coef, levels)
    for step in range(SUBSTEPS):
        east_rim = passed_along(p_now[:, :1, :], "gx", -1)
        north_rim = passed_along(p_now[:, :, :1], "gy", -1)
        east_p = jnp.concatenate([p_now[:, 1:, :], east_rim], axis=1)
        north_p = jnp.concatenate([p_now[:, :, 1:], north_rim], axis=2)
        u_now = u_now - accel * (east_p - p_now)
        v_now = v_now - accel * (north_p - p_now)
        west_rim = passed_along(u_now[:, -1:, :], "gx", 1)
        south_rim = passed_along(v_now[:, :, -1:], "gy", 1)
        west_u = jnp.concatenate([west_rim, u_now[:, :-1, :]], axis=1)
        south_v = jnp.concatenate([south_rim, v_now[:, :, :-1]], axis=2)
        w_now, p_now = column_part(u_now, v_now, west_u, south_v, w_now, p_now, vert_coef, factors)
    return (u_now, v_now, w_now, p_now)


def solution(mesh):
    placed = (
        P(None, "gx", "gy"),
        P(None, "gx", "gy"),
        P(None, "gx", "gy"),
        P(None, "gx", "gy"),
        P("gx", "gy"),
        P(None, None, None, None, ("gy", "gx")),
        P(None, None, None, None, ("gx", "gy")),
        P("gx", "gy"),
    )
    return jax.shard_map(
        per_device,
        mesh=mesh,
        in_specs=placed,
        out_specs=(
            P(None, "gx", "gy"),
            P(None, "gx", "gy"),
            P(None, "gx", "gy"),
            P(None, "gx", "gy"),
        ),
        check_vma=False,
    )
```

profile of v0, /device:TPU:88, one launch (start us, length us, event | category | flops | bytes accessed | tf_op | source)
XLA Modules:
  0.0 398.4 jit_solution(15434892561254640329)
XLA Ops:
  1.8 4.1 %reshape.57 = f32[8,1,28800]{2,1,0:T(1,128)} reshape(f32[8,2,3,5,16,60]{5,4,3,2,1,0:T(8,128)S(1)} %broadcast_bitcast_fusion) | data formatting | bytes 1843200
  5.9 5.7 %all-to-all-start = ((f32[8,1,28800]{2,1,0:T(1,128)}), f32[8,1,28800]{2,1,0:T(1,128)S(1)}, u32[]{:S(2)}, u32[]{:S(2)}) async-start(f32[8,1,28800]{2,1,0:T(1,128)} %reshape.57), calls=%async_computation | async-start | bytes 1843200 | tf_op jit(solution)/shard_map/all_to_all | solution.py:22
  11.6 24.6 %all_gather.3 = f32[2,3,60,5,64]{2,0,3,1,4:T(2,128)S(1)} all-gather(f32[2,3,60,5,4]{2,0,3,1,4:T(2,128)S(1)} %copy.2894), channel_id=1, replica_groups=mesh['gx'=8,'gy'=16] {'gy'}, dimensions={4}, use_global_device_ids=true | all-gather | bytes 489600 | tf_op jit(solution)/shard_map/all_gather | solution.py:101
  46.1 4.0 %reduce = f32[8,28800]{1,0:T(8,128)} reduce(f32[8,1,28800]{2,1,0:T(1,128)S(1)} %all-to-all-done, f32[]{:T(128)} %broadcast.4793), dimensions={1}, to_apply=%all_to_all.3.reduce_sub_computation | reduce | bytes 1843204 | tf_op jit(solution)/shard_map/all_to_all | solution.py:22
  50.1 4.1 %reshape.58 = f32[8,2,3,5,16,60]{5,4,3,2,1,0:T(8,128)S(1)} reshape(f32[8,28800]{1,0:T(8,128)} %reduce) | data formatting | bytes 1843200
  56.0 3.8 multiply_add_fusion.6
  73.3 4.1 %rev.23 = f32[60,5,64]{1,2,0:T(8,128)} reverse(f32[60,5,64]{1,2,0:T(8,128)} %bitcast.4723), dimensions={1} | reverse | bytes 153600 | tf_op jit(solution)/shard_map/rev | solution.py:75
  80.0 4.1 %rev.19 = f32[60,5,64]{1,2,0:T(8,128)} reverse(f32[60,5,64]{1,2,0:T(8,128)} %bitcast.4724), dimensions={1} | reverse | bytes 153600 | tf_op jit(solution)/shard_map/rev | solution.py:75
  94.7 7.6 %fusion.6 = (f32[60,64,128]{2,1,0:T(8,128)S(1)}, f32[60,64,128]{2,1,0:T(8,128)S(1)}) fusion(f32[60,64,128]{2,1,0:T(8,128)S(1)} %multiply_add_fusion.6, f32[60,64,1]{2,1,0:T(8,128)} %copy.2906, f32[60,64,127]{2,1,0:T(8,128)} %slice.1762, f32[60,64,5]{2,1,0:T(8,128)} %bitcast.4718, f32[60,64,5]{2,1,0:T(8,128)} %bitcast.4717, f32[60,5,128]{2,1,0:T(8,128)S(1)} %rev.22, ...), kind=kLoop, calls=%fused_computation.9 | loop fusion | flops 15728640 | bytes 14815232 | tf_op jit(solution)/shard_map/sub | solution.py:135
  103.5 5.4 %collective-permute-start.1 = (f32[60,1,128]{2,1,0:T(1,128)S(1)}, f32[60,1,128]{2,1,0:T(1,128)S(1)}, u32[]{:S(2)}, u32[]{:S(2)}) collective-permute-start(f32[60,1,128]{2,1,0:T(1,128)S(1)} %slice.1756), channel_id=1, source_target_pairs={{0,16},{16,32},{32,48},{48,64},{64,80},{80,96},{96,112},{1,17},{17... | collective-permute-start | bytes 92168 | tf_op jit(solution)/shard_map/ppermute | solution.py:34
  115.5 6.3 %collective-permute-done.3 = f32[60,64,1]{1,2,0:T(1,128)S(1)} collective-permute-done((f32[60,64,1]{1,2,0:T(1,128)S(1)}, f32[60,64,1]{1,2,0:T(1,128)S(1)}, u32[]{:S(2)}, u32[]{:S(2)}) %collective-permute-start.3) | collective-permute-done | bytes 15392 | tf_op jit(solution)/shard_map/ppermute | solution.py:34
  123.8 5.0 %fusion.4 = f32[60,64,128]{2,1,0:T(8,128)S(1)} fusion(f32[60,64,128]{2,1,0:T(8,128)S(1)} %multiply_add_fusion.6, f32[60,64,128]{2,1,0:T(8,128)} %copy-done.7, f32[60,63,128]{2,1,0:T(8,128)} %bitcast.4708, f32[60,1,128]{2,1,0:T(1,128)S(1)} %collective-permute-done.1, f32[60,64,128]{2,1,0:T(8,128)} %copy-done.2, f32[60,64,127]{2,1,0:T(8,128)} %bitcast.4703, ...), kind=kLoop, calls=%fused_computation.6 | loop fusion | flops 3440640 | bytes 11796480 | tf_op jit(solution)/shard_map/sub | solution.py:90
  147.4 5.1 %fusion.13 = (f32[60,64,128]{2,1,0:T(8,128)S(1)}, f32[60,64,128]{2,1,0:T(8,128)S(1)}) fusion(f32[60,64,128]{2,1,0:T(8,128)} %copy-done.2, f32[60,64,128]{2,1,0:T(8,128)S(1)} %multiply_subtract_fusion.5, f32[60,64,1]{2,1,0:T(8,128)} %copy.2910, f32[60,64,127]{2,1,0:T(8,128)} %slice.1831, f32[60,64,128]{2,1,0:T(8,128)} %copy-done.7, ...), kind=kLoop, calls=%fused_computation.20 | loop fusion | flops 3932160 | bytes 13762560 | tf_op jit(solution)/shard_map/sub | solution.py:135
  154.5 6.0 %collective-permute-start.5 = (f32[60,1,128]{2,1,0:T(1,128)}, f32[60,1,128]{2,1,0:T(1,128)}, u32[]{:S(2)}, u32[]{:S(2)}) collective-permute-start(f32[60,1,128]{2,1,0:T(1,128)} %slice.1829), channel_id=1, source_target_pairs={{0,16},{16,32},{32,48},{48,64},{64,80},{80,96},{96,112},{1,17},{17... | collective-permute-start | bytes 92168 | tf_op jit(solution)/shard_map/ppermute | solution.py:34
  167.4 6.8 %collective-permute-done.7 = f32[60,64,1]{1,2,0:T(1,128)} collective-permute-done((f32[60,64,1]{1,2,0:T(1,128)}, f32[60,64,1]{1,2,0:T(1,128)}, u32[]{:S(2)}, u32[]{:S(2)}) %collective-permute-start.7) | collective-permute-done | bytes 15392 | tf_op jit(solution)/shard_map/ppermute | solution.py:34
  176.9 5.0 %fusion.11 = f32[60,64,128]{2,1,0:T(8,128)S(1)} fusion(f32[60,64,128]{2,1,0:T(8,128)S(1)} %multiply_subtract_fusion.5, f32[60,64,128]{2,1,0:T(8,128)} %copy-done.8, f32[60,63,128]{2,1,0:T(8,128)} %bitcast.4709, f32[60,1,128]{2,1,0:T(1,128)} %collective-permute-done.5, f32[60,64,128]{2,1,0:T(8,128)} %copy-done.3, f32[60,64,127]{2,1,0:T(8,128)} %bitcast.4704, ...), kind=kLoop, calls=%fused_computation.17 | loop fusion | flops 3440640 | bytes 11796480 | tf_op jit(solution)/shard_map/sub | solution.py:90
  199.8 5.1 %fusion.20 = (f32[60,64,128]{2,1,0:T(8,128)S(1)}, f32[60,64,128]{2,1,0:T(8,128)S(1)}) fusion(f32[60,64,128]{2,1,0:T(8,128)} %copy-done.3, f32[60,64,128]{2,1,0:T(8,128)S(1)} %multiply_subtract_fusion.4, f32[60,64,1]{2,1,0:T(8,128)} %copy.2914, f32[60,64,127]{2,1,0:T(8,128)} %slice.1900, f32[60,64,128]{2,1,0:T(8,128)} %copy-done.8, ...), kind=kLoop, calls=%fused_computation.31 | loop fusion | flops 3932160 | bytes 13762560 | tf_op jit(solution)/shard_map/sub | solution.py:135
  206.8 6.0 %collective-permute-start.9 = (f32[60,1,128]{2,1,0:T(1,128)}, f32[60,1,128]{2,1,0:T(1,128)}, u32[]{:S(2)}, u32[]{:S(2)}) collective-permute-start(f32[60,1,128]{2,1,0:T(1,128)} %slice.1898), channel_id=1, source_target_pairs={{0,16},{16,32},{32,48},{48,64},{64,80},{80,96},{96,112},{1,17},{17... | collective-permute-start | bytes 92168 | tf_op jit(solution)/shard_map/ppermute | solution.py:34
  219.8 6.8 %collective-permute-done.11 = f32[60,64,1]{1,2,0:T(1,128)} collective-permute-done((f32[60,64,1]{1,2,0:T(1,128)}, f32[60,64,1]{1,2,0:T(1,128)}, u32[]{:S(2)}, u32[]{:S(2)}) %collective-permute-start.11) | collective-permute-done | bytes 15392 | tf_op jit(solution)/shard_map/ppermute | solution.py:34
  229.3 5.0 %fusion.18 = f32[60,64,128]{2,1,0:T(8,128)S(1)} fusion(f32[60,64,128]{2,1,0:T(8,128)S(1)} %multiply_subtract_fusion.4, f32[60,64,128]{2,1,0:T(8,128)} %copy-done.9, f32[60,63,128]{2,1,0:T(8,128)} %bitcast.4710, f32[60,1,128]{2,1,0:T(1,128)} %collective-permute-done.9, f32[60,64,128]{2,1,0:T(8,128)} %copy-done.4, f32[60,64,127]{2,1,0:T(8,128)} %bitcast.4705, ...), kind=kLoop, calls=%fused_computation.28 | loop fusion | flops 3440640 | bytes 11796480 | tf_op jit(solution)/shard_map/sub | solution.py:90
  252.1 5.1 %fusion.27 = (f32[60,64,128]{2,1,0:T(8,128)S(1)}, f32[60,64,128]{2,1,0:T(8,128)S(1)}) fusion(f32[60,64,128]{2,1,0:T(8,128)} %copy-done.4, f32[60,64,128]{2,1,0:T(8,128)S(1)} %multiply_subtract_fusion.3, f32[60,64,1]{2,1,0:T(8,128)} %copy.2918, f32[60,64,127]{2,1,0:T(8,128)} %slice.1969, f32[60,64,128]{2,1,0:T(8,128)} %copy-done.9, ...), kind=kLoop, calls=%fused_computation.42 | loop fusion | flops 3932160 | bytes 13762560 | tf_op jit(solution)/shard_map/sub | solution.py:135
  259.2 6.0 %collective-permute-start.13 = (f32[60,1,128]{2,1,0:T(1,128)}, f32[60,1,128]{2,1,0:T(1,128)}, u32[]{:S(2)}, u32[]{:S(2)}) collective-permute-start(f32[60,1,128]{2,1,0:T(1,128)} %slice.1967), channel_id=1, source_target_pairs={{0,16},{16,32},{32,48},{48,64},{64,80},{80,96},{96,112},{1,17},{17... | collective-permute-start | bytes 92168 | tf_op jit(solution)/shard_map/ppermute | solution.py:34
  272.2 6.8 %collective-permute-done.15 = f32[60,64,1]{1,2,0:T(1,128)} collective-permute-done((f32[60,64,1]{1,2,0:T(1,128)}, f32[60,64,1]{1,2,0:T(1,128)}, u32[]{:S(2)}, u32[]{:S(2)}) %collective-permute-start.15) | collective-permute-done | bytes 15392 | tf_op jit(solution)/shard_map/ppermute | solution.py:34
  281.7 5.0 %fusion.25 = f32[60,64,128]{2,1,0:T(8,128)S(1)} fusion(f32[60,64,128]{2,1,0:T(8,128)S(1)} %multiply_subtract_fusion.3, f32[60,64,128]{2,1,0:T(8,128)} %copy-done.10, f32[60,63,128]{2,1,0:T(8,128)} %bitcast.4711, f32[60,1,128]{2,1,0:T(1,128)} %collective-permute-done.13, f32[60,64,128]{2,1,0:T(8,128)} %copy-done.5, f32[60,64,127]{2,1,0:T(8,128)} %bitcast.4706, ...), kind=kLoop, calls=%fused_computation.39 | loop fusion | flops 3440640 | bytes 11796480 | tf_op jit(solution)/shard_map/sub | solution.py:90
  304.5 5.1 %fusion.34 = (f32[60,64,128]{2,1,0:T(8,128)S(1)}, f32[60,64,128]{2,1,0:T(8,128)S(1)}) fusion(f32[60,64,128]{2,1,0:T(8,128)} %copy-done.5, f32[60,64,128]{2,1,0:T(8,128)S(1)} %multiply_subtract_fusion.2, f32[60,64,1]{2,1,0:T(8,128)} %copy.2922, f32[60,64,127]{2,1,0:T(8,128)} %slice.2038, f32[60,64,128]{2,1,0:T(8,128)} %copy-done.10, ...), kind=kLoop, calls=%fused_computation.53 | loop fusion | flops 3932160 | bytes 13762560 | tf_op jit(solution)/shard_map/sub | solution.py:135
  311.5 6.0 %collective-permute-start.17 = (f32[60,1,128]{2,1,0:T(1,128)}, f32[60,1,128]{2,1,0:T(1,128)}, u32[]{:S(2)}, u32[]{:S(2)}) collective-permute-start(f32[60,1,128]{2,1,0:T(1,128)} %slice.2036), channel_id=1, source_target_pairs={{0,16},{16,32},{32,48},{48,64},{64,80},{80,96},{96,112},{1,17},{17... | collective-permute-start | bytes 92168 | tf_op jit(solution)/shard_map/ppermute | solution.py:34
  324.8 6.5 %collective-permute-done.19 = f32[60,64,1]{1,2,0:T(1,128)} collective-permute-done((f32[60,64,1]{1,2,0:T(1,128)}, f32[60,64,1]{1,2,0:T(1,128)}, u32[]{:S(2)}, u32[]{:S(2)}) %collective-permute-start.19) | collective-permute-done | bytes 15392 | tf_op jit(solution)/shard_map/ppermute | solution.py:34
  334.0 5.0 %fusion.32 = f32[60,64,128]{2,1,0:T(8,128)S(1)} fusion(f32[60,64,128]{2,1,0:T(8,128)S(1)} %multiply_subtract_fusion.2, f32[60,64,128]{2,1,0:T(8,128)} %copy-done.11, f32[60,63,128]{2,1,0:T(8,128)} %bitcast.4712, f32[60,1,128]{2,1,0:T(1,128)} %collective-permute-done.17, f32[60,64,128]{2,1,0:T(8,128)} %copy-done.6, f32[60,64,127]{2,1,0:T(8,128)} %bitcast.4707, ...), kind=kLoop, calls=%fused_computation.50 | loop fusion | flops 3440640 | bytes 11796480 | tf_op jit(solution)/shard_map/sub | solution.py:90
  356.9 5.1 %fusion.38 = (f32[60,64,128]{2,1,0:T(8,128)S(1)}, f32[60,64,128]{2,1,0:T(8,128)S(1)}) fusion(f32[60,64,128]{2,1,0:T(8,128)} %copy-done.6, f32[60,64,128]{2,1,0:T(8,128)S(1)} %multiply_subtract_fusion.1, f32[60,64,1]{2,1,0:T(8,128)} %copy.2926, f32[60,64,127]{2,1,0:T(8,128)} %slice.2105, f32[60,64,128]{2,1,0:T(8,128)} %copy-done.11, ...), kind=kLoop, calls=%fused_computation.60 | loop fusion | flops 3932160 | bytes 13762560 | tf_op jit(solution)/shard_map/sub | solution.py:135
  364.0 6.0 %collective-permute-start.22 = (f32[60,1,128]{2,1,0:T(1,128)}, f32[60,1,128]{2,1,0:T(1,128)}, u32[]{:S(2)}, u32[]{:S(2)}) collective-permute-start(f32[60,1,128]{2,1,0:T(1,128)} %slice.2107), channel_id=1, source_target_pairs={{0,16},{16,32},{32,48},{48,64},{64,80},{80,96},{96,112},{1,17},{17... | collective-permute-start | bytes 92168 | tf_op jit(solution)/shard_map/ppermute | solution.py:34
  377.0 6.8 %collective-permute-done.23 = f32[60,64,1]{1,2,0:T(1,128)} collective-permute-done((f32[60,64,1]{1,2,0:T(1,128)}, f32[60,64,1]{1,2,0:T(1,128)}, u32[]{:S(2)}, u32[]{:S(2)}) %collective-permute-start.23) | collective-permute-done | bytes 15392 | tf_op jit(solution)/shard_map/ppermute | solution.py:34
  386.5 5.1 %fusion.41 = f32[60,64,128]{2,1,0:T(8,128)S(1)} fusion(f32[60,64,128]{2,1,0:T(8,128)S(1)} %multiply_subtract_fusion.1, f32[60,64,128]{2,1,0:T(8,128)} %copy-done.14, f32[60,63,128]{2,1,0:T(8,128)} %bitcast.4714, f32[60,1,128]{2,1,0:T(1,128)} %collective-permute-done.22, f32[60,64,128]{2,1,0:T(8,128)} %copy-done.12, f32[60,64,127]{2,1,0:T(8,128)} %bitcast.4713, ...), kind=kLoop, calls=%fused_computation.64 | loop fusion | flops 3440640 | bytes 11796480 | tf_op jit(solution)/shard_map/sub | solution.py:90
  (673 shorter events, 200.1 us)
Async XLA Ops:
  1.8 9.8 %copy-start.80 = (f32[2,3,60,5,4]{2,4,3,1,0:T(4,128)S(1)}, f32[2,3,60,5,4]{2,4,3,1,0:T(4,128)}, u32[]{:S(2)}) copy-start(f32[2,3,60,5,4]{2,4,3,1,0:T(4,128)} %param.14) | copy-start | bytes 86404
  5.9 39.7 %all-to-all-start = ((f32[8,1,28800]{2,1,0:T(1,128)}), f32[8,1,28800]{2,1,0:T(1,128)S(1)}, u32[]{:S(2)}, u32[]{:S(2)}) async-start(f32[8,1,28800]{2,1,0:T(1,128)} %reshape.57), calls=%async_computation | async-start | bytes 1843200 | tf_op jit(solution)/shard_map/all_to_all | solution.py:22
  60.4 34.2 %collective-permute-start = (f32[60,1,128]{2,1,0:T(1,128)}, f32[60,1,128]{2,1,0:T(1,128)}, u32[]{:S(2)}, u32[]{:S(2)}) collective-permute-start(f32[60,1,128]{2,1,0:T(1,128)} %slice.1755), channel_id=1, source_target_pairs={{16,0},{32,16},{48,32},{64,48},{80,64},{96,80},{112,96},{17,1},{33... | collective-permute-start | bytes 92168 | tf_op jit(solution)/shard_map/ppermute | solution.py:34
  63.7 7.0 %copy-start.76 = (f32[1,1,60,5,64]{2,0,3,1,4:T(1,128)S(1)}, f32[1,1,60,5,64]{2,0,3,1,4:T(1,128)}, u32[]{:S(2)}) copy-start(f32[1,1,60,5,64]{2,0,3,1,4:T(1,128)} %get-tuple-element.720) | copy-start | bytes 230404
  65.0 27.0 %collective-permute-start.2 = (f32[60,64,1]{1,2,0:T(1,128)}, f32[60,64,1]{1,2,0:T(1,128)}, u32[]{:S(2)}, u32[]{:S(2)}) collective-permute-start(f32[60,64,1]{1,2,0:T(1,128)} %copy.2905), channel_id=1, source_target_pairs={{1,0},{2,1},{3,2},{4,3},{5,4},{6,5},{7,6},{8,7},{9,8},{10,9},{11,1... | collective-permute-start | bytes 46088 | tf_op jit(solution)/shard_map/ppermute | solution.py:34
  103.5 20.2 %collective-permute-start.1 = (f32[60,1,128]{2,1,0:T(1,128)S(1)}, f32[60,1,128]{2,1,0:T(1,128)S(1)}, u32[]{:S(2)}, u32[]{:S(2)}) collective-permute-start(f32[60,1,128]{2,1,0:T(1,128)S(1)} %slice.1756), channel_id=1, source_target_pairs={{0,16},{16,32},{32,48},{48,64},{64,80},{80,96},{96,112},{1,17},{17... | collective-permute-start | bytes 92168 | tf_op jit(solution)/shard_map/ppermute | solution.py:34
  113.0 8.8 %collective-permute-start.3 = (f32[60,64,1]{1,2,0:T(1,128)S(1)}, f32[60,64,1]{1,2,0:T(1,128)S(1)}, u32[]{:S(2)}, u32[]{:S(2)}) collective-permute-start(f32[60,64,1]{1,2,0:T(1,128)S(1)} %copy.2907), channel_id=1, source_target_pairs={{0,1},{1,2},{2,3},{3,4},{4,5},{5,6},{6,7},{7,8},{8,9},{9,10},{10,1... | collective-permute-start | bytes 46088 | tf_op jit(solution)/shard_map/ppermute | solution.py:34
  136.3 11.1 %collective-permute-start.4 = (f32[60,1,128]{2,1,0:T(1,128)}, f32[60,1,128]{2,1,0:T(1,128)}, u32[]{:S(2)}, u32[]{:S(2)}) collective-permute-start(f32[60,1,128]{2,1,0:T(1,128)} %slice.1828), channel_id=1, source_target_pairs={{16,0},{32,16},{48,32},{64,48},{80,64},{96,80},{112,96},{17,1},{33... | collective-permute-start | bytes 92168 | tf_op jit(solution)/shard_map/ppermute | solution.py:34
  139.4 5.3 %collective-permute-start.6 = (f32[60,64,1]{1,2,0:T(1,128)}, f32[60,64,1]{1,2,0:T(1,128)}, u32[]{:S(2)}, u32[]{:S(2)}) collective-permute-start(f32[60,64,1]{1,2,0:T(1,128)} %copy.2909), channel_id=1, source_target_pairs={{1,0},{2,1},{3,2},{4,3},{5,4},{6,5},{7,6},{8,7},{9,8},{10,9},{11,1... | collective-permute-start | bytes 46088 | tf_op jit(solution)/shard_map/ppermute | solution.py:34
  152.6 7.9 %copy-start.3 = (f32[60,64,128]{2,1,0:T(8,128)}, f32[60,64,128]{2,1,0:T(8,128)S(1)}, u32[]{:S(2)}) copy-start(f32[60,64,128]{2,1,0:T(8,128)S(1)} %get-tuple-element.711) | copy-start | bytes 5898244
  154.5 22.5 %collective-permute-start.5 = (f32[60,1,128]{2,1,0:T(1,128)}, f32[60,1,128]{2,1,0:T(1,128)}, u32[]{:S(2)}, u32[]{:S(2)}) collective-permute-start(f32[60,1,128]{2,1,0:T(1,128)} %slice.1829), channel_id=1, source_target_pairs={{0,16},{16,32},{32,48},{48,64},{64,80},{80,96},{96,112},{1,17},{17... | collective-permute-start | bytes 92168 | tf_op jit(solution)/shard_map/ppermute | solution.py:34
  165.1 9.1 %collective-permute-start.7 = (f32[60,64,1]{1,2,0:T(1,128)}, f32[60,64,1]{1,2,0:T(1,128)}, u32[]{:S(2)}, u32[]{:S(2)}) collective-permute-start(f32[60,64,1]{1,2,0:T(1,128)} %copy.2911), channel_id=1, source_target_pairs={{0,1},{1,2},{2,3},{3,4},{4,5},{5,6},{6,7},{7,8},{8,9},{9,10},{10,1... | collective-permute-start | bytes 46088 | tf_op jit(solution)/shard_map/ppermute | solution.py:34
  188.6 11.1 %collective-permute-start.8 = (f32[60,1,128]{2,1,0:T(1,128)}, f32[60,1,128]{2,1,0:T(1,128)}, u32[]{:S(2)}, u32[]{:S(2)}) collective-permute-start(f32[60,1,128]{2,1,0:T(1,128)} %slice.1897), channel_id=1, source_target_pairs={{16,0},{32,16},{48,32},{64,48},{80,64},{96,80},{112,96},{17,1},{33... | collective-permute-start | bytes 92168 | tf_op jit(solution)/shard_map/ppermute | solution.py:34
  191.8 5.3 %collective-permute-start.10 = (f32[60,64,1]{1,2,0:T(1,128)}, f32[60,64,1]{1,2,0:T(1,128)}, u32[]{:S(2)}, u32[]{:S(2)}) collective-permute-start(f32[60,64,1]{1,2,0:T(1,128)} %copy.2913), channel_id=1, source_target_pairs={{1,0},{2,1},{3,2},{4,3},{5,4},{6,5},{7,6},{8,7},{9,8},{10,9},{11,1... | collective-permute-start | bytes 46088 | tf_op jit(solution)/shard_map/ppermute | solution.py:34
  204.9 7.9 %copy-start.4 = (f32[60,64,128]{2,1,0:T(8,128)}, f32[60,64,128]{2,1,0:T(8,128)S(1)}, u32[]{:S(2)}) copy-start(f32[60,64,128]{2,1,0:T(8,128)S(1)} %get-tuple-element.709) | copy-start | bytes 5898244
  206.8 22.5 %collective-permute-start.9 = (f32[60,1,128]{2,1,0:T(1,128)}, f32[60,1,128]{2,1,0:T(1,128)}, u32[]{:S(2)}, u32[]{:S(2)}) collective-permute-start(f32[60,1,128]{2,1,0:T(1,128)} %slice.1898), channel_id=1, source_target_pairs={{0,16},{16,32},{32,48},{48,64},{64,80},{80,96},{96,112},{1,17},{17... | collective-permute-start | bytes 92168 | tf_op jit(solution)/shard_map/ppermute | solution.py:34
  217.5 9.1 %collective-permute-start.11 = (f32[60,64,1]{1,2,0:T(1,128)}, f32[60,64,1]{1,2,0:T(1,128)}, u32[]{:S(2)}, u32[]{:S(2)}) collective-permute-start(f32[60,64,1]{1,2,0:T(1,128)} %copy.2915), channel_id=1, source_target_pairs={{0,1},{1,2},{2,3},{3,4},{4,5},{5,6},{6,7},{7,8},{8,9},{9,10},{10,1... | collective-permute-start | bytes 46088 | tf_op jit(solution)/shard_map/ppermute | solution.py:34
  241.0 11.1 %collective-permute-start.12 = (f32[60,1,128]{2,1,0:T(1,128)}, f32[60,1,128]{2,1,0:T(1,128)}, u32[]{:S(2)}, u32[]{:S(2)}) collective-permute-start(f32[60,1,128]{2,1,0:T(1,128)} %slice.1966), channel_id=1, source_target_pairs={{16,0},{32,16},{48,32},{64,48},{80,64},{96,80},{112,96},{17,1},{33... | collective-permute-start | bytes 92168 | tf_op jit(solution)/shard_map/ppermute | solution.py:34
  244.2 5.3 %collective-permute-start.14 = (f32[60,64,1]{1,2,0:T(1,128)}, f32[60,64,1]{1,2,0:T(1,128)}, u32[]{:S(2)}, u32[]{:S(2)}) collective-permute-start(f32[60,64,1]{1,2,0:T(1,128)} %copy.2917), channel_id=1, source_target_pairs={{1,0},{2,1},{3,2},{4,3},{5,4},{6,5},{7,6},{8,7},{9,8},{10,9},{11,1... | collective-permute-start | bytes 46088 | tf_op jit(solution)/shard_map/ppermute | solution.py:34
  257.3 7.9 %copy-start.5 = (f32[60,64,128]{2,1,0:T(8,128)}, f32[60,64,128]{2,1,0:T(8,128)S(1)}, u32[]{:S(2)}) copy-start(f32[60,64,128]{2,1,0:T(8,128)S(1)} %get-tuple-element.707) | copy-start | bytes 5898244
  259.2 22.5 %collective-permute-start.13 = (f32[60,1,128]{2,1,0:T(1,128)}, f32[60,1,128]{2,1,0:T(1,128)}, u32[]{:S(2)}, u32[]{:S(2)}) collective-permute-start(f32[60,1,128]{2,1,0:T(1,128)} %slice.1967), channel_id=1, source_target_pairs={{0,16},{16,32},{32,48},{48,64},{64,80},{80,96},{96,112},{1,17},{17... | collective-permute-start | bytes 92168 | tf_op jit(solution)/shard_map/ppermute | solution.py:34
  269.9 9.1 %collective-permute-start.15 = (f32[60,64,1]{1,2,0:T(1,128)}, f32[60,64,1]{1,2,0:T(1,128)}, u32[]{:S(2)}, u32[]{:S(2)}) collective-permute-start(f32[60,64,1]{1,2,0:T(1,128)} %copy.2919), channel_id=1, source_target_pairs={{0,1},{1,2},{2,3},{3,4},{4,5},{5,6},{6,7},{7,8},{8,9},{9,10},{10,1... | collective-permute-start | bytes 46088 | tf_op jit(solution)/shard_map/ppermute | solution.py:34
  293.3 11.1 %collective-permute-start.16 = (f32[60,1,128]{2,1,0:T(1,128)}, f32[60,1,128]{2,1,0:T(1,128)}, u32[]{:S(2)}, u32[]{:S(2)}) collective-permute-start(f32[60,1,128]{2,1,0:T(1,128)} %slice.2035), channel_id=1, source_target_pairs={{16,0},{32,16},{48,32},{64,48},{80,64},{96,80},{112,96},{17,1},{33... | collective-permute-start | bytes 92168 | tf_op jit(solution)/shard_map/ppermute | solution.py:34
  296.5 5.3 %collective-permute-start.18 = (f32[60,64,1]{1,2,0:T(1,128)}, f32[60,64,1]{1,2,0:T(1,128)}, u32[]{:S(2)}, u32[]{:S(2)}) collective-permute-start(f32[60,64,1]{1,2,0:T(1,128)} %copy.2921), channel_id=1, source_target_pairs={{1,0},{2,1},{3,2},{4,3},{5,4},{6,5},{7,6},{8,7},{9,8},{10,9},{11,1... | collective-permute-start | bytes 46088 | tf_op jit(solution)/shard_map/ppermute | solution.py:34
  309.6 7.9 %copy-start.6 = (f32[60,64,128]{2,1,0:T(8,128)}, f32[60,64,128]{2,1,0:T(8,128)S(1)}, u32[]{:S(2)}) copy-start(f32[60,64,128]{2,1,0:T(8,128)S(1)} %get-tuple-element.705) | copy-start | bytes 5898244
  311.5 22.5 %collective-permute-start.17 = (f32[60,1,128]{2,1,0:T(1,128)}, f32[60,1,128]{2,1,0:T(1,128)}, u32[]{:S(2)}, u32[]{:S(2)}) collective-permute-start(f32[60,1,128]{2,1,0:T(1,128)} %slice.2036), channel_id=1, source_target_pairs={{0,16},{16,32},{32,48},{48,64},{64,80},{80,96},{96,112},{1,17},{17... | collective-permute-start | bytes 92168 | tf_op jit(solution)/shard_map/ppermute | solution.py:34
  322.2 9.1 %collective-permute-start.19 = (f32[60,64,1]{1,2,0:T(1,128)}, f32[60,64,1]{1,2,0:T(1,128)}, u32[]{:S(2)}, u32[]{:S(2)}) collective-permute-start(f32[60,64,1]{1,2,0:T(1,128)} %copy.2923), channel_id=1, source_target_pairs={{0,1},{1,2},{2,3},{3,4},{4,5},{5,6},{6,7},{7,8},{8,9},{9,10},{10,1... | collective-permute-start | bytes 46088 | tf_op jit(solution)/shard_map/ppermute | solution.py:34
  345.7 11.1 %collective-permute-start.20 = (f32[60,1,128]{2,1,0:T(1,128)}, f32[60,1,128]{2,1,0:T(1,128)}, u32[]{:S(2)}, u32[]{:S(2)}) collective-permute-start(f32[60,1,128]{2,1,0:T(1,128)} %slice.2104), channel_id=1, source_target_pairs={{16,0},{32,16},{48,32},{64,48},{80,64},{96,80},{112,96},{17,1},{33... | collective-permute-start | bytes 92168 | tf_op jit(solution)/shard_map/ppermute | solution.py:34
  348.9 5.3 %collective-permute-start.21 = (f32[60,64,1]{1,2,0:T(1,128)}, f32[60,64,1]{1,2,0:T(1,128)}, u32[]{:S(2)}, u32[]{:S(2)}) collective-permute-start(f32[60,64,1]{1,2,0:T(1,128)} %copy.2925), channel_id=1, source_target_pairs={{1,0},{2,1},{3,2},{4,3},{5,4},{6,5},{7,6},{8,7},{9,8},{10,9},{11,1... | collective-permute-start | bytes 46088 | tf_op jit(solution)/shard_map/ppermute | solution.py:34
  362.0 8.0 %copy-start.12 = (f32[60,64,128]{2,1,0:T(8,128)}, f32[60,64,128]{2,1,0:T(8,128)S(1)}, u32[]{:S(2)}) copy-start(f32[60,64,128]{2,1,0:T(8,128)S(1)} %get-tuple-element.703) | copy-start | bytes 5898244
  364.0 22.5 %collective-permute-start.22 = (f32[60,1,128]{2,1,0:T(1,128)}, f32[60,1,128]{2,1,0:T(1,128)}, u32[]{:S(2)}, u32[]{:S(2)}) collective-permute-start(f32[60,1,128]{2,1,0:T(1,128)} %slice.2107), channel_id=1, source_target_pairs={{0,16},{16,32},{32,48},{48,64},{64,80},{80,96},{96,112},{1,17},{17... | collective-permute-start | bytes 92168 | tf_op jit(solution)/shard_map/ppermute | solution.py:34
  374.7 9.1 %collective-permute-start.23 = (f32[60,64,1]{1,2,0:T(1,128)}, f32[60,64,1]{1,2,0:T(1,128)}, u32[]{:S(2)}, u32[]{:S(2)}) collective-permute-start(f32[60,64,1]{1,2,0:T(1,128)} %copy.2927), channel_id=1, source_target_pairs={{0,1},{1,2},{2,3},{3,4},{4,5},{5,6},{6,7},{7,8},{8,9},{9,10},{10,1... | collective-permute-start | bytes 46088 | tf_op jit(solution)/shard_map/ppermute | solution.py:34
  (75 other events, 99.0 us)
where the time goes:
time: 405 us; the launch traced here: 398 us
  local copies, waits for them, and re-layouts  160 us (40%)
  other arithmetic  88.6 us (22%)
  starting transfers between devices  80.3 us (20%)
  waiting for transfers between devices  40.1 us (10%)
  blocking collectives  24.6 us (6%)
  between operations  4.64 us (1%)
    ppermute x24, starting transfers between devices, passed_along(): return lax.ppermute(block, axis, route)  74.5 us
    ppermute x24, waiting for transfers between devices, passed_along(): return lax.ppermute(block, axis, route)  40.1 us
    unnamed x510, local copies, waits for them, and re-layouts  33.7 us
    sub x6, other arithmetic, per_device(): v_now = v_now - accel * (north_p - p_now)  33.2 us
    ppermute x12, local copies, waits for them, and re-layouts, passed_along(): return lax.ppermute(block, axis, route)  31.4 us
    sub x6, other arithmetic, column_part(): sectioned = p_old - spread * diverge  30.3 us
    slice x12, local copies, waits for them, and re-layouts, per_device(): south_rim = passed_along(v_now[:, :, -1:], 'gy', 1)  27.2 us
    all_gather x1, blocking collectives, per_device(): side_vals = lax.all_gather(sn_slab, 'gy', axis=4, tiled=True)  24.6 us
  transfers between devices with their start and end apart: 25, of which 6 were waited for; matrix products, arithmetic and copies ran while one was open for 29% of the time, Pallas kernels for 0%

commit v1 on v0

v1 whole, which is shorter than its diff:
```python
import jax
import jax.numpy as jnp
from jax import lax
from jax.experimental import pallas as pl
from jax.experimental.pallas import tpu as pltpu
from jax.sharding import PartitionSpec as P

SUBSTEPS = 6
HALO = 6
OFF = 16
ZG = 6
LANES = 128
ACCEL = 0.3
SPREAD = 0.3
SROW = 8
NROW = 32
SROWS = 56

VMEM = pl.BlockSpec(memory_space=pltpu.VMEM)


def passed_along(block, axis, distance):
    devices = range(lax.axis_size(axis))
    route = [(i - distance, i) for i in devices if i - distance in devices]
    return lax.ppermute(block, axis, route)


def lane_pairs(bands):
    levels = bands.shape[-1]
    low = jnp.pad(bands[:8], ((0, 0), (0, 0), (0, LANES - levels)))
    high = jnp.pad(bands[8:], ((0, 1), (0, 0), (64, 64 - levels)))
    return low + high


def to_edges(slab, axis):
    size = lax.axis_size(axis)
    t = jnp.transpose(slab, (0, 1, 3, 4, 2))
    first = lane_pairs(t[0].reshape(15, *t.shape[3:]))
    last = lane_pairs(t[1, :, ::-1].reshape(15, *t.shape[3:]))
    zero = jnp.zeros((size - 2, *first.shape), first.dtype)
    sent = jnp.concatenate([first[None], zero, last[None]], axis=0)
    return lax.all_to_all(sent, axis, 0, 0, tiled=True)


def iota8(dim):
    return lax.broadcasted_iota(jnp.int32, (8, LANES), dim)


def blend_kernel(nx, ny, u, v, p, w, coef, width, weg, sng, ub, vb, pb, east, west, cw, ce, bs, bt, wsn):
    levels, size_x, _ = u.shape
    gx = lax.axis_index("gx")
    gy = lax.axis_index("gy")
    blocks = size_x // 8
    groups = weg.shape[0]
    zero = jnp.zeros((8, LANES), jnp.float32)

    def clear(i, _):
        for k in range(3):
            cw[k, pl.ds(pl.multiple_of(i * 8, 8), 8), :] = zero
            ce[k, pl.ds(pl.multiple_of(i * 8, 8), 8), :] = zero
            bs[k, pl.ds(pl.multiple_of(i * 8, 8), 8), :] = zero
        return 0

    lax.fori_loop(0, 64, clear, 0)
    for s in range(8):
        a = jnp.concatenate([weg[g, s] for g in range(groups)], axis=0).T
        b = jnp.concatenate([sng[s], jnp.zeros((LANES - size_x, LANES), jnp.float32)], axis=0).T
        for half in range(2):
            kj = s + 8 * half
            if kj < 15:
                k, j = kj // 5, kj % 5
                cw[k, pl.ds(j, 64, stride=8), :] = a[64 * half : 64 * half + 64]
                ce[k, pl.ds(3 + j, 64, stride=8), :] = a[64 * half : 64 * half + 64]
                bs[k, pl.ds(j, 64, stride=8), :] = b[64 * half : 64 * half + 64]
    for k in range(3):
        for g in range(4):
            bt[k, g] = bs[k, g * LANES : (g + 1) * LANES, :].T

    sub = iota8(0).astype(jnp.float32)
    lane = iota8(1).astype(jnp.float32)
    x0 = (gx * size_x).astype(jnp.float32)
    y0 = (gy * LANES).astype(jnp.float32)
    is_north = gy == lax.axis_size("gy") - 1
    rate_w = width[0:8, :].astype(jnp.float32)
    rate_e = width[size_x - 8 : size_x, :].astype(jnp.float32)
    weight_w = jnp.maximum(rate_w - (sub + x0), 0.0) / rate_w
    dist_e = (nx - 1.0) - (sub + (x0 + (size_x - 8.0)))
    weight_e = jnp.maximum(rate_e - dist_e, 0.0) / rate_e

    fields = ((p, pb, 2), (u, ub, 0), (v, vb, 1))

    def take(z, _):
        rows = pl.ds(pl.multiple_of(z * 8, 8), 8)
        for src, dst, k in fields:
            for b in range(blocks):
                val = src[z, 8 * b : 8 * b + 8, :]
                if b == 0:
                    val = val + weight_w * (cw[k, rows, :] - val)
                if b == blocks - 1:
                    val = val + weight_e * (ce[k, rows, :] - val)
                dst[z, 8 * b : 8 * b + 8, :] = val
        return 0

    lax.fori_loop(0, levels, take, 0)

    @pl.when((gy == 0) | is_north)
    def _():
        dist = jnp.where(is_north, (ny - 1.0) - (lane + y0), lane + y0)
        for b in range(blocks):
            rate = width[8 * b : 8 * b + 8, :].astype(jnp.float32)
            wsn[8 * b : 8 * b + 8, :] = jnp.maximum(rate - dist, 0.0) / rate
        base = jnp.where(is_north, 123 + LANES, LANES)

        def sides(z, _):
            g = z // 16
            shift = lax.rem(base - 8 * lax.rem(z, 16), LANES)
            for _, dst, k in fields:
                for b in range(blocks):
                    band = pltpu.roll(bt[k, g, 8 * b : 8 * b + 8, :], shift, 1)
                    val = dst[z, 8 * b : 8 * b + 8, :]
                    dst[z, 8 * b : 8 * b + 8, :] = val + wsn[8 * b : 8 * b + 8, :] * (band - val)
            return 0

        lax.fori_loop(0, levels, sides, 0)

    def pack(z, _):
        for f, src in enumerate((pb, ub, vb, w)):
            east[z, HALO * f : HALO * f + HALO, :] = src[z, size_x - HALO : size_x, :]
            west[z, HALO * f : HALO * f + HALO, :] = src[z, 0:HALO, :]
        return 0

    lax.fori_loop(0, levels, pack, 0)
    for msg, lo in ((east, size_x - HALO), (west, 0)):
        for b in range(3):
            msg[levels, 8 * b : 8 * b + 8, :] = zero
        msg[levels, 0:HALO, :] = coef[lo : lo + HALO, :]


def strip_kernel(p, u, v, w, coef, from_w, from_e, own, own_r, north, south, halo):
    levels, size_x, _ = u.shape
    blocks = size_x // 8
    zero = jnp.zeros((8, LANES), jnp.float32)
    lane_group = iota8(1) // 16

    def unpack(z, _):
        for f in range(4):
            halo[f, z, 0:8, :] = zero
            halo[f, z, 8:16, :] = zero
            halo[f, z, 2:8, :] = from_w[z, HALO * f : HALO * f + HALO, :]
            halo[f, z, 8:14, :] = from_e[z, HALO * f : HALO * f + HALO, :]
        return 0

    lax.fori_loop(0, levels + 1, unpack, 0)

    def turned(parts):
        rows = [zero] + parts + [zero] * (LANES // 8 - 1 - len(parts))
        return jnp.concatenate(rows, axis=0).T

    for f, src in enumerate((p, u, v, w)):

        def group(g, _):
            acc = None
            for zi in range(ZG):
                z = g * ZG + zi
                parts = [halo[f, z, 0:8, :]]
                parts += [src[z, 8 * b : 8 * b + 8, :] for b in range(blocks)]
                parts += [halo[f, z, 8:16, :]]
                parts = [pltpu.roll(part, (8 + 16 * zi) % LANES, 1) for part in parts]
                if acc is None:
                    acc = parts
                else:
                    acc = [jnp.where(lane_group == zi, part, old) for part, old in zip(parts, acc)]
            t = turned(acc)
            for zi in range(ZG):
                z = g * ZG + zi
                both = t[16 * zi : 16 * zi + 16]
                own[f, z] = both
                north[z, HALO * f : HALO * f + HALO, :] = both[2:8]
                south[z, HALO * f : HALO * f + HALO, :] = both[8:14]
            return 0

        lax.fori_loop(0, levels // ZG, group, 0)

    parts = [halo[0, levels, 0:8, :]]
    parts += [coef[8 * b : 8 * b + 8, :] for b in range(blocks)]
    parts += [halo[0, levels, 8:16, :]]
    t = turned([pltpu.roll(part, 8, 1) for part in parts])
    own_r[...] = t[0:16]
    for msg in (north, south):
        for b in range(3):
            msg[levels, 8 * b : 8 * b + 8, :] = zero
    north[levels, 0:HALO, :] = t[2:8]
    south[levels, 0:HALO, :] = t[8:14]


def step_kernel(
    ub, vb, pb, w_in, coef, from_w, from_e, own, own_r, from_s, from_n,
    u_out, v_out, w_out, p_out,
    P_, E_, W_, S_, M_, R_, sP, sE, sW, sU, sM, sR, rows, T_,
):
    levels, size_x, _ = ub.shape
    blocks = size_x // 8
    starts = [8 * b for b in range(1, blocks + 3)]
    main = [OFF + 8 * b for b in range(blocks)]
    sstarts = [SROW, SROW + 8, NROW, NROW + 8]
    zero = jnp.zeros((8, LANES), jnp.float32)
    sub = iota8(0)
    lane = iota8(1)
    is_west = lax.axis_index("gx") == 0
    is_east = lax.axis_index("gx") == lax.axis_size("gx") - 1
    is_south = lax.axis_index("gy") == 0
    is_north = lax.axis_index("gy") == lax.axis_size("gy") - 1
    mask_w = (sub == 0) & is_west
    mask_e = (sub == 7) & is_east
    smask_w = (lane == OFF) & is_west
    smask_e = (lane == OFF + size_x - 1) & is_east
    smask_s = (sub == 0) & is_south
    smask_n = (sub == 7) & is_north
    lane0 = lane == 0
    lane127 = lane == LANES - 1
    AB = ACCEL * SPREAD

    def unpack(z, _):
        for f, src, dst, sdst in ((0, pb, P_, sP), (1, ub, S_, sU), (2, vb, M_, sM), (3, w_in, W_, sW)):
            scale = 2.0 if f == 3 else 1.0
            for r in (0, 8, OFF + size_x, OFF + size_x + 8):
                dst[z, r : r + 8, :] = zero
            for b in range(blocks):
                dst[z, OFF + 8 * b : OFF + 8 * b + 8, :] = src[z, 8 * b : 8 * b + 8, :] * scale
            lo = HALO * f
            dst[z, OFF - HALO : OFF, :] = from_w[z, lo : lo + HALO, :] * scale
            dst[z, OFF + size_x : OFF + size_x + HALO, :] = from_e[z, lo : lo + HALO, :] * scale
            for r in range(0, SROWS, 8):
                sdst[z, r : r + 8, :] = zero
            sdst[z, SROW + 8 : SROW + 16, :] = own[f, z, 8:16, :] * scale
            sdst[z, NROW : NROW + 8, :] = own[f, z, 0:8, :] * scale
            sdst[z, SROW + 8 - HALO : SROW + 8, :] = from_s[z, lo : lo + HALO, :] * scale
            sdst[z, NROW + 8 : NROW + 8 + HALO, :] = from_n[z, lo : lo + HALO, :] * scale
        return 0

    lax.fori_loop(0, levels, unpack, 0)
    R_[...] = jnp.zeros_like(R_)
    R_[OFF : OFF + size_x, :] = coef[...]
    R_[OFF - HALO : OFF, :] = from_w[levels, 0:HALO, :]
    R_[OFF + size_x : OFF + size_x + HALO, :] = from_e[levels, 0:HALO, :]
    sR[...] = jnp.zeros_like(sR)
    sR[SROW + 8 : SROW + 16, :] = own_r[8:16, :]
    sR[NROW : NROW + 8, :] = own_r[0:8, :]
    sR[SROW + 8 - HALO : SROW + 8, :] = from_s[levels, 0:HALO, :]
    sR[NROW + 8 : NROW + 8 + HALO, :] = from_n[levels, 0:HALO, :]
    rows[...] = jnp.zeros_like(rows)

    def strip_init(z, _):
        for s in sstarts:
            u = sU[z, s : s + 8, :]
            v = sM[z, s : s + 8, :]
            v_s = sM[z, s - 1 : s + 7, :]
            sE[z, s : s + 8, :] = SPREAD * ((u - pltpu.roll(u, 1, 1)) + (v - v_s))
        rows[SUBSTEPS, pl.ds(2 * z, 1), :] = sM[z, SROW + 7 : SROW + 8, :]
        return 0

    lax.fori_loop(0, levels, strip_init, 0)

    def factors(coefs, dst, at):
        def body(z, prev):
            new = []
            for s, m in zip(at, prev):
                r = coefs[s : s + 8, :]
                m = 1.0 / (1.0 + 2.0 * r - r * r * m)
                dst[z, s : s + 8, :] = m
                new.append(m)
            return tuple(new)

        lax.fori_loop(0, levels, body, tuple(zero for _ in at))

    factors(sR, sM, sstarts)

    def substep(pp, ww, mm, rr, at, sectioned):
        def store(z, qs):
            for s, q in zip(at, qs):
                pp[z, s : s + 8, :] = q

        def down(z, qs, qn, ds):
            new = []
            for i, s in enumerate(at):
                rhs = ww[z, s : s + 8, :] + (qs[i] if qn is None else qs[i] - qn[i])
                if ds is not None:
                    rhs = rhs + rr[s : s + 8, :] * ds[i]
                d = mm[z, s : s + 8, :] * rhs
                ww[z, s : s + 8, :] = d
                new.append(d)
            return tuple(new)

        qs = sectioned(0)
        store(0, qs)

        def fwd(z, carry):
            qs, ds = carry
            qn = sectioned(z)
            store(z, qn)
            return qn, down(z - 1, qs, qn, ds)

        qs, ds = lax.fori_loop(1, levels, fwd, (qs, tuple(zero for _ in at)))
        ws = down(levels - 1, qs, None, ds)

        def bwd(i, ws):
            z = levels - 2 - i
            new = []
            for j, s in enumerate(at):
                w = ww[z, s : s + 8, :] + mm[z, s : s + 8, :] * (rr[s : s + 8, :] * ws[j])
                ww[z, s : s + 8, :] = w
                pp[z + 1, s : s + 8, :] = pp[z + 1, s : s + 8, :] - 0.25 * (ws[j] - w)
                new.append(w)
            return tuple(new)

        ws = lax.fori_loop(0, levels - 1, bwd, ws)
        for j, s in enumerate(at):
            pp[0, s : s + 8, :] = pp[0, s : s + 8, :] - 0.25 * ws[j]

    def strip_step(k, _):
        def sectioned(z):
            qs = []
            for s in sstarts:
                p = sP[z, s : s + 8, :]
                p_s = sP[z, s - 1 : s + 7, :]
                p_n = sP[z, s + 1 : s + 9, :]
                p_w = jnp.where(smask_w, p, pltpu.roll(p, 1, 1))
                p_e = jnp.where(smask_e, 0.0, pltpu.roll(p, LANES - 1, 1))
                if s == SROW + 8:
                    p_s = jnp.where(smask_s, p, p_s)
                if s == NROW:
                    p_n = jnp.where(smask_n, 0.0, p_n)
                e = sE[z, s : s + 8, :] - AB * (((p_w + p_e) + (p_s + p_n)) - 4.0 * p)
                sE[z, s : s + 8, :] = e
                qs.append(p - e)
            edge_s = jnp.where(is_south, sP[z, SROW + 8 : SROW + 9, :], sP[z, SROW + 7 : SROW + 8, :])
            edge_n = jnp.where(is_north, 0.0, sP[z, NROW + 8 : NROW + 9, :])
            rows[k, pl.ds(2 * z, 1), :] = edge_s
            rows[k, pl.ds(lax.rem(2 * z + LANES - 1, LANES), 1), :] = edge_n
            return tuple(qs)

        substep(sP, sW, sM, sR, sstarts, sectioned)
        return 0

    lax.fori_loop(0, SUBSTEPS, strip_step, 0)

    for k in range(SUBSTEPS + 1):
        T_[k] = rows[k].T

    def edges(k, z, s):
        return pltpu.roll(T_[k, s : s + 8, :], lax.rem(2 * LANES - 2 * z, LANES), 1)

    def main_init(z, _):
        for s in starts:
            u = S_[z, s : s + 8, :]
            u_w = S_[z, s - 1 : s + 7, :]
            v = M_[z, s : s + 8, :]
            v_s = jnp.where(lane0, edges(SUBSTEPS, z, s), pltpu.roll(v, 1, 1))
            E_[z, s : s + 8, :] = SPREAD * ((u - u_w) + (v - v_s))
        for s in starts:
            S_[z, s : s + 8, :] = zero
        return 0

    lax.fori_loop(0, levels, main_init, 0)
    factors(R_, M_, starts)

    def main_step(k, _):
        def sectioned(z):
            qs = []
            for s in starts:
                p = P_[z, s : s + 8, :]
                p_w = P_[z, s - 1 : s + 7, :]
                p_e = P_[z, s + 1 : s + 9, :]
                if s == main[0]:
                    p_w = jnp.where(mask_w, p, p_w)
                if s == main[-1]:
                    p_e = jnp.where(mask_e, 0.0, p_e)
                edge = edges(k, z, s)
                p_s = jnp.where(lane0, edge, pltpu.roll(p, 1, 1))
                p_n = jnp.where(lane127, edge, pltpu.roll(p, LANES - 1, 1))
                e = E_[z, s : s + 8, :] - AB * (((p_w + p_e) + (p_s + p_n)) - 4.0 * p)
                E_[z, s : s + 8, :] = e
                S_[z, s : s + 8, :] = S_[z, s : s + 8, :] + p
                qs.append(p - e)
            return tuple(qs)

        substep(P_, W_, M_, R_, starts, sectioned)
        return 0

    lax.fori_loop(0, SUBSTEPS, main_step, 0)

    total = T_[0]
    for k in range(1, SUBSTEPS):
        total = total + T_[k]
    T_[0] = total

    def finish(z, _):
        for b, s in enumerate(main):
            at = slice(8 * b, 8 * b + 8)
            total = S_[z, s : s + 8, :]
            east = S_[z, s + 1 : s + 9, :]
            if s == main[-1]:
                east = jnp.where(mask_e, 0.0, east)
            north = jnp.where(lane127, edges(0, z, s), pltpu.roll(total, LANES - 1, 1))
            u_out[z, at, :] = ub[z, at, :] - ACCEL * (east - total)
            v_out[z, at, :] = vb[z, at, :] - ACCEL * (north - total)
            w_out[z, at, :] = 0.5 * W_[z, s : s + 8, :]
            p_out[z, at, :] = P_[z, s : s + 8, :]
        return 0

    lax.fori_loop(0, levels, finish, 0)


def per_device(u_wind, v_wind, w_wind, pressure, vert_coef, we_slab, sn_slab, relax_width):
    levels, size_x, size_y = pressure.shape
    nx = float(size_x * lax.axis_size("gx"))
    ny = float(size_y * lax.axis_size("gy"))
    weg = to_edges(we_slab, "gx")
    sng = to_edges(sn_slab, "gy")
    sng = jnp.transpose(sng, (1, 0, 2, 3)).reshape(8, size_x, LANES)
    f32 = jnp.float32
    block = jax.ShapeDtypeStruct(pressure.shape, f32)
    message = jax.ShapeDtypeStruct((levels + 1, 4 * HALO, LANES), f32)
    ext = size_x + 2 * OFF

    def kernel(*args):
        blend_kernel(nx, ny, *args)

    ub, vb, pb, east, west = pl.pallas_call(
        kernel,
        out_shape=(block, block, block, message, message),
        in_specs=[VMEM] * 8,
        out_specs=[VMEM] * 5,
        scratch_shapes=[
            pltpu.VMEM((3, 512, LANES), f32),
            pltpu.VMEM((3, 512, LANES), f32),
            pltpu.VMEM((3, 512, LANES), f32),
            pltpu.VMEM((3, 4, LANES, LANES), f32),
            pltpu.VMEM((size_x, LANES), f32),
        ],
        compiler_params=pltpu.CompilerParams(vmem_limit_bytes=30 << 20),
        name="blend",
    )(u_wind, v_wind, pressure, w_wind, vert_coef, relax_width, weg, sng)
    from_w = passed_along(east, "gx", 1)
    from_e = passed_along(west, "gx", -1)

    own, own_r, north, south = pl.pallas_call(
        strip_kernel,
        out_shape=(
            jax.ShapeDtypeStruct((4, levels, 16, LANES), f32),
            jax.ShapeDtypeStruct((16, LANES), f32),
            message,
            message,
        ),
        in_specs=[VMEM] * 7,
        out_specs=[VMEM] * 4,
        scratch_shapes=[pltpu.VMEM((4, levels + 1, 16, LANES), f32)],
        compiler_params=pltpu.CompilerParams(vmem_limit_bytes=30 << 20),
        name="strips",
    )(pb, ub, vb, w_wind, vert_coef, from_w, from_e)
    from_s = passed_along(north, "gy", 1)
    from_n = passed_along(south, "gy", -1)

    big = pltpu.VMEM((levels, ext, LANES), f32)
    strip = pltpu.VMEM((levels, SROWS, LANES), f32)
    return pl.pallas_call(
        step_kernel,
        out_shape=(block, block, block, block),
        in_specs=[VMEM] * 11,
        out_specs=[VMEM] * 4,
        scratch_shapes=[big] * 5
        + [pltpu.VMEM((ext, LANES), f32)]
        + [strip] * 5
        + [
            pltpu.VMEM((SROWS, LANES), f32),
            pltpu.VMEM((SUBSTEPS + 1, LANES, LANES), f32),
            pltpu.VMEM((SUBSTEPS + 1, LANES, LANES), f32),
        ],
        compiler_params=pltpu.CompilerParams(vmem_limit_bytes=56 << 20),
        name="substeps",
    )(ub, vb, pb, w_wind, vert_coef, from_w, from_e, own, own_r, from_s, from_n)


def solution(mesh):
    placed = (
        P(None, "gx", "gy"),
        P(None, "gx", "gy"),
        P(None, "gx", "gy"),
        P(None, "gx", "gy"),
        P("gx", "gy"),
        P(None, None, None, None, ("gy", "gx")),
        P(None, None, None, None, ("gx", "gy")),
        P("gx", "gy"),
    )
    return jax.shard_map(
        per_device,
        mesh=mesh,
        in_specs=placed,
        out_specs=(P(None, "gx", "gy"),) * 4,
        check_vma=False,
    )
```

time: 405 us -> 205 us (0.51)
  the two profiles are of different devices: /device:TPU:88 before, /device:TPU:31 now
where the time goes in v1:
time: 205 us; the launch traced here: 204 us
  Pallas kernels  118 us (58%)
  waiting for transfers between devices  46.4 us (23%)
  starting transfers between devices  27.6 us (13%)
  local copies, waits for them, and re-layouts  9.59 us (5%)
    pallas_call x1, Pallas kernels, per_device(): pl.pallas_call(step_kernel, out_shape=(block, block, block, block), in_sp...  107 us
    ppermute x4, waiting for transfers between devices, passed_along(): return lax.ppermute(block, axis, route)  33.9 us
    ppermute x4, starting transfers between devices, passed_along(): return lax.ppermute(block, axis, route)  14.6 us
    all_to_all x2, starting transfers between devices, to_edges(): return lax.all_to_all(sent, axis, 0, 0, tiled=True)  13 us
    all_to_all x2, waiting for transfers between devices, to_edges(): return lax.all_to_all(sent, axis, 0, 0, tiled=True)  12.5 us
    pallas_call x1, Pallas kernels, per_device(): pl.pallas_call(strip_kernel, out_shape=(jax.ShapeDtypeStruct((4, levels,...  8.67 us
    unnamed x30, local copies, waits for them, and re-layouts  7.45 us
  transfers between devices with their start and end apart: 6, of which 6 were waited for; matrix products, arithmetic and copies ran while one was open for 1% of the time, Pallas kernels for 0%

profile of v1, /device:TPU:31, one launch (start us, length us, event | category | flops | bytes accessed | tf_op | source)
XLA Modules:
  0.0 204.2 jit_solution(14655269077382156093)
XLA Ops:
  0.6 0.8 fusion.1
  1.5 0.1 pad.37.clone
  1.5 0.1 add_bitcast_fusion.2
  1.6 0.8 pad_maximum_fusion.1
  2.4 8.4 %all-to-all-start.1 = ((f32[16,8,4,128]{3,2,1,0:T(4,128)}), f32[16,8,4,128]{3,2,1,0:T(4,128)S(1)}, u32[]{:S(2)}, u32[]{:S(2)}) async-start(f32[16,8,4,128]{3,2,1,0:T(4,128)} %pad_maximum_fusion.1), calls=%async_computation.1 | async-start | bytes 524288 | tf_op jit(solution)/shard_map/all_to_all | solution.py:42
  10.8 0.0 copy-start.10
  10.8 0.0 copy-start.11
  10.9 1.1 fusion
  12.1 0.1 add_bitcast_fusion
  12.2 0.1 pad.40.clone
  12.2 0.9 pad_maximum_fusion
  13.1 5.1 %all-to-all-done.1 = f32[16,8,4,128]{3,2,1,0:T(4,128)S(1)} async-done(((f32[16,8,4,128]{3,2,1,0:T(4,128)}), f32[16,8,4,128]{3,2,1,0:T(4,128)S(1)}, u32[]{:S(2)}, u32[]{:S(2)}) %all-to-all-start.1) | async-done | bytes 262176 | tf_op jit(solution)/shard_map/all_to_all | solution.py:42
  18.2 4.6 %all-to-all-start = ((f32[8,8,16,128]{3,2,1,0:T(8,128)}), f32[8,8,16,128]{3,2,1,0:T(8,128)S(1)}, u32[]{:S(2)}, u32[]{:S(2)}) async-start(f32[8,8,16,128]{3,2,1,0:T(8,128)} %pad_maximum_fusion), calls=%async_computation | async-start | bytes 1048576 | tf_op jit(solution)/shard_map/all_to_all | solution.py:42
  22.8 7.4 %all-to-all-done.args_6_ = f32[8,8,16,128]{3,2,1,0:T(8,128)S(1)} async-done(((f32[8,8,16,128]{3,2,1,0:T(8,128)}), f32[8,8,16,128]{3,2,1,0:T(8,128)S(1)}, u32[]{:S(2)}, u32[]{:S(2)}) %all-to-all-start) | async-done | bytes 524320 | tf_op jit(solution)/shard_map/all_to_all | solution.py:42
  30.3 1.5 copy-done.6
  31.8 1.5 copy-done.7
  33.4 1.5 copy-done.8
  34.9 2.2 %blend.1 = (f32[60,64,128]{2,1,0:T(8,128)S(1)}, f32[60,64,128]{2,1,0:T(8,128)S(1)}, f32[60,64,128]{2,1,0:T(8,128)S(1)}, f32[61,24,128]{2,1,0:T(8,128)S(1)}, f32[61,24,128]{2,1,0:T(8,128)S(1)}) custom-call(f32[60,64,128]{2,1,0:T(8,128)S(1)} %copy-done.6, f32[60,64,128]{2,1,0:T(8,128)S(1)} %copy-done.7, f32[60,64,128]{2,1,0:T(8,128)S(1)} %copy-done.8, ...), custom_call_target="tpu_custom_call" | custom-call | tf_op jit(solution)/shard_map/blend/pallas_call | solution.py:429
  37.2 4.7 %collective-permute-start = (f32[61,24,128]{2,1,0:T(8,128)S(1)}, f32[61,24,128]{2,1,0:T(8,128)S(1)}, u32[]{:S(2)}, u32[]{:S(2)}) collective-permute-start(f32[61,24,128]{2,1,0:T(8,128)S(1)} %get-tuple-element.16), channel_id=1, source_target_pairs={{0,16},{16,32},{32,48},{48,64},{64,80},{80,96},{96,112},{1,17},{17... | collective-permute-start | bytes 2248712 | tf_op jit(solution)/shard_map/ppermute | solution.py:25
  41.9 1.9 collective-permute-start.1
  43.8 13.4 %collective-permute-done.from_w = f32[61,24,128]{2,1,0:T(8,128)S(1)} collective-permute-done((f32[61,24,128]{2,1,0:T(8,128)S(1)}, f32[61,24,128]{2,1,0:T(8,128)S(1)}, u32[]{:S(2)}, u32[]{:S(2)}) %collective-permute-start) | collective-permute-done | bytes 749600 | tf_op jit(solution)/shard_map/ppermute | solution.py:25
  57.2 5.9 %collective-permute-done.1.from_e = f32[61,24,128]{2,1,0:T(8,128)S(1)} collective-permute-done((f32[61,24,128]{2,1,0:T(8,128)S(1)}, f32[61,24,128]{2,1,0:T(8,128)S(1)}, u32[]{:S(2)}, u32[]{:S(2)}) %collective-permute-start.1) | collective-permute-done | bytes 749600 | tf_op jit(solution)/shard_map/ppermute | solution.py:25
  63.1 8.7 %strips.1 = (f32[4,60,16,128]{3,2,1,0:T(8,128)S(1)}, f32[16,128]{1,0:T(8,128)S(1)}, f32[61,24,128]{2,1,0:T(8,128)S(1)}, f32[61,24,128]{2,1,0:T(8,128)S(1)}) custom-call(f32[60,64,128]{2,1,0:T(8,128)S(1)} %get-tuple-element.15.p.pb, f32[60,64,128]{2,1,0:T(8,128)S(1)} %get-tuple-element.13.u.ub, f32[60,64,128]{2,1,0:T(8,128)S(1)} %get-tuple-element.14.v.vb, ...), custom_call_target="tpu_custom_call" | custom-call | tf_op jit(solution)/shard_map/strips/pallas_call | solution.py:447
  71.8 0.0 copy-done.3
  71.8 1.3 copy-done.9
  73.1 0.6 copy-done.12
  73.7 6.1 %collective-permute-start.2 = (f32[61,24,128]{2,1,0:T(8,128)S(1)}, f32[61,24,128]{2,1,0:T(8,128)S(1)}, u32[]{:S(2)}, u32[]{:S(2)}) collective-permute-start(f32[61,24,128]{2,1,0:T(8,128)S(1)} %get-tuple-element.20), channel_id=1, source_target_pairs={{0,1},{1,2},{2,3},{3,4},{4,5},{5,6},{6,7},{7,8},{8,9},{9,10},{10,1... | collective-permute-start | bytes 2248712 | tf_op jit(solution)/shard_map/ppermute | solution.py:25
  79.8 1.9 collective-permute-start.3
  81.8 6.6 %collective-permute-done.2.from_s = f32[61,24,128]{2,1,0:T(8,128)S(1)} collective-permute-done((f32[61,24,128]{2,1,0:T(8,128)S(1)}, f32[61,24,128]{2,1,0:T(8,128)S(1)}, u32[]{:S(2)}, u32[]{:S(2)}) %collective-permute-start.2) | collective-permute-done | bytes 749600 | tf_op jit(solution)/shard_map/ppermute | solution.py:25
  88.4 8.0 %collective-permute-done.3.from_n = f32[61,24,128]{2,1,0:T(8,128)S(1)} collective-permute-done((f32[61,24,128]{2,1,0:T(8,128)S(1)}, f32[61,24,128]{2,1,0:T(8,128)S(1)}, u32[]{:S(2)}, u32[]{:S(2)}) %collective-permute-start.3) | collective-permute-done | bytes 749600 | tf_op jit(solution)/shard_map/ppermute | solution.py:25
  96.4 0.9 copy-done.14
  97.2 106.9 %substeps.1 = (f32[60,64,128]{2,1,0:T(8,128)}, f32[60,64,128]{2,1,0:T(8,128)}, f32[60,64,128]{2,1,0:T(8,128)}, f32[60,64,128]{2,1,0:T(8,128)}) custom-call(f32[60,64,128]{2,1,0:T(8,128)} %copy-done.1, f32[60,64,128]{2,1,0:T(8,128)} %copy-done.2, f32[60,64,128]{2,1,0:T(8,128)} %copy-done.3, f32[60,64,128]{2,1,0:T(8,128)} %w_in.1, f32[64,128]{1,0:T(8,128)} %coef.3, ...), custom_call_target="tpu_custom_call" | custom-call | tf_op jit(solution)/shard_map/substeps/pallas_call | solution.py:466
  (34 shorter events, 0.1 us)
Async XLA Ops:
  2.4 15.8 %all-to-all-start.1 = ((f32[16,8,4,128]{3,2,1,0:T(4,128)}), f32[16,8,4,128]{3,2,1,0:T(4,128)S(1)}, u32[]{:S(2)}, u32[]{:S(2)}) async-start(f32[16,8,4,128]{3,2,1,0:T(4,128)} %pad_maximum_fusion.1), calls=%async_computation.1 | async-start | bytes 524288 | tf_op jit(solution)/shard_map/all_to_all | solution.py:42
  10.8 19.5 %copy-start = (f32[60,64,128]{2,1,0:T(8,128)S(1)}, f32[60,64,128]{2,1,0:T(8,128)}, u32[]{:S(2)}) copy-start(f32[60,64,128]{2,1,0:T(8,128)} %w_in.1) | copy-start | bytes 5898244
  10.8 19.4 %copy-start.10 = (f32[64,128]{1,0:T(8,128)S(1)}, f32[64,128]{1,0:T(8,128)}, u32[]{:S(2)}) copy-start(f32[64,128]{1,0:T(8,128)} %coef.3) | copy-start | bytes 98308
  10.8 19.4 %copy-start.11 = (s32[64,128]{1,0:T(8,128)S(1)}, s32[64,128]{1,0:T(8,128)}, u32[]{:S(2)}) copy-start(s32[64,128]{1,0:T(8,128)} %args_5_.4) | copy-start | bytes 98308
  18.2 12.1 %all-to-all-start = ((f32[8,8,16,128]{3,2,1,0:T(8,128)}), f32[8,8,16,128]{3,2,1,0:T(8,128)S(1)}, u32[]{:S(2)}, u32[]{:S(2)}) async-start(f32[8,8,16,128]{3,2,1,0:T(8,128)} %pad_maximum_fusion), calls=%async_computation | async-start | bytes 1048576 | tf_op jit(solution)/shard_map/all_to_all | solution.py:42
  30.3 1.5 copy-start.6
  31.8 1.5 copy-start.7
  33.4 1.5 copy-start.8
  37.2 34.6 %copy-start.1 = (f32[60,64,128]{2,1,0:T(8,128)}, f32[60,64,128]{2,1,0:T(8,128)S(1)}, u32[]{:S(2)}) copy-start(f32[60,64,128]{2,1,0:T(8,128)S(1)} %get-tuple-element.13.u.ub) | copy-start | bytes 5898244
  37.2 34.6 %copy-start.2 = (f32[60,64,128]{2,1,0:T(8,128)}, f32[60,64,128]{2,1,0:T(8,128)S(1)}, u32[]{:S(2)}) copy-start(f32[60,64,128]{2,1,0:T(8,128)S(1)} %get-tuple-element.14.v.vb) | copy-start | bytes 5898244
  37.2 34.6 %copy-start.3 = (f32[60,64,128]{2,1,0:T(8,128)}, f32[60,64,128]{2,1,0:T(8,128)S(1)}, u32[]{:S(2)}) copy-start(f32[60,64,128]{2,1,0:T(8,128)S(1)} %get-tuple-element.15.p.pb) | copy-start | bytes 5898244
  37.2 20.0 %collective-permute-start = (f32[61,24,128]{2,1,0:T(8,128)S(1)}, f32[61,24,128]{2,1,0:T(8,128)S(1)}, u32[]{:S(2)}, u32[]{:S(2)}) collective-permute-start(f32[61,24,128]{2,1,0:T(8,128)S(1)} %get-tuple-element.16), channel_id=1, source_target_pairs={{0,16},{16,32},{32,48},{48,64},{64,80},{80,96},{96,112},{1,17},{17... | collective-permute-start | bytes 2248712 | tf_op jit(solution)/shard_map/ppermute | solution.py:25
  41.9 21.2 %collective-permute-start.1 = (f32[61,24,128]{2,1,0:T(8,128)S(1)}, f32[61,24,128]{2,1,0:T(8,128)S(1)}, u32[]{:S(2)}, u32[]{:S(2)}) collective-permute-start(f32[61,24,128]{2,1,0:T(8,128)S(1)} %get-tuple-element.17), channel_id=1, source_target_pairs={{16,0},{32,16},{48,32},{64,48},{80,64},{96,80},{112,96},{17,1},{33... | collective-permute-start | bytes 2248712 | tf_op jit(solution)/shard_map/ppermute | solution.py:25
  57.2 14.7 %copy-start.4 = (f32[61,24,128]{2,1,0:T(8,128)}, f32[61,24,128]{2,1,0:T(8,128)S(1)}, u32[]{:S(2)}) copy-start(f32[61,24,128]{2,1,0:T(8,128)S(1)} %collective-permute-done.from_w) | copy-start | bytes 2248708
  63.1 8.7 %copy-start.5 = (f32[61,24,128]{2,1,0:T(8,128)}, f32[61,24,128]{2,1,0:T(8,128)S(1)}, u32[]{:S(2)}) copy-start(f32[61,24,128]{2,1,0:T(8,128)S(1)} %collective-permute-done.1.from_e) | copy-start | bytes 2248708
  71.8 1.3 copy-start.9
  73.1 0.6 copy-start.12
  73.7 14.6 %collective-permute-start.2 = (f32[61,24,128]{2,1,0:T(8,128)S(1)}, f32[61,24,128]{2,1,0:T(8,128)S(1)}, u32[]{:S(2)}, u32[]{:S(2)}) collective-permute-start(f32[61,24,128]{2,1,0:T(8,128)S(1)} %get-tuple-element.20), channel_id=1, source_target_pairs={{0,1},{1,2},{2,3},{3,4},{4,5},{5,6},{6,7},{7,8},{8,9},{9,10},{10,1... | collective-permute-start | bytes 2248712 | tf_op jit(solution)/shard_map/ppermute | solution.py:25
  79.8 16.5 %collective-permute-start.3 = (f32[61,24,128]{2,1,0:T(8,128)S(1)}, f32[61,24,128]{2,1,0:T(8,128)S(1)}, u32[]{:S(2)}, u32[]{:S(2)}) collective-permute-start(f32[61,24,128]{2,1,0:T(8,128)S(1)} %get-tuple-element.21), channel_id=1, source_target_pairs={{1,0},{2,1},{3,2},{4,3},{5,4},{6,5},{7,6},{8,7},{9,8},{10,9},{11,1... | collective-permute-start | bytes 2248712 | tf_op jit(solution)/shard_map/ppermute | solution.py:25
  88.4 8.0 %copy-start.13 = (f32[61,24,128]{2,1,0:T(8,128)}, f32[61,24,128]{2,1,0:T(8,128)S(1)}, u32[]{:S(2)}) copy-start(f32[61,24,128]{2,1,0:T(8,128)S(1)} %collective-permute-done.2.from_s) | copy-start | bytes 2248708
  96.4 0.9 copy-start.14

commit v2 on v1

v2 whole, which is shorter than its diff:
```python
import jax
import jax.numpy as jnp
from jax import lax
from jax.experimental import pallas as pl
from jax.experimental.pallas import tpu as pltpu
from jax.sharding import PartitionSpec as P

SUBSTEPS = 6
HALO = 6
OFF = 16
ZG = 6
LANES = 128
ACCEL = 0.3
SPREAD = 0.3
SROW = 8
NROW = 24
SROWS = 48
MU = 4
SU = 6

VMEM = pl.BlockSpec(memory_space=pltpu.VMEM)


def passed_along(block, axis, distance):
    devices = range(lax.axis_size(axis))
    route = [(i - distance, i) for i in devices if i - distance in devices]
    return lax.ppermute(block, axis, route)


def lane_pairs(bands):
    levels = bands.shape[-1]
    low = jnp.pad(bands[:8], ((0, 0), (0, 0), (0, LANES - levels)))
    high = jnp.pad(bands[8:], ((0, 1), (0, 0), (64, 64 - levels)))
    return low + high


def to_edges(slab, axis):
    size = lax.axis_size(axis)
    t = jnp.transpose(slab, (0, 1, 3, 4, 2))
    first = lane_pairs(t[0].reshape(15, *t.shape[3:]))
    last = lane_pairs(t[1, :, ::-1].reshape(15, *t.shape[3:]))
    zero = jnp.zeros((size - 2, *first.shape), first.dtype)
    sent = jnp.concatenate([first[None], zero, last[None]], axis=0)
    return lax.all_to_all(sent, axis, 0, 0, tiled=True)


def iota8(dim):
    return lax.broadcasted_iota(jnp.int32, (8, LANES), dim)


def axis_ends(axis):
    at = lax.axis_index(axis)
    return at == 0, at == lax.axis_size(axis) - 1


def loop(count, unroll, body, carry):
    assert count % unroll == 0

    def trip(g, carry):
        for i in range(unroll):
            carry = body(g * unroll + i, carry)
        return carry

    return lax.fori_loop(0, count // unroll, trip, carry)


def each(count, unroll, body):
    def step(i, carry):
        body(i)
        return carry

    loop(count, unroll, step, 0)


def side_bands(sng, bs, bt, size_x):
    zero = jnp.zeros((8, LANES), jnp.float32)

    def clear(i):
        for k in range(3):
            bs[k, pl.ds(pl.multiple_of(i * 8, 8), 8), :] = zero

    each(64, 4, clear)
    for s in range(8):
        b = jnp.concatenate([sng[s], jnp.zeros((LANES - size_x, LANES), jnp.float32)], axis=0).T
        for half in range(2):
            kj = s + 8 * half
            if kj < 15:
                bs[kj // 5, pl.ds(kj % 5, 64, stride=8), :] = b[64 * half : 64 * half + 64]
    for k in range(3):
        for g in range(4):
            bt[k, g] = bs[k, g * LANES : (g + 1) * LANES, :].T


def side_weight(ny, width, rows):
    is_south, is_north = axis_ends("gy")
    y = iota8(1).astype(jnp.float32) + (lax.axis_index("gy") * LANES).astype(jnp.float32)
    dist = jnp.where(is_north, (ny - 1.0) - y, y)
    rate = width[rows, :].astype(jnp.float32)
    return jnp.maximum(rate - dist, 0.0) / rate


def side_band(bt, k, z, rows):
    _, is_north = axis_ends("gy")
    base = jnp.where(is_north, 123 + LANES, LANES)
    shift = lax.rem(base - 8 * lax.rem(z, 16), LANES)
    return pltpu.roll(bt[k, z // 16, rows, :], shift, 1)


def rim_kernel(ny, u, v, p, w, coef, width, sng, east, west, bs, bt):
    levels, size_x, _ = u.shape
    is_south, is_north = axis_ends("gy")
    zero = jnp.zeros((8, LANES), jnp.float32)
    for msg, lo in ((east, size_x - HALO), (west, 0)):
        for b in range(3):
            msg[levels, 8 * b : 8 * b + 8, :] = zero
        msg[levels, 0:HALO, :] = coef[lo : lo + HALO, :]

    def plain(z):
        for f, src in enumerate((p, u, v, w)):
            east[z, HALO * f : HALO * f + HALO, :] = src[z, size_x - HALO : size_x, :]
            west[z, HALO * f : HALO * f + HALO, :] = src[z, 0:HALO, :]

    each(levels, 2, plain)

    @pl.when(is_south | is_north)
    def _():
        side_bands(sng, bs, bt, size_x)
        at_e = slice(size_x - 8, size_x)
        at_w = slice(0, 8)
        weight_e = side_weight(ny, width, at_e)
        weight_w = side_weight(ny, width, at_w)

        def sides(z):
            for f, (src, k) in enumerate(((p, 2), (u, 0), (v, 1))):
                val = src[z, at_e, :]
                val = val + weight_e * (side_band(bt, k, z, at_e) - val)
                east[z, HALO * f : HALO * f + HALO, :] = val[8 - HALO :]
                val = src[z, at_w, :]
                val = val + weight_w * (side_band(bt, k, z, at_w) - val)
                west[z, HALO * f : HALO * f + HALO, :] = val[:HALO]

        each(levels, 6, sides)


def blend_kernel(nx, ny, u, v, p, width, weg, sng, ub, vb, pb, cw, ce, bs, bt):
    levels, size_x, _ = u.shape
    blocks = size_x // 8
    groups = weg.shape[0]
    is_south, is_north = axis_ends("gy")
    is_west, is_east = axis_ends("gx")
    zero = jnp.zeros((8, LANES), jnp.float32)
    fields = ((p, pb, 2), (u, ub, 0), (v, vb, 1))

    def take(z):
        for src, dst, _ in fields:
            for b in range(blocks):
                dst[z, 8 * b : 8 * b + 8, :] = src[z, 8 * b : 8 * b + 8, :]

    each(levels, 2, take)

    @pl.when(is_west | is_east)
    def _():
        def clear(i):
            for k in range(3):
                cw[k, pl.ds(pl.multiple_of(i * 8, 8), 8), :] = zero
                ce[k, pl.ds(pl.multiple_of(i * 8, 8), 8), :] = zero

        each(64, 4, clear)
        for s in range(8):
            a = jnp.concatenate([weg[g, s] for g in range(groups)], axis=0).T
            for half in range(2):
                kj = s + 8 * half
                if kj < 15:
                    k, j = kj // 5, kj % 5
                    cw[k, pl.ds(j, 64, stride=8), :] = a[64 * half : 64 * half + 64]
                    ce[k, pl.ds(3 + j, 64, stride=8), :] = a[64 * half : 64 * half + 64]
        x = iota8(0).astype(jnp.float32) + (lax.axis_index("gx") * size_x).astype(jnp.float32)
        rate_w = width[0:8, :].astype(jnp.float32)
        rate_e = width[size_x - 8 : size_x, :].astype(jnp.float32)
        weight_w = jnp.maximum(rate_w - x, 0.0) / rate_w
        weight_e = jnp.maximum(rate_e - ((nx - 1.0) - (x + (size_x - 8.0))), 0.0) / rate_e

        def ends(z):
            rows = pl.ds(pl.multiple_of(z * 8, 8), 8)
            for src, dst, k in fields:
                val = dst[z, 0:8, :]
                dst[z, 0:8, :] = val + weight_w * (cw[k, rows, :] - val)
                val = dst[z, size_x - 8 : size_x, :]
                dst[z, size_x - 8 : size_x, :] = val + weight_e * (ce[k, rows, :] - val)

        each(levels, 3, ends)

    @pl.when(is_south | is_north)
    def _():
        side_bands(sng, bs, bt, size_x)
        for b in range(blocks):
            at = slice(8 * b, 8 * b + 8)
            weight = side_weight(ny, width, at)

            def sides(z):
                for _, dst, k in fields:
                    val = dst[z, at, :]
                    dst[z, at, :] = val + weight * (side_band(bt, k, z, at) - val)

            each(levels, 12 if levels % 12 == 0 else 6, sides)


def strip_kernel(p, u, v, w, coef, from_w, from_e, own, own_r, north, south, halo):
    levels, size_x, _ = u.shape
    blocks = size_x // 8
    zero = jnp.zeros((8, LANES), jnp.float32)
    lane_group = iota8(1) // 16

    for f in range(4):

        def unpack(z):
            halo[f, z, 2:8, :] = from_w[z, HALO * f : HALO * f + HALO, :]
            halo[f, z, 8:14, :] = from_e[z, HALO * f : HALO * f + HALO, :]

        each(levels, 6, unpack)
    halo[4, 0, 2:8, :] = from_w[levels, 0:HALO, :]
    halo[4, 0, 8:14, :] = from_e[levels, 0:HALO, :]

    def turned(parts):
        rows = [zero] + parts + [zero] * (LANES // 8 - 1 - len(parts))
        return jnp.concatenate(rows, axis=0).T

    def group(g, _):
        for f, src in enumerate((p, u, v, w)):
            acc = None
            for zi in range(ZG):
                z = g * ZG + zi
                parts = [halo[f, z, 0:8, :]]
                parts += [src[z, 8 * b : 8 * b + 8, :] for b in range(blocks)]
                parts += [halo[f, z, 8:16, :]]
                parts = [pltpu.roll(part, (8 + 16 * zi) % LANES, 1) for part in parts]
                if acc is None:
                    acc = parts
                else:
                    acc = [jnp.where(lane_group == zi, part, old) for part, old in zip(parts, acc)]
            t = turned(acc)
            for zi in range(ZG):
                z = g * ZG + zi
                both = t[16 * zi : 16 * zi + 16]
                own[f, z] = both
                north[z, HALO * f : HALO * f + HALO, :] = both[2:8]
                south[z, HALO * f : HALO * f + HALO, :] = both[8:14]
        return 0

    lax.fori_loop(0, levels // ZG, group, 0)

    parts = [halo[4, 0, 0:8, :]]
    parts += [coef[8 * b : 8 * b + 8, :] for b in range(blocks)]
    parts += [halo[4, 0, 8:16, :]]
    t = turned([pltpu.roll(part, 8, 1) for part in parts])
    own_r[...] = t[0:16]
    for msg in (north, south):
        for b in range(3):
            msg[levels, 8 * b : 8 * b + 8, :] = zero
    north[levels, 0:HALO, :] = t[2:8]
    south[levels, 0:HALO, :] = t[8:14]


def step_kernel(
    ub, vb, pb, w_in, coef, from_w, from_e, own, own_r, from_s, from_n,
    u_out, v_out, w_out, p_out,
    P_, E_, W_, S_, M_, Q_, R_, sP, sE, sW, sQ, sM, sR, rows, T_,
):
    levels, size_x, _ = ub.shape
    blocks = size_x // 8
    starts = [8 * b for b in range(1, blocks + 3)]
    main = [OFF + 8 * b for b in range(blocks)]
    sstarts = [SROW, SROW + 8, NROW, NROW + 8]
    zero = jnp.zeros((8, LANES), jnp.float32)
    sub = iota8(0)
    lane = iota8(1)
    is_west, is_east = axis_ends("gx")
    is_south, is_north = axis_ends("gy")
    mask_w = (sub == 0) & is_west
    mask_e = (sub == 7) & is_east
    smask_w = (lane == OFF) & is_west
    smask_e = (lane == OFF + size_x - 1) & is_east
    smask_s = (sub == 0) & is_south
    smask_n = (sub == 7) & is_north
    lane0 = lane == 0
    lane127 = lane == LANES - 1
    AB = ACCEL * SPREAD

    def unpack(z):
        for f, src, dst, sdst in ((0, pb, P_, sP), (1, ub, S_, sQ), (2, vb, M_, sM), (3, w_in, W_, sW)):
            scale = 2.0 if f == 3 else 1.0
            lo = HALO * f
            for b in range(blocks):
                dst[z, OFF + 8 * b : OFF + 8 * b + 8, :] = src[z, 8 * b : 8 * b + 8, :] * scale
            dst[z, OFF - HALO : OFF, :] = from_w[z, lo : lo + HALO, :] * scale
            dst[z, OFF + size_x : OFF + size_x + HALO, :] = from_e[z, lo : lo + HALO, :] * scale
            sdst[z, SROW + 8 : SROW + 16, :] = own[f, z, 8:16, :] * scale
            sdst[z, NROW : NROW + 8, :] = own[f, z, 0:8, :] * scale
            sdst[z, SROW + 8 - HALO : SROW + 8, :] = from_s[z, lo : lo + HALO, :] * scale
            sdst[z, NROW + 8 : NROW + 8 + HALO, :] = from_n[z, lo : lo + HALO, :] * scale

    each(levels, 1, unpack)
    R_[OFF : OFF + size_x, :] = coef[...]
    R_[OFF - HALO : OFF, :] = from_w[levels, 0:HALO, :]
    R_[OFF + size_x : OFF + size_x + HALO, :] = from_e[levels, 0:HALO, :]
    sR[SROW + 8 : SROW + 16, :] = own_r[8:16, :]
    sR[NROW : NROW + 8, :] = own_r[0:8, :]
    sR[SROW + 8 - HALO : SROW + 8, :] = from_s[levels, 0:HALO, :]
    sR[NROW + 8 : NROW + 8 + HALO, :] = from_n[levels, 0:HALO, :]

    def strip_init(z):
        for s in sstarts:
            u = sQ[z, s : s + 8, :]
            v = sM[z, s : s + 8, :]
            v_s = sM[z, s - 1 : s + 7, :]
            sE[z, s : s + 8, :] = SPREAD * ((u - pltpu.roll(u, 1, 1)) + (v - v_s))
        rows[SUBSTEPS, pl.ds(2 * z, 1), :] = sM[z, SROW + 7 : SROW + 8, :]

    each(levels, 6, strip_init)

    def factors(coefs, dst, at):
        def body(z, prev):
            new = []
            for s, m in zip(at, prev):
                r = coefs[s : s + 8, :]
                m = 1.0 / (1.0 + 2.0 * r - r * r * m)
                dst[z, s : s + 8, :] = m
                new.append(m)
            return tuple(new)

        lax.fori_loop(0, levels, body, tuple(zero for _ in at))

    factors(sR, sM, sstarts)

    def substep(pp, qq, ww, mm, rr, at, sectioned, size, size_b):
        def down(z, qs, ds, last=False):
            new = []
            qn = None if last else [qq[z + 1, s : s + 8, :] for s in at]
            for i, s in enumerate(at):
                rhs = ww[z, s : s + 8, :] + (qs[i] if last else qs[i] - qn[i])
                if ds is not None:
                    rhs = rhs + rr[s : s + 8, :] * ds[i]
                d = mm[z, s : s + 8, :] * rhs
                ww[z, s : s + 8, :] = d
                new.append(d)
            return qn, tuple(new)

        groups = levels // size
        for i in range(size):
            sectioned(i)
        for i in range(size):
            sectioned(size + i)
        qs = [qq[0, s : s + 8, :] for s in at]
        ds = None
        for i in range(size - 1):
            qs, ds = down(i, qs, ds)

        def fwd(g, ds):
            for i in range(size):
                sectioned((g + 1) * size + i)
            qs = [qq[g * size - 1, s : s + 8, :] for s in at]
            for i in range(size):
                qs, ds = down(g * size - 1 + i, qs, ds)
            return ds

        ds = lax.fori_loop(1, groups - 1, fwd, ds)
        first = (groups - 1) * size - 1
        qs = [qq[first, s : s + 8, :] for s in at]
        for i in range(size):
            qs, ds = down(first + i, qs, ds)
        _, ws = down(levels - 1, qs, ds, last=True)

        def up(z, ws):
            new = []
            for j, s in enumerate(at):
                w = ww[z, s : s + 8, :] + mm[z, s : s + 8, :] * (rr[s : s + 8, :] * ws[j])
                ww[z, s : s + 8, :] = w
                pp[z + 1, s : s + 8, :] = qq[z + 1, s : s + 8, :] - 0.25 * (ws[j] - w)
                new.append(w)
            return tuple(new)

        for i in range(size_b - 1):
            ws = up(levels - 2 - i, ws)

        def bwd(g, ws):
            for i in range(size_b):
                ws = up(levels - 1 - size_b - g * size_b - i, ws)
            return ws

        ws = lax.fori_loop(0, levels // size_b - 1, bwd, ws)
        for j, s in enumerate(at):
            pp[0, s : s + 8, :] = qq[0, s : s + 8, :] - 0.25 * ws[j]

    def strip_step(k, _):
        def sectioned(z):
            for s in sstarts:
                p = sP[z, s : s + 8, :]
                p_s = sP[z, s - 1 : s + 7, :]
                p_n = sP[z, s + 1 : s + 9, :]
                p_w = jnp.where(smask_w, p, pltpu.roll(p, 1, 1))
                p_e = jnp.where(smask_e, 0.0, pltpu.roll(p, LANES - 1, 1))
                if s == SROW + 8:
                    p_s = jnp.where(smask_s, p, p_s)
                if s == NROW:
                    p_n = jnp.where(smask_n, 0.0, p_n)
                e = sE[z, s : s + 8, :] - AB * (((p_w + p_e) + (p_s + p_n)) - 4.0 * p)
                sE[z, s : s + 8, :] = e
                sQ[z, s : s + 8, :] = p - e
            edge_s = jnp.where(is_south, sP[z, SROW + 8 : SROW + 9, :], sP[z, SROW + 7 : SROW + 8, :])
            edge_n = jnp.where(is_north, 0.0, sP[z, NROW + 8 : NROW + 9, :])
            rows[k, pl.ds(2 * z, 1), :] = edge_s
            rows[k, pl.ds(lax.rem(2 * z + LANES - 1, LANES), 1), :] = edge_n

        substep(sP, sQ, sW, sM, sR, sstarts, sectioned, SU, 6)
        return 0

    lax.fori_loop(0, SUBSTEPS, strip_step, 0)

    for k in range(SUBSTEPS + 1):
        T_[k] = rows[k].T

    def edges(k, z, s):
        return pltpu.roll(T_[k, s : s + 8, :], lax.rem(2 * LANES - 2 * z, LANES), 1)

    def main_init(z):
        for s in starts:
            u = S_[z, s : s + 8, :]
            u_w = S_[z, s - 1 : s + 7, :]
            v = M_[z, s : s + 8, :]
            v_s = jnp.where(lane0, edges(SUBSTEPS, z, s), pltpu.roll(v, 1, 1))
            E_[z, s : s + 8, :] = SPREAD * ((u - u_w) + (v - v_s))

    each(levels, 3, main_init)

    def clear(z):
        for s in starts[1:]:
            S_[z, s : s + 8, :] = zero

    each(levels, 3, clear)
    factors(R_, M_, starts)

    def main_step(k, _):
        def sectioned(z):
            for s in starts:
                p = P_[z, s : s + 8, :]
                p_w = P_[z, s - 1 : s + 7, :]
                p_e = P_[z, s + 1 : s + 9, :]
                if s == main[0]:
                    p_w = jnp.where(mask_w, p, p_w)
                if s == main[-1]:
                    p_e = jnp.where(mask_e, 0.0, p_e)
                edge = edges(k, z, s)
                p_s = jnp.where(lane0, edge, pltpu.roll(p, 1, 1))
                p_n = jnp.where(lane127, edge, pltpu.roll(p, LANES - 1, 1))
                e = E_[z, s : s + 8, :] - AB * (((p_w + p_e) + (p_s + p_n)) - 4.0 * p)
                E_[z, s : s + 8, :] = e
                if s != starts[0]:
                    S_[z, s : s + 8, :] = S_[z, s : s + 8, :] + p
                Q_[z, s : s + 8, :] = p - e

        substep(P_, Q_, W_, M_, R_, starts, sectioned, MU, 3)
        return 0

    lax.fori_loop(0, SUBSTEPS, main_step, 0)

    total = T_[0]
    for k in range(1, SUBSTEPS):
        total = total + T_[k]
    T_[0] = total

    def finish(z):
        for b, s in enumerate(main):
            at = slice(8 * b, 8 * b + 8)
            total = S_[z, s : s + 8, :]
            east = S_[z, s + 1 : s + 9, :]
            if s == main[-1]:
                east = jnp.where(mask_e, 0.0, east)
            north = jnp.where(lane127, edges(0, z, s), pltpu.roll(total, LANES - 1, 1))
            u_out[z, at, :] = ub[z, at, :] - ACCEL * (east - total)
            v_out[z, at, :] = vb[z, at, :] - ACCEL * (north - total)
            w_out[z, at, :] = 0.5 * W_[z, s : s + 8, :]
            p_out[z, at, :] = P_[z, s : s + 8, :]

    each(levels, 3, finish)


def per_device(u_wind, v_wind, w_wind, pressure, vert_coef, we_slab, sn_slab, relax_width):
    levels, size_x, size_y = pressure.shape
    nx = float(size_x * lax.axis_size("gx"))
    ny = float(size_y * lax.axis_size("gy"))
    weg = to_edges(we_slab, "gx")
    sng = to_edges(sn_slab, "gy")
    sng = jnp.transpose(sng, (1, 0, 2, 3)).reshape(8, size_x, LANES)
    f32 = jnp.float32
    block = jax.ShapeDtypeStruct(pressure.shape, f32)
    message = jax.ShapeDtypeStruct((levels + 1, 4 * HALO, LANES), f32)
    ext = size_x + 2 * OFF

    bands = pltpu.VMEM((3, 512, LANES), f32)
    turned = pltpu.VMEM((3, 4, LANES, LANES), f32)
    east, west = pl.pallas_call(
        lambda *refs: rim_kernel(ny, *refs),
        out_shape=(message, message),
        in_specs=[VMEM] * 7,
        out_specs=[VMEM] * 2,
        scratch_shapes=[bands, turned],
        compiler_params=pltpu.CompilerParams(vmem_limit_bytes=24 << 20),
        name="rims",
    )(u_wind, v_wind, pressure, w_wind, vert_coef, relax_width, sng)
    ub, vb, pb = pl.pallas_call(
        lambda *refs: blend_kernel(nx, ny, *refs),
        out_shape=(block, block, block),
        in_specs=[VMEM] * 6,
        out_specs=[VMEM] * 3,
        scratch_shapes=[bands, bands, bands, turned],
        compiler_params=pltpu.CompilerParams(vmem_limit_bytes=24 << 20),
        name="blend",
    )(u_wind, v_wind, pressure, relax_width, weg, sng)
    from_w = passed_along(east, "gx", 1)
    from_e = passed_along(west, "gx", -1)

    own, own_r, north, south = pl.pallas_call(
        strip_kernel,
        out_shape=(
            jax.ShapeDtypeStruct((4, levels, 16, LANES), f32),
            jax.ShapeDtypeStruct((16, LANES), f32),
            message,
            message,
        ),
        in_specs=[VMEM] * 7,
        out_specs=[VMEM] * 4,
        scratch_shapes=[pltpu.VMEM((5, levels, 16, LANES), f32)],
        compiler_params=pltpu.CompilerParams(vmem_limit_bytes=24 << 20),
        name="strips",
    )(pb, ub, vb, w_wind, vert_coef, from_w, from_e)
    from_s = passed_along(north, "gy", 1)
    from_n = passed_along(south, "gy", -1)

    big = pltpu.VMEM((levels, ext, LANES), f32)
    strip = pltpu.VMEM((levels, SROWS, LANES), f32)
    return pl.pallas_call(
        step_kernel,
        out_shape=(block, block, block, block),
        in_specs=[VMEM] * 11,
        out_specs=[VMEM] * 4,
        scratch_shapes=[big] * 6
        + [pltpu.VMEM((ext, LANES), f32)]
        + [strip] * 5
        + [
            pltpu.VMEM((SROWS, LANES), f32),
            pltpu.VMEM((SUBSTEPS + 1, LANES, LANES), f32),
            pltpu.VMEM((SUBSTEPS + 1, LANES, LANES), f32),
        ],
        compiler_params=pltpu.CompilerParams(vmem_limit_bytes=40 << 20),
        name="substeps",
    )(ub, vb, pb, w_wind, vert_coef, from_w, from_e, own, own_r, from_s, from_n)


def solution(mesh):
    placed = (
        P(None, "gx", "gy"),
        P(None, "gx", "gy"),
        P(None, "gx", "gy"),
        P(None, "gx", "gy"),
        P("gx", "gy"),
        P(None, None, None, None, ("gy", "gx")),
        P(None, None, None, None, ("gx", "gy")),
        P("gx", "gy"),
    )
    return jax.shard_map(
        per_device,
        mesh=mesh,
        in_specs=placed,
        out_specs=(P(None, "gx", "gy"),) * 4,
        check_vma=False,
    )
```

time: 205 us -> 130 us (0.63)
  Pallas kernels: 118 us -> 54.5 us
  waiting for transfers between devices: 46.4 us -> 20.9 us
  blocking collectives: 0 us -> 24.7 us
  starting transfers between devices: 27.6 us -> 20.7 us
  local copies, waits for them, and re-layouts: 9.59 us -> 6.79 us
    pallas_call x1, Pallas kernels: 107 us -> 48.4 us  [per_device(): pl.pallas_call(step_kernel, out_shape=(block, block, block, block), in_sp...]
    all_to_all x0 -> x1, blocking collectives: none -> 24.7 us  [to_edges(): return lax.all_to_all(sent, axis, 0, 0, tiled=True)]
    ppermute x4, waiting for transfers between devices: 33.9 us -> 14.6 us  [passed_along(): return lax.ppermute(block, axis, route)]
    all_to_all x2 -> x1, waiting for transfers between devices: 12.5 us -> 6.32 us  [to_edges(): return lax.all_to_all(sent, axis, 0, 0, tiled=True)]
    all_to_all x2 -> x1, starting transfers between devices: 13 us -> 8.39 us  [to_edges(): return lax.all_to_all(sent, axis, 0, 0, tiled=True)]
    pallas_call x1, Pallas kernels: 8.67 us -> 5.28 us  [per_device(): pl.pallas_call(strip_kernel, out_shape=(jax.ShapeDtypeStruct((4, levels,...]
    unnamed x30 -> x12, local copies, waits for them, and re-layouts: 7.45 us -> 4.64 us
    ppermute x4, starting transfers between devices: 14.6 us -> 12.3 us  [passed_along(): return lax.ppermute(block, axis, route)]
  transfers between devices with their start and end apart: 6 -> 5, of which waited for: 6 -> 3; matrix products, arithmetic and copies ran while one was open for 1% -> 1% of each run, Pallas kernels for 0% -> 0%
where the time goes in v2:
time: 130 us; the launch traced here: 129 us
  Pallas kernels  54.5 us (42%)
  blocking collectives  24.7 us (19%)
  waiting for transfers between devices  20.9 us (16%)
  starting transfers between devices  20.7 us (16%)
  local copies, waits for them, and re-layouts  6.79 us (5%)
    pallas_call x1, Pallas kernels, per_device(): pl.pallas_call(step_kernel, out_shape=(block, block, block, block), in_sp...  48.4 us
    all_to_all x1, blocking collectives, to_edges(): return lax.all_to_all(sent, axis, 0, 0, tiled=True)  24.7 us
    ppermute x4, waiting for transfers between devices, passed_along(): return lax.ppermute(block, axis, route)  14.6 us
    ppermute x4, starting transfers between devices, passed_along(): return lax.ppermute(block, axis, route)  12.3 us
    all_to_all x1, starting transfers between devices, to_edges(): return lax.all_to_all(sent, axis, 0, 0, tiled=True)  8.39 us
    all_to_all x1, waiting for transfers between devices, to_edges(): return lax.all_to_all(sent, axis, 0, 0, tiled=True)  6.32 us
    pallas_call x1, Pallas kernels, per_device(): pl.pallas_call(strip_kernel, out_shape=(jax.ShapeDtypeStruct((4, levels,...  5.28 us
    unnamed x12, local copies, waits for them, and re-layouts  4.64 us
  transfers between devices with their start and end apart: 5, of which 3 were waited for; matrix products, arithmetic and copies ran while one was open for 1% of the time, Pallas kernels for 0%

profile of v2, /device:TPU:31, one launch (start us, length us, event | category | flops | bytes accessed | tf_op | source)
XLA Modules:
  0.0 129.5 jit_solution(7345750794944065544)
XLA Ops:
  0.6 0.0 copy-start.4
  0.6 0.0 copy-start
  0.7 0.0 copy-start.5
  0.7 0.9 fusion.1
  1.6 0.1 pad.37.clone
  1.7 0.1 add_bitcast_fusion.2
  1.8 0.8 pad_maximum_fusion.1
  2.6 8.4 %all-to-all-start.1 = ((f32[16,8,4,128]{3,2,1,0:T(4,128)}), f32[16,8,4,128]{3,2,1,0:T(4,128)S(1)}, u32[]{:S(2)}, u32[]{:S(2)}) async-start(f32[16,8,4,128]{3,2,1,0:T(4,128)} %pad_maximum_fusion.1), calls=%async_computation.1 | async-start | bytes 524288 | tf_op jit(solution)/shard_map/all_to_all | solution.py:44
  11.0 1.0 fusion
  12.1 6.3 %all-to-all-done.1 = f32[16,8,4,128]{3,2,1,0:T(4,128)S(1)} async-done(((f32[16,8,4,128]{3,2,1,0:T(4,128)}), f32[16,8,4,128]{3,2,1,0:T(4,128)S(1)}, u32[]{:S(2)}, u32[]{:S(2)}) %all-to-all-start.1) | async-done | bytes 262176 | tf_op jit(solution)/shard_map/all_to_all | solution.py:44
  18.4 0.0 copy-done.4
  18.4 0.0 copy-done
  18.5 0.0 copy-start.1
  18.5 1.5 %copy-done.1 = f32[60,64,128]{2,1,0:T(8,128)S(1)} copy-done((f32[60,64,128]{2,1,0:T(8,128)S(1)}, f32[60,64,128]{2,1,0:T(8,128)}, u32[]{:S(2)}) %copy-start.1) | copy-done | bytes 1966104
  20.0 1.5 %copy-done.2 = f32[60,64,128]{2,1,0:T(8,128)S(1)} copy-done((f32[60,64,128]{2,1,0:T(8,128)S(1)}, f32[60,64,128]{2,1,0:T(8,128)}, u32[]{:S(2)}) %copy-start.2) | copy-done | bytes 1966104
  21.5 1.5 %copy-done.3 = f32[60,64,128]{2,1,0:T(8,128)S(1)} copy-done((f32[60,64,128]{2,1,0:T(8,128)S(1)}, f32[60,64,128]{2,1,0:T(8,128)}, u32[]{:S(2)}) %copy-start.3) | copy-done | bytes 1966104
  23.1 0.4 rims.1
  23.5 2.3 %collective-permute-start = (f32[61,24,128]{2,1,0:T(8,128)S(1)}, f32[61,24,128]{2,1,0:T(8,128)S(1)}, u32[]{:S(2)}, u32[]{:S(2)}) collective-permute-start(f32[61,24,128]{2,1,0:T(8,128)S(1)} %get-tuple-element.16), channel_id=1, source_target_pairs={{0,16},{16,32},{32,48},{48,64},{64,80},{80,96},{96,112},{1,17},{17... | collective-permute-start | bytes 2248712 | tf_op jit(solution)/shard_map/ppermute | solution.py:27
  25.8 3.0 %collective-permute-start.1 = (f32[61,24,128]{2,1,0:T(8,128)S(1)}, f32[61,24,128]{2,1,0:T(8,128)S(1)}, u32[]{:S(2)}, u32[]{:S(2)}) collective-permute-start(f32[61,24,128]{2,1,0:T(8,128)S(1)} %get-tuple-element.17), channel_id=1, source_target_pairs={{16,0},{32,16},{48,32},{64,48},{80,64},{96,80},{112,96},{17,1},{33... | collective-permute-start | bytes 2248712 | tf_op jit(solution)/shard_map/ppermute | solution.py:27
  28.8 0.1 add_bitcast_fusion
  28.9 0.1 pad.40.clone
  29.0 0.1 pad_maximum_fusion
  29.1 24.7 %all_to_all.10.refs_4_ = f32[8,8,16,128]{3,2,1,0:T(8,128)S(1)} all-to-all(f32[8,8,16,128]{3,2,1,0:T(8,128)S(1)} %pad_maximum_fusion), channel_id=1, replica_groups=mesh['gx'=8,'gy'=16] {'gx'}, dimensions={0} | all-to-all | bytes 1048576 | tf_op jit(solution)/shard_map/all_to_all | solution.py:44
  53.7 0.4 blend.1
  54.2 0.0 collective-permute-done.from_w
  54.2 0.0 collective-permute-done.1.from_e
  54.2 5.3 %strips.1 = (f32[4,60,16,128]{3,2,1,0:T(8,128)S(1)}, f32[16,128]{1,0:T(8,128)S(1)}, f32[61,24,128]{2,1,0:T(8,128)S(1)}, f32[61,24,128]{2,1,0:T(8,128)S(1)}) custom-call(f32[60,64,128]{2,1,0:T(8,128)S(1)} %get-tuple-element.15.p.pb, f32[60,64,128]{2,1,0:T(8,128)S(1)} %get-tuple-element.13.u.ub, f32[60,64,128]{2,1,0:T(8,128)S(1)} %get-tuple-element.14.v.vb, ...), custom_call_target="tpu_custom_call" | custom-call | tf_op jit(solution)/shard_map/strips/pallas_call | solution.py:522
  59.5 5.1 %collective-permute-start.2 = (f32[61,24,128]{2,1,0:T(8,128)S(1)}, f32[61,24,128]{2,1,0:T(8,128)S(1)}, u32[]{:S(2)}, u32[]{:S(2)}) collective-permute-start(f32[61,24,128]{2,1,0:T(8,128)S(1)} %get-tuple-element.20), channel_id=1, source_target_pairs={{0,1},{1,2},{2,3},{3,4},{4,5},{5,6},{6,7},{7,8},{8,9},{9,10},{10,1... | collective-permute-start | bytes 2248712 | tf_op jit(solution)/shard_map/ppermute | solution.py:27
  64.6 1.9 %collective-permute-start.3 = (f32[61,24,128]{2,1,0:T(8,128)S(1)}, f32[61,24,128]{2,1,0:T(8,128)S(1)}, u32[]{:S(2)}, u32[]{:S(2)}) collective-permute-start(f32[61,24,128]{2,1,0:T(8,128)S(1)} %get-tuple-element.21), channel_id=1, source_target_pairs={{1,0},{2,1},{3,2},{4,3},{5,4},{6,5},{7,6},{8,7},{9,8},{10,9},{11,1... | collective-permute-start | bytes 2248712 | tf_op jit(solution)/shard_map/ppermute | solution.py:27
  66.5 6.6 %collective-permute-done.2.from_s = f32[61,24,128]{2,1,0:T(8,128)S(1)} collective-permute-done((f32[61,24,128]{2,1,0:T(8,128)S(1)}, f32[61,24,128]{2,1,0:T(8,128)S(1)}, u32[]{:S(2)}, u32[]{:S(2)}) %collective-permute-start.2) | collective-permute-done | bytes 749600 | tf_op jit(solution)/shard_map/ppermute | solution.py:27
  73.1 8.0 %collective-permute-done.3.from_n = f32[61,24,128]{2,1,0:T(8,128)S(1)} collective-permute-done((f32[61,24,128]{2,1,0:T(8,128)S(1)}, f32[61,24,128]{2,1,0:T(8,128)S(1)}, u32[]{:S(2)}, u32[]{:S(2)}) %collective-permute-start.3) | collective-permute-done | bytes 749600 | tf_op jit(solution)/shard_map/ppermute | solution.py:27
  81.1 48.4 %substeps.1 = (f32[60,64,128]{2,1,0:T(8,128)}, f32[60,64,128]{2,1,0:T(8,128)}, f32[60,64,128]{2,1,0:T(8,128)}, f32[60,64,128]{2,1,0:T(8,128)}) custom-call(f32[60,64,128]{2,1,0:T(8,128)S(1)} %get-tuple-element.13.u.ub, f32[60,64,128]{2,1,0:T(8,128)S(1)} %get-tuple-element.14.v.vb, f32[60,64,128]{2,1,0:T(8,128)S(1)} %get-tuple-element.15.p.pb, ...), custom_call_target="tpu_custom_call" | custom-call | tf_op jit(solution)/shard_map/substeps/pallas_call | solution.py:541
  (16 shorter events, 0.1 us)
Async XLA Ops:
  0.6 17.8 %copy-start.4 = (f32[64,128]{1,0:T(8,128)S(1)}, f32[64,128]{1,0:T(8,128)}, u32[]{:S(2)}) copy-start(f32[64,128]{1,0:T(8,128)} %coef.3) | copy-start | bytes 98308
  0.6 17.8 %copy-start = (f32[60,64,128]{2,1,0:T(8,128)S(1)}, f32[60,64,128]{2,1,0:T(8,128)}, u32[]{:S(2)}) copy-start(f32[60,64,128]{2,1,0:T(8,128)} %w_in.1) | copy-start | bytes 5898244
  0.7 17.8 %copy-start.5 = (s32[64,128]{1,0:T(8,128)S(1)}, s32[64,128]{1,0:T(8,128)}, u32[]{:S(2)}) copy-start(s32[64,128]{1,0:T(8,128)} %refs_5_.1) | copy-start | bytes 98308
  2.6 15.8 %all-to-all-start.1 = ((f32[16,8,4,128]{3,2,1,0:T(4,128)}), f32[16,8,4,128]{3,2,1,0:T(4,128)S(1)}, u32[]{:S(2)}, u32[]{:S(2)}) async-start(f32[16,8,4,128]{3,2,1,0:T(4,128)} %pad_maximum_fusion.1), calls=%async_computation.1 | async-start | bytes 524288 | tf_op jit(solution)/shard_map/all_to_all | solution.py:44
  18.5 1.5 %copy-start.1 = (f32[60,64,128]{2,1,0:T(8,128)S(1)}, f32[60,64,128]{2,1,0:T(8,128)}, u32[]{:S(2)}) copy-start(f32[60,64,128]{2,1,0:T(8,128)} %refs_0_.3) | copy-start | bytes 5898244
  20.0 1.5 %copy-start.2 = (f32[60,64,128]{2,1,0:T(8,128)S(1)}, f32[60,64,128]{2,1,0:T(8,128)}, u32[]{:S(2)}) copy-start(f32[60,64,128]{2,1,0:T(8,128)} %refs_1_.3) | copy-start | bytes 5898244
  21.5 1.5 %copy-start.3 = (f32[60,64,128]{2,1,0:T(8,128)S(1)}, f32[60,64,128]{2,1,0:T(8,128)}, u32[]{:S(2)}) copy-start(f32[60,64,128]{2,1,0:T(8,128)} %refs_2_.3) | copy-start | bytes 5898244
  23.5 30.7 %collective-permute-start = (f32[61,24,128]{2,1,0:T(8,128)S(1)}, f32[61,24,128]{2,1,0:T(8,128)S(1)}, u32[]{:S(2)}, u32[]{:S(2)}) collective-permute-start(f32[61,24,128]{2,1,0:T(8,128)S(1)} %get-tuple-element.16), channel_id=1, source_target_pairs={{0,16},{16,32},{32,48},{48,64},{64,80},{80,96},{96,112},{1,17},{17... | collective-permute-start | bytes 2248712 | tf_op jit(solution)/shard_map/ppermute | solution.py:27
  25.8 28.4 %collective-permute-start.1 = (f32[61,24,128]{2,1,0:T(8,128)S(1)}, f32[61,24,128]{2,1,0:T(8,128)S(1)}, u32[]{:S(2)}, u32[]{:S(2)}) collective-permute-start(f32[61,24,128]{2,1,0:T(8,128)S(1)} %get-tuple-element.17), channel_id=1, source_target_pairs={{16,0},{32,16},{48,32},{64,48},{80,64},{96,80},{112,96},{17,1},{33... | collective-permute-start | bytes 2248712 | tf_op jit(solution)/shard_map/ppermute | solution.py:27
  59.5 13.6 %collective-permute-start.2 = (f32[61,24,128]{2,1,0:T(8,128)S(1)}, f32[61,24,128]{2,1,0:T(8,128)S(1)}, u32[]{:S(2)}, u32[]{:S(2)}) collective-permute-start(f32[61,24,128]{2,1,0:T(8,128)S(1)} %get-tuple-element.20), channel_id=1, source_target_pairs={{0,1},{1,2},{2,3},{3,4},{4,5},{5,6},{6,7},{7,8},{8,9},{9,10},{10,1... | collective-permute-start | bytes 2248712 | tf_op jit(solution)/shard_map/ppermute | solution.py:27
  64.6 16.5 %collective-permute-start.3 = (f32[61,24,128]{2,1,0:T(8,128)S(1)}, f32[61,24,128]{2,1,0:T(8,128)S(1)}, u32[]{:S(2)}, u32[]{:S(2)}) collective-permute-start(f32[61,24,128]{2,1,0:T(8,128)S(1)} %get-tuple-element.21), channel_id=1, source_target_pairs={{1,0},{2,1},{3,2},{4,3},{5,4},{6,5},{7,6},{8,7},{9,8},{10,9},{11,1... | collective-permute-start | bytes 2248712 | tf_op jit(solution)/shard_map/ppermute | solution.py:27

commit v3 on v2

v3 whole, which is shorter than its diff:
```python
import jax
import jax.numpy as jnp
from jax import lax
from jax.experimental import pallas as pl
from jax.experimental.pallas import tpu as pltpu
from jax.sharding import PartitionSpec as P


SUBSTEPS = 6
HALO = 6
OFF = 16
ZG = 6
SB = 5
ZS = 12
LANES = 128
ACCEL = 0.3
SPREAD = 0.3
SROW = 8
NROW = 24
SROWS = 48
MU = 10
SU = 12

VMEM = pl.BlockSpec(memory_space=pltpu.VMEM)
HBM = pl.BlockSpec(memory_space=pltpu.HBM)


def passed_along(block, axis, distance):
    devices = range(lax.axis_size(axis))
    route = [(i - distance, i) for i in devices if i - distance in devices]
    return lax.ppermute(block, axis, route)


def lane_pairs(bands):
    levels = bands.shape[-1]
    low = jnp.pad(bands[:8], ((0, 0), (0, 0), (0, LANES - levels)))
    high = jnp.pad(bands[8:], ((0, 1), (0, 0), (64, 64 - levels)))
    return low + high


def to_edges(slab, axis):
    size = lax.axis_size(axis)
    t = jnp.transpose(slab, (0, 1, 3, 4, 2))
    first = lane_pairs(t[0].reshape(15, *t.shape[3:]))
    last = lane_pairs(t[1, :, ::-1].reshape(15, *t.shape[3:]))
    zero = jnp.zeros((size - 2, *first.shape), first.dtype)
    sent = jnp.concatenate([first[None], zero, last[None]], axis=0)
    return lax.all_to_all(sent, axis, 0, 0, tiled=True)


def iota8(dim):
    return lax.broadcasted_iota(jnp.int32, (8, LANES), dim)


def axis_ends(axis):
    at = lax.axis_index(axis)
    return at == 0, at == lax.axis_size(axis) - 1


def loop(count, unroll, body, carry):
    assert count % unroll == 0

    def trip(g, carry):
        for i in range(unroll):
            carry = body(g * unroll + i, carry)
        return carry

    return lax.fori_loop(0, count // unroll, trip, carry)


def each(count, unroll, body):
    def step(i, carry):
        body(i)
        return carry

    loop(count, unroll, step, 0)


def side_bands(sn_w, sng, sn_e, bs, bt):
    zero = jnp.zeros((8, LANES), jnp.float32)
    spare = jnp.zeros((LANES - 16 - sng.shape[1], LANES), jnp.float32)

    def clear(i):
        for k in range(3):
            bs[k, pl.ds(pl.multiple_of(i * 8, 8), 8), :] = zero

    each(64, 4, clear)
    for s in range(8):
        b = jnp.concatenate([sn_w[s], sng[s], sn_e[s], spare], axis=0).T
        for half in range(2):
            kj = s + 8 * half
            if kj < 15:
                bs[kj // 5, pl.ds(kj % 5, 64, stride=8), :] = b[64 * half : 64 * half + 64]
    for k in range(3):
        for g in range(4):
            bt[k, g] = bs[k, g * LANES : (g + 1) * LANES, :].T


def end_bands(weg, cw, ce):
    groups = weg.shape[0]
    zero = jnp.zeros((8, LANES), jnp.float32)

    def clear(i):
        for k in range(3):
            cw[k, pl.ds(pl.multiple_of(i * 8, 8), 8), :] = zero
            ce[k, pl.ds(pl.multiple_of(i * 8, 8), 8), :] = zero

    each(64, 4, clear)
    for s in range(8):
        a = jnp.concatenate([weg[g, s] for g in range(groups)], axis=0).T
        for half in range(2):
            kj = s + 8 * half
            if kj < 15:
                k, j = kj // 5, kj % 5
                cw[k, pl.ds(j, 64, stride=8), :] = a[64 * half : 64 * half + 64]
                ce[k, pl.ds(3 + j, 64, stride=8), :] = a[64 * half : 64 * half + 64]


def rim_kernel(p, u, v, w, coef, width, east, west, held, sems):
    levels, size_x, _ = u.shape
    zero = jnp.zeros((8, LANES), jnp.float32)
    copies = []
    for f, src in enumerate((p, u, v, w)):
        for side, lo in enumerate((size_x - 8, 0)):
            copies.append(pltpu.make_async_copy(src.at[:, lo : lo + 8, :], held.at[side, f], sems.at[side, f]))
    for copy in copies:
        copy.start()
    for msg, lo in ((east, size_x - HALO), (west, 0)):
        for b in range(3):
            msg[levels, 8 * b : 8 * b + 8, :] = zero
        msg[levels, 0:HALO, :] = coef[lo : lo + HALO, :]
        msg[levels, HALO : 2 * HALO, :] = width[lo : lo + HALO, :].astype(jnp.float32)
    for copy in copies:
        copy.wait()

    def pack(z):
        for f in range(4):
            east[z, HALO * f : HALO * f + HALO, :] = held[0, f, z, 8 - HALO : 8, :]
            west[z, HALO * f : HALO * f + HALO, :] = held[1, f, z, 0:HALO, :]

    each(levels, 4, pack)


def strip_kernel(
    nx, ny, p, u, v, w, coef, width, weg, sn_w, sng, sn_e, from_w, from_e,
    px, ux, vx, wx, halo_r, own, own_r, north, south,
    cw, ce, bs, bt, rate_, sems,
):
    levels, size_x, _ = u.shape
    blocks = size_x // 8
    starts = [OFF - 8 + 8 * b for b in range(blocks + 2)]
    ends_at = (OFF, OFF + size_x - 8)
    zero = jnp.zeros((8, LANES), jnp.float32)
    is_west, is_east = axis_ends("gx")
    is_south, is_north = axis_ends("gy")
    fields = ((p, px, 2), (u, ux, 0), (v, vx, 1), (w, wx, None))
    copies = [
        pltpu.make_async_copy(src, dst.at[:, OFF : OFF + size_x, :], sems.at[f])
        for f, (src, dst, _) in enumerate(fields)
    ]
    for copy in copies:
        copy.start()

    for f, (_, dst, _) in enumerate(fields):

        def unpack(z):
            dst[z, OFF - HALO : OFF, :] = from_w[z, HALO * f : HALO * f + HALO, :]
            dst[z, OFF + size_x : OFF + size_x + HALO, :] = from_e[z, HALO * f : HALO * f + HALO, :]

        each(levels, 6, unpack)
    halo_r[2:8, :] = from_w[levels, 0:HALO, :]
    halo_r[8:14, :] = from_e[levels, 0:HALO, :]

    @pl.when(is_west | is_east)
    def _():
        end_bands(weg, cw, ce)

    @pl.when(is_south | is_north)
    def _():
        side_bands(sn_w, sng, sn_e, bs, bt)
        rate_[2:8, :] = from_w[levels, HALO : 2 * HALO, :]
        rate_[8 : 8 + size_x, :] = width[...].astype(jnp.float32)
        rate_[8 + size_x : 14 + size_x, :] = from_e[levels, HALO : 2 * HALO, :]

    def ends(dst, k):
        x = iota8(0).astype(jnp.float32) + (lax.axis_index("gx") * size_x).astype(jnp.float32)
        rate_w = width[0:8, :].astype(jnp.float32)
        rate_e = width[size_x - 8 : size_x, :].astype(jnp.float32)
        weight_w = jnp.maximum(rate_w - x, 0.0) / rate_w
        weight_e = jnp.maximum(rate_e - ((nx - 1.0) - (x + (size_x - 8.0))), 0.0) / rate_e

        def body(z):
            rows = pl.ds(pl.multiple_of(z * 8, 8), 8)
            for at, weight, band in zip(ends_at, (weight_w, weight_e), (cw, ce)):
                val = dst[z, at : at + 8, :]
                dst[z, at : at + 8, :] = val + weight * (band[k, rows, :] - val)

        each(levels, 6, body)

    def sides(dst, k):
        y = iota8(1).astype(jnp.float32) + (lax.axis_index("gy") * LANES).astype(jnp.float32)
        dist = jnp.where(is_north, (ny - 1.0) - y, y)
        base = jnp.where(is_north, 123 + LANES, LANES)
        for first in range(0, blocks + 2, SB):
            some = range(first, min(first + SB, blocks + 2))
            weights = []
            for b in some:
                rate = jnp.maximum(rate_[8 * b : 8 * b + 8, :], 1.0)
                weights.append(jnp.maximum(rate - dist, 0.0) / rate)

            def trip(g, _):
                new = []
                for i in range(ZS):
                    z = g * ZS + i
                    shift = lax.rem(base - 8 * lax.rem(z, 16), LANES)
                    for b, weight in zip(some, weights):
                        band = pltpu.roll(bt[k, z // 16, 8 * b : 8 * b + 8, :], shift, 1)
                        val = dst[z, starts[b] : starts[b] + 8, :]
                        new.append(val + weight * (band - val))
                for i in range(ZS):
                    for j, b in enumerate(some):
                        dst[g * ZS + i, starts[b] : starts[b] + 8, :] = new[i * len(some) + j]
                return 0

            lax.fori_loop(0, levels // ZS, trip, 0)

    lane_group = iota8(1) // 16

    def turned(parts):
        rows = [zero] + parts + [zero] * (LANES // 8 - 1 - len(parts))
        return jnp.concatenate(rows, axis=0).T

    for f, (_, dst, k) in enumerate(fields):
        copies[f].wait()
        if k is not None:

            @pl.when(is_west | is_east)
            def _():
                ends(dst, k)

            @pl.when(is_south | is_north)
            def _():
                sides(dst, k)

        def group(g, _):
            acc = None
            for zi in range(ZG):
                z = g * ZG + zi
                parts = [dst[z, s : s + 8, :] for s in starts]
                if k is None:
                    parts = [2.0 * part for part in parts]
                    for s, part in zip(starts, parts):
                        dst[z, s : s + 8, :] = part
                parts = [pltpu.roll(part, (8 + 16 * zi) % LANES, 1) for part in parts]
                if acc is None:
                    acc = parts
                else:
                    acc = [jnp.where(lane_group == zi, part, old) for part, old in zip(parts, acc)]
            t = turned(acc)
            for zi in range(ZG):
                z = g * ZG + zi
                both = t[16 * zi : 16 * zi + 16]
                own[f, z] = both
                north[z, HALO * f : HALO * f + HALO, :] = both[2:8]
                south[z, HALO * f : HALO * f + HALO, :] = both[8:14]
            return 0

        lax.fori_loop(0, levels // ZG, group, 0, unroll=2)

    parts = [halo_r[0:8, :]]
    parts += [coef[8 * b : 8 * b + 8, :] for b in range(blocks)]
    parts += [halo_r[8:16, :]]
    t = turned([pltpu.roll(part, 8, 1) for part in parts])
    own_r[...] = t[0:16]
    for msg in (north, south):
        for b in range(3):
            msg[levels, 8 * b : 8 * b + 8, :] = zero
    north[levels, 0:HALO, :] = t[2:8]
    south[levels, 0:HALO, :] = t[8:14]


def step_kernel(
    px, ux, vx, wx, coef, halo_r, own, own_r, from_s, from_n,
    u_out, v_out, w_out, p_out,
    P_, E_, W_, S_, M_, Q_, R_, sP, sE, sW, sQ, sM, sR, rows, T_, sems,
):
    levels, size_x, _ = u_out.shape
    blocks = size_x // 8
    starts = [8 * b for b in range(1, blocks + 3)]
    main = [OFF + 8 * b for b in range(blocks)]
    sstarts = [SROW, SROW + 8, NROW, NROW + 8]
    zero = jnp.zeros((8, LANES), jnp.float32)
    sub = iota8(0)
    lane = iota8(1)
    is_west, is_east = axis_ends("gx")
    is_south, is_north = axis_ends("gy")
    mask_w = (sub == 0) & is_west
    mask_e = (sub == 7) & is_east
    smask_w = (lane == OFF) & is_west
    smask_e = (lane == OFF + size_x - 1) & is_east
    smask_s = (sub == 0) & is_south
    smask_n = (sub == 7) & is_north
    lane0 = lane == 0
    lane127 = lane == LANES - 1
    AB = ACCEL * SPREAD

    def unpack(z):
        for f, dst in enumerate((sP, sQ, sM, sW)):
            lo = HALO * f
            dst[z, SROW + 8 : SROW + 16, :] = own[f, z, 8:16, :]
            dst[z, NROW : NROW + 8, :] = own[f, z, 0:8, :]
            dst[z, SROW + 8 - HALO : SROW + 8, :] = from_s[z, lo : lo + HALO, :]
            dst[z, NROW + 8 : NROW + 8 + HALO, :] = from_n[z, lo : lo + HALO, :]

    each(levels, 2, unpack)
    R_[OFF : OFF + size_x, :] = coef[...]
    R_[OFF - 8 : OFF, :] = halo_r[0:8, :]
    R_[OFF + size_x : OFF + size_x + 8, :] = halo_r[8:16, :]
    sR[SROW + 8 : SROW + 16, :] = own_r[8:16, :]
    sR[NROW : NROW + 8, :] = own_r[0:8, :]
    sR[SROW + 8 - HALO : SROW + 8, :] = from_s[levels, 0:HALO, :]
    sR[NROW + 8 : NROW + 8 + HALO, :] = from_n[levels, 0:HALO, :]

    def strip_init(z):
        for s in sstarts:
            u = sQ[z, s : s + 8, :]
            v = sM[z, s : s + 8, :]
            v_s = sM[z, s - 1 : s + 7, :]
            sE[z, s : s + 8, :] = SPREAD * ((u - pltpu.roll(u, 1, 1)) + (v - v_s))
        rows[SUBSTEPS, pl.ds(2 * z, 1), :] = sM[z, SROW + 7 : SROW + 8, :]

    each(levels, 6, strip_init)

    def factors(coefs, dst, at):
        def body(z, prev):
            new = []
            for s, m in zip(at, prev):
                r = coefs[s : s + 8, :]
                m = 1.0 / (1.0 + 2.0 * r - r * r * m)
                dst[z, s : s + 8, :] = m
                new.append(m)
            return tuple(new)

        lax.fori_loop(0, levels, body, tuple(zero for _ in at))

    factors(sR, sM, sstarts)

    def descend(qq, ww, mm, rr, at, sectioned, size):
        def down(z, qs, ds, last=False):
            new = []
            qn = None if last else [qq[z + 1, s : s + 8, :] for s in at]
            for i, s in enumerate(at):
                rhs = ww[z, s : s + 8, :] + (qs[i] if last else qs[i] - qn[i])
                if ds is not None:
                    rhs = rhs + rr[s : s + 8, :] * ds[i]
                d = mm[z, s : s + 8, :] * rhs
                ww[z, s : s + 8, :] = d
                new.append(d)
            return qn, tuple(new)

        groups = levels // size
        for i in range(2 * size):
            sectioned(i)
        qs = [qq[0, s : s + 8, :] for s in at]
        ds = None
        for i in range(size - 1):
            qs, ds = down(i, qs, ds)

        def fwd(g, ds):
            qs = [qq[g * size - 1, s : s + 8, :] for s in at]
            for i in range(size):
                qs, ds = down(g * size - 1 + i, qs, ds)
            for i in range(size):
                sectioned((g + 1) * size + i)
            return ds

        ds = lax.fori_loop(1, groups - 1, fwd, ds)
        first = (groups - 1) * size - 1
        qs = [qq[first, s : s + 8, :] for s in at]
        for i in range(size):
            qs, ds = down(first + i, qs, ds)
        return down(levels - 1, qs, ds, last=True)[1]

    def ascend(pp, qq, ww, mm, rr, at, ws, size, scale=1.0, done=None):
        def up(z, ws):
            new = []
            for j, s in enumerate(at):
                w = ww[z, s : s + 8, :] + mm[z, s : s + 8, :] * (rr[s : s + 8, :] * ws[j])
                ww[z, s : s + 8, :] = w if scale == 1.0 else scale * w
                pp[z + 1, s : s + 8, :] = qq[z + 1, s : s + 8, :] - 0.25 * (ws[j] - w)
                new.append(w)
            return tuple(new)

        chunk = levels // 4 if done else levels
        if scale != 1.0:
            for j, s in enumerate(at):
                ww[levels - 1, s : s + 8, :] = scale * ws[j]
        for hi in range(levels, 0, -chunk):
            top = hi - 1
            left = chunk
            if hi == levels:
                for i in range(size - 1):
                    ws = up(levels - 2 - i, ws)
                top = levels - 1 - size
                left = chunk - size

            def bwd(g, ws):
                for i in range(size):
                    ws = up(top - g * size - i, ws)
                return ws

            ws = lax.fori_loop(0, left // size, bwd, ws)
            if hi == chunk:
                for j, s in enumerate(at):
                    pp[0, s : s + 8, :] = qq[0, s : s + 8, :] - 0.25 * ws[j]
            if done:
                done(hi - chunk, hi)

    def strip_step(k, _):
        def sectioned(z):
            for s in sstarts:
                p = sP[z, s : s + 8, :]
                p_s = sP[z, s - 1 : s + 7, :]
                p_n = sP[z, s + 1 : s + 9, :]
                p_w = jnp.where(smask_w, p, pltpu.roll(p, 1, 1))
                p_e = jnp.where(smask_e, 0.0, pltpu.roll(p, LANES - 1, 1))
                if s == SROW + 8:
                    p_s = jnp.where(smask_s, p, p_s)
                if s == NROW:
                    p_n = jnp.where(smask_n, 0.0, p_n)
                e = sE[z, s : s + 8, :] - AB * (((p_w + p_e) + (p_s + p_n)) - 4.0 * p)
                sE[z, s : s + 8, :] = e
                sQ[z, s : s + 8, :] = p - e
            edge_s = jnp.where(is_south, sP[z, SROW + 8 : SROW + 9, :], sP[z, SROW + 7 : SROW + 8, :])
            edge_n = jnp.where(is_north, 0.0, sP[z, NROW + 8 : NROW + 9, :])
            rows[k, pl.ds(2 * z, 1), :] = edge_s
            rows[k, pl.ds(lax.rem(2 * z + LANES - 1, LANES), 1), :] = edge_n

        ws = descend(sQ, sW, sM, sR, sstarts, sectioned, SU)
        ascend(sP, sQ, sW, sM, sR, sstarts, ws, 6)
        return 0

    lax.fori_loop(0, SUBSTEPS, strip_step, 0)

    for k in range(SUBSTEPS + 1):
        T_[k] = rows[k].T

    def edges(k, z, s):
        return pltpu.roll(T_[k, s : s + 8, :], lax.rem(2 * LANES - 2 * z, LANES), 1)

    def main_init(z):
        for s in starts:
            u = ux[z, s : s + 8, :]
            u_w = ux[z, s - 1 : s + 7, :]
            v = vx[z, s : s + 8, :]
            v_s = jnp.where(lane0, edges(SUBSTEPS, z, s), pltpu.roll(v, 1, 1))
            E_[z, s : s + 8, :] = SPREAD * ((u - u_w) + (v - v_s))
            P_[z, s : s + 8, :] = px[z, s : s + 8, :]
            W_[z, s : s + 8, :] = wx[z, s : s + 8, :]
            if s != starts[0]:
                S_[z, s : s + 8, :] = zero

    each(levels, 6, main_init)
    factors(R_, M_, starts)

    def main_down(k):
        def sectioned(z):
            for s in starts:
                p = P_[z, s : s + 8, :]
                p_w = P_[z, s - 1 : s + 7, :]
                p_e = P_[z, s + 1 : s + 9, :]
                if s == main[0]:
                    p_w = jnp.where(mask_w, p, p_w)
                if s == main[-1]:
                    p_e = jnp.where(mask_e, 0.0, p_e)
                edge = edges(k, z, s)
                p_s = jnp.where(lane0, edge, pltpu.roll(p, 1, 1))
                p_n = jnp.where(lane127, edge, pltpu.roll(p, LANES - 1, 1))
                e = E_[z, s : s + 8, :] - AB * (((p_w + p_e) + (p_s + p_n)) - 4.0 * p)
                E_[z, s : s + 8, :] = e
                if s != starts[0]:
                    S_[z, s : s + 8, :] = S_[z, s : s + 8, :] + p
                Q_[z, s : s + 8, :] = p - e

        return descend(Q_, W_, M_, R_, starts, sectioned, MU)

    def main_step(k, _):
        ws = main_down(k)
        ascend(P_, Q_, W_, M_, R_, starts, ws, 3)
        return 0

    lax.fori_loop(0, SUBSTEPS - 1, main_step, 0)
    ws = main_down(SUBSTEPS - 1)

    total = T_[0]
    for k in range(1, SUBSTEPS):
        total = total + T_[k]
    T_[0] = total

    chunk = levels // 4
    copies = []

    def send(src, dst, lo, hi):
        at = slice(OFF, OFF + size_x)
        copy = pltpu.make_async_copy(src.at[lo:hi, at, :], dst.at[lo:hi], sems.at[len(copies)])
        copy.start()
        copies.append(copy)

    def finish(z):
        for s in main:
            total = S_[z, s : s + 8, :]
            east = S_[z, s + 1 : s + 9, :]
            if s == main[-1]:
                east = jnp.where(mask_e, 0.0, east)
            north = jnp.where(lane127, edges(0, z, s), pltpu.roll(total, LANES - 1, 1))
            E_[z, s : s + 8, :] = ux[z, s : s + 8, :] - ACCEL * (east - total)
            S_[z, s : s + 8, :] = vx[z, s : s + 8, :] - ACCEL * (north - total)

    for c in range(4):
        each(chunk, chunk if chunk < 5 else 5, lambda i: finish(c * chunk + i))
        send(E_, u_out, c * chunk, (c + 1) * chunk)
        send(S_, v_out, c * chunk, (c + 1) * chunk)

    def done(lo, hi):
        send(W_, w_out, lo, hi)
        send(P_, p_out, lo + 1 if lo else 0, min(hi + 1, levels))

    ascend(P_, Q_, W_, M_, R_, main, ws[1 : 1 + blocks], chunk if chunk < 5 else 5, 0.5, done)
    for copy in copies:
        copy.wait()


def whole(u_wind, v_wind, w_wind, pressure, vert_coef, we_slab, sn_slab, relax_width):
    levels, size_x, size_y = pressure.shape
    stay = [pltpu.with_memory_space_constraint(x, pltpu.HBM) for x in (pressure, u_wind, v_wind, w_wind)]
    nx = float(size_x * lax.axis_size("gx"))
    ny = float(size_y * lax.axis_size("gy"))
    f32 = jnp.float32
    block = jax.ShapeDtypeStruct(pressure.shape, f32)
    message = jax.ShapeDtypeStruct((levels + 1, 4 * HALO, LANES), f32)
    ext = size_x + 2 * OFF
    extended = jax.ShapeDtypeStruct((levels, ext, LANES), f32)

    east, west = pl.pallas_call(
        rim_kernel,
        out_shape=(message, message),
        in_specs=[HBM] * 4 + [VMEM] * 2,
        out_specs=[VMEM] * 2,
        scratch_shapes=[
            pltpu.VMEM((2, 4, levels, 8, LANES), f32),
            pltpu.SemaphoreType.DMA((2, 4)),
        ],
        compiler_params=pltpu.CompilerParams(vmem_limit_bytes=24 << 20),
        name="rims",
    )(*stay, vert_coef, relax_width)
    from_w = passed_along(east, "gx", 1)
    from_e = passed_along(west, "gx", -1)

    sng = to_edges(sn_slab, "gy")
    sng = jnp.transpose(sng, (1, 0, 2, 3)).reshape(8, size_x, LANES)
    sn_w = passed_along(sng[:, size_x - 8 :], "gx", 1)
    sn_e = passed_along(sng[:, :8], "gx", -1)
    weg = to_edges(we_slab, "gx")

    bands = pltpu.VMEM((3, 512, LANES), f32)
    px, ux, vx, wx, halo_r, own, own_r, north, south = pl.pallas_call(
        lambda *refs: strip_kernel(nx, ny, *refs),
        out_shape=(
            extended,
            extended,
            extended,
            extended,
            jax.ShapeDtypeStruct((16, LANES), f32),
            jax.ShapeDtypeStruct((4, levels, 16, LANES), f32),
            jax.ShapeDtypeStruct((16, LANES), f32),
            message,
            message,
        ),
        in_specs=[HBM] * 4 + [VMEM] * 8,
        out_specs=[VMEM] * 9,
        scratch_shapes=[
            bands,
            bands,
            bands,
            pltpu.VMEM((3, 4, LANES, LANES), f32),
            pltpu.VMEM((size_x + 16, LANES), f32),
            pltpu.SemaphoreType.DMA((4,)),
        ],
        compiler_params=pltpu.CompilerParams(vmem_limit_bytes=24 << 20),
        name="strips",
    )(*stay, vert_coef, relax_width, weg, sn_w, sng, sn_e, from_w, from_e)
    from_s = passed_along(north, "gy", 1)
    from_n = passed_along(south, "gy", -1)

    big = pltpu.VMEM((levels, ext, LANES), f32)
    strip = pltpu.VMEM((levels, SROWS, LANES), f32)
    return pl.pallas_call(
        step_kernel,
        out_shape=(block, block, block, block),
        in_specs=[VMEM] * 10,
        out_specs=[HBM] * 4,
        scratch_shapes=[big] * 6
        + [pltpu.VMEM((ext, LANES), f32)]
        + [strip] * 5
        + [
            pltpu.VMEM((SROWS, LANES), f32),
            pltpu.VMEM((SUBSTEPS + 1, LANES, LANES), f32),
            pltpu.VMEM((SUBSTEPS + 1, LANES, LANES), f32),
            pltpu.SemaphoreType.DMA((16,)),
        ],
        compiler_params=pltpu.CompilerParams(vmem_limit_bytes=32 << 20),
        name="substeps",
    )(px, ux, vx, wx, vert_coef, halo_r, own, own_r, from_s, from_n)


def solution(mesh):
    placed = (
        P(None, "gx", "gy"),
        P(None, "gx", "gy"),
        P(None, "gx", "gy"),
        P(None, "gx", "gy"),
        P("gx", "gy"),
        P(None, None, None, None, ("gy", "gx")),
        P(None, None, None, None, ("gx", "gy")),
        P("gx", "gy"),
    )
    return jax.shard_map(
        whole,
        mesh=mesh,
        in_specs=placed,
        out_specs=(P(None, "gx", "gy"),) * 4,
        check_vma=False,
    )
```

time: 130 us -> 112 us (0.86)
  blocking collectives: 24.7 us -> 0 us
  starting transfers between devices: 20.7 us -> 33.7 us
  Pallas kernels: 54.5 us -> 45.6 us
  waiting for transfers between devices: 20.9 us -> 27 us
  local copies, waits for them, and re-layouts: 6.79 us -> 2.58 us
    all_to_all x1 -> x0, blocking collectives: 24.7 us -> none  [to_edges(): return lax.all_to_all(sent, axis, 0, 0, tiled=True)]
    ppermute x4 -> x6, waiting for transfers between devices: 14.6 us -> 26.4 us  [passed_along(): return lax.ppermute(block, axis, route)]
    pallas_call x4 -> x3, Pallas kernels: 54.5 us -> 45.6 us  [the longest x1 35.2 us: whole(): pl.pallas_call(step_kernel, out_shape=(block, block, block, block), in_sp...]
    ppermute x4 -> x6, starting transfers between devices: 12.3 us -> 20.7 us  [passed_along(): return lax.ppermute(block, axis, route)]
    all_to_all x1 -> x2, waiting for transfers between devices: 6.32 us -> 0.54 us  [to_edges(): return lax.all_to_all(sent, axis, 0, 0, tiled=True)]
    all_to_all x1 -> x2, starting transfers between devices: 8.39 us -> 13 us  [to_edges(): return lax.all_to_all(sent, axis, 0, 0, tiled=True)]
    unnamed x12 -> x10, local copies, waits for them, and re-layouts: 4.64 us -> 1.53 us
  transfers between devices with their start and end apart: 5 -> 8, of which waited for: 3 -> 4; matrix products, arithmetic and copies ran while one was open for 1% -> 1% of each run, Pallas kernels for 0% -> 3%
where the time goes in v3:
time: 112 us
  Pallas kernels  45.6 us (41%)
  starting transfers between devices  33.7 us (30%)
  waiting for transfers between devices  27 us (24%)
  local copies, waits for them, and re-layouts  2.58 us (2%)
  other arithmetic  1.89 us (2%)
    pallas_call x1, Pallas kernels, whole(): pl.pallas_call(step_kernel, out_shape=(block, block, block, block), in_sp...  35.2 us
    ppermute x6, waiting for transfers between devices, passed_along(): return lax.ppermute(block, axis, route)  26.4 us
    ppermute x6, starting transfers between devices, passed_along(): return lax.ppermute(block, axis, route)  20.7 us
    all_to_all x2, starting transfers between devices, to_edges(): return lax.all_to_all(sent, axis, 0, 0, tiled=True)  13 us
    pallas_call x1, Pallas kernels, whole(): pl.pallas_call(lambda *refs: strip_kernel(nx, ny, *refs), out_shape=(exte...  7.61 us
    pallas_call x1, Pallas kernels, whole(): pl.pallas_call(rim_kernel, out_shape=(message, message), in_specs=[HBM] *...  2.83 us
  transfers between devices with their start and end apart: 8, of which 4 were waited for; matrix products, arithmetic and copies ran while one was open for 1% of the time, Pallas kernels for 3%

profile of v3, /device:TPU:31, one launch (start us, length us, event | category | flops | bytes accessed | tf_op | source)
XLA Modules:
  0.0 111.6 jit_solution(14873051018235843062)
XLA Ops:
  0.6 0.8 fusion.2
  1.5 0.1 pad.37.clone
  1.5 0.1 add_bitcast_fusion.2
  1.6 0.8 pad_maximum_fusion.1
  2.4 8.4 %all-to-all-start.1 = ((f32[16,8,4,128]{3,2,1,0:T(4,128)}), f32[16,8,4,128]{3,2,1,0:T(4,128)S(1)}, u32[]{:S(2)}, u32[]{:S(2)}) async-start(f32[16,8,4,128]{3,2,1,0:T(4,128)} %pad_maximum_fusion.1), calls=%async_computation.1 | async-start | bytes 524288 | tf_op jit(solution)/shard_map/all_to_all | solution.py:48
  10.8 0.8 copy-done
  11.6 0.8 copy-done.2
  12.3 2.8 %rims.1 = (f32[61,24,128]{2,1,0:T(8,128)}, f32[61,24,128]{2,1,0:T(8,128)S(1)}) custom-call(f32[60,64,128]{2,1,0:T(8,128)} %refs_0_.1, f32[60,64,128]{2,1,0:T(8,128)} %refs_1_.1, f32[60,64,128]{2,1,0:T(8,128)} %refs_2_.1, f32[60,64,128]{2,1,0:T(8,128)} %refs_3_.1, f32[64,128]{1,0:T(8,128)S(1)} %copy-done, s32[64,128]{1,0:T(8,128)S(1)} %copy-done.2), custom_call_target="tpu_custom_call" | custom-call | tf_op jit(solution)/shard_map/rims/pallas_call | solution.py:544
  15.2 2.3 %collective-permute-start.2 = (f32[61,24,128]{2,1,0:T(8,128)}, f32[61,24,128]{2,1,0:T(8,128)S(1)}, u32[]{:S(2)}, u32[]{:S(2)}) collective-permute-start(f32[61,24,128]{2,1,0:T(8,128)} %get-tuple-element.15), channel_id=1, source_target_pairs={{0,16},{16,32},{32,48},{48,64},{64,80},{80,96},{96,112},{1,17},{17... | collective-permute-start | bytes 2248712 | tf_op jit(solution)/shard_map/ppermute | solution.py:31
  17.5 3.0 %collective-permute-start.3 = (f32[61,24,128]{2,1,0:T(8,128)S(1)}, f32[61,24,128]{2,1,0:T(8,128)S(1)}, u32[]{:S(2)}, u32[]{:S(2)}) collective-permute-start(f32[61,24,128]{2,1,0:T(8,128)S(1)} %get-tuple-element.16), channel_id=1, source_target_pairs={{16,0},{32,16},{48,32},{64,48},{80,64},{96,80},{112,96},{17,1},{33... | collective-permute-start | bytes 2248712 | tf_op jit(solution)/shard_map/ppermute | solution.py:31
  20.5 0.0 copy-done.4
  20.5 0.0 copy-start.1
  20.5 0.0 copy-start.3
  20.6 0.1 add_bitcast_fusion
  20.7 0.1 pad.40.clone
  20.8 0.9 pad_maximum_fusion
  21.7 0.0 all-to-all-done.1
  21.7 4.6 %all-to-all-start = ((f32[8,8,16,128]{3,2,1,0:T(8,128)}), f32[8,8,16,128]{3,2,1,0:T(8,128)S(1)}, u32[]{:S(2)}, u32[]{:S(2)}) async-start(f32[8,8,16,128]{3,2,1,0:T(8,128)} %pad_maximum_fusion), calls=%async_computation | async-start | bytes 1048576 | tf_op jit(solution)/shard_map/all_to_all | solution.py:48
  26.4 2.5 %collective-permute-start.1 = (f32[8,8,128]{2,1,0:T(8,128)S(1)}, f32[8,8,128]{2,1,0:T(8,128)S(1)}, u32[]{:S(2)}, u32[]{:S(2)}) collective-permute-start(f32[8,8,128]{2,1,0:T(8,128)S(1)} %get-tuple-element.26), channel_id=1, source_target_pairs={{16,0},{32,16},{48,32},{64,48},{80,64},{96,80},{112,96},{17,1},{33... | collective-permute-start | bytes 98312 | tf_op jit(solution)/shard_map/ppermute | solution.py:31
  28.9 4.9 %collective-permute-start = (f32[8,8,128]{2,1,0:T(8,128)S(1)}, f32[8,8,128]{2,1,0:T(8,128)S(1)}, u32[]{:S(2)}, u32[]{:S(2)}) collective-permute-start(f32[8,8,128]{2,1,0:T(8,128)S(1)} %get-tuple-element.27), channel_id=1, source_target_pairs={{0,16},{16,32},{32,48},{48,64},{64,80},{80,96},{96,112},{1,17},{17... | collective-permute-start | bytes 98312 | tf_op jit(solution)/shard_map/ppermute | solution.py:31
  33.8 11.8 %collective-permute-done.1.refs_9_ = f32[8,8,128]{2,1,0:T(8,128)S(1)} collective-permute-done((f32[8,8,128]{2,1,0:T(8,128)S(1)}, f32[8,8,128]{2,1,0:T(8,128)S(1)}, u32[]{:S(2)}, u32[]{:S(2)}) %collective-permute-start.1) | collective-permute-done | bytes 32800 | tf_op jit(solution)/shard_map/ppermute | solution.py:31
  45.6 0.0 collective-permute-done.refs_7_
  45.6 0.5 all-to-all-done.refs_6_
  46.1 0.0 collective-permute-done.2.refs_10_
  46.1 0.0 collective-permute-done.3.refs_11_
  46.1 0.0 copy-done.1
  46.2 7.6 %strips.1 = (f32[60,96,128]{2,1,0:T(8,128)S(1)}, f32[60,96,128]{2,1,0:T(8,128)S(1)}, f32[60,96,128]{2,1,0:T(8,128)S(1)}, f32[60,96,128]{2,1,0:T(8,128)S(1)}, f32...) custom-call(f32[60,64,128]{2,1,0:T(8,128)} %refs_0_.1, ...), custom_call_target="tpu_custom_call" | custom-call | tf_op jit(solution)/shard_map/strips/pallas_call | solution.py:566
  53.8 6.1 %collective-permute-start.4 = (f32[61,24,128]{2,1,0:T(8,128)S(1)}, f32[61,24,128]{2,1,0:T(8,128)S(1)}, u32[]{:S(2)}, u32[]{:S(2)}) collective-permute-start(f32[61,24,128]{2,1,0:T(8,128)S(1)} %get-tuple-element.24), channel_id=1, source_target_pairs={{0,1},{1,2},{2,3},{3,4},{4,5},{5,6},{6,7},{7,8},{8,9},{9,10},{10,1... | collective-permute-start | bytes 2248712 | tf_op jit(solution)/shard_map/ppermute | solution.py:31
  59.9 1.9 %collective-permute-start.5 = (f32[61,24,128]{2,1,0:T(8,128)S(1)}, f32[61,24,128]{2,1,0:T(8,128)S(1)}, u32[]{:S(2)}, u32[]{:S(2)}) collective-permute-start(f32[61,24,128]{2,1,0:T(8,128)S(1)} %get-tuple-element.25), channel_id=1, source_target_pairs={{1,0},{2,1},{3,2},{4,3},{5,4},{6,5},{7,6},{8,7},{9,8},{10,9},{11,1... | collective-permute-start | bytes 2248712 | tf_op jit(solution)/shard_map/ppermute | solution.py:31
  61.8 6.6 %collective-permute-done.4.from_s = f32[61,24,128]{2,1,0:T(8,128)S(1)} collective-permute-done((f32[61,24,128]{2,1,0:T(8,128)S(1)}, f32[61,24,128]{2,1,0:T(8,128)S(1)}, u32[]{:S(2)}, u32[]{:S(2)}) %collective-permute-start.4) | collective-permute-done | bytes 749600 | tf_op jit(solution)/shard_map/ppermute | solution.py:31
  68.4 8.0 %collective-permute-done.5.from_n = f32[61,24,128]{2,1,0:T(8,128)S(1)} collective-permute-done((f32[61,24,128]{2,1,0:T(8,128)S(1)}, f32[61,24,128]{2,1,0:T(8,128)S(1)}, u32[]{:S(2)}, u32[]{:S(2)}) %collective-permute-start.5) | collective-permute-done | bytes 749600 | tf_op jit(solution)/shard_map/ppermute | solution.py:31
  76.4 35.2 %substeps.1 = (f32[60,64,128]{2,1,0:T(8,128)}, f32[60,64,128]{2,1,0:T(8,128)}, f32[60,64,128]{2,1,0:T(8,128)}, f32[60,64,128]{2,1,0:T(8,128)}) custom-call(f32[60,96,128]{2,1,0:T(8,128)S(1)} %get-tuple-element.17.px, f32[60,96,128]{2,1,0:T(8,128)S(1)} %get-tuple-element.18.ux, f32[60,96,128]{2,1,0:T(8,128)S(1)} %get-tuple-element.19.vx, ...), custom_call_target="tpu_custom_call" | custom-call | tf_op jit(solution)/shard_map/substeps/pallas_call | solution.py:597
  (19 shorter events, 0.1 us)
Async XLA Ops:
  2.4 19.3 %all-to-all-start.1 = ((f32[16,8,4,128]{3,2,1,0:T(4,128)}), f32[16,8,4,128]{3,2,1,0:T(4,128)S(1)}, u32[]{:S(2)}, u32[]{:S(2)}) async-start(f32[16,8,4,128]{3,2,1,0:T(4,128)} %pad_maximum_fusion.1), calls=%async_computation.1 | async-start | bytes 524288 | tf_op jit(solution)/shard_map/all_to_all | solution.py:48
  10.8 0.8 copy-start
  11.6 0.8 copy-start.2
  12.3 8.1 %copy-start.4 = (f32[2,3,60,5,16]{2,4,3,1,0:T(8,128)S(1)}, f32[2,3,60,5,16]{2,4,3,1,0:T(8,128)}, u32[]{:S(2)}) copy-start(f32[2,3,60,5,16]{2,4,3,1,0:T(8,128)} %param.13) | copy-start | bytes 345604
  15.2 31.0 %collective-permute-start.2 = (f32[61,24,128]{2,1,0:T(8,128)}, f32[61,24,128]{2,1,0:T(8,128)S(1)}, u32[]{:S(2)}, u32[]{:S(2)}) collective-permute-start(f32[61,24,128]{2,1,0:T(8,128)} %get-tuple-element.15), channel_id=1, source_target_pairs={{0,16},{16,32},{32,48},{48,64},{64,80},{80,96},{96,112},{1,17},{17... | collective-permute-start | bytes 2248712 | tf_op jit(solution)/shard_map/ppermute | solution.py:31
  17.5 28.7 %collective-permute-start.3 = (f32[61,24,128]{2,1,0:T(8,128)S(1)}, f32[61,24,128]{2,1,0:T(8,128)S(1)}, u32[]{:S(2)}, u32[]{:S(2)}) collective-permute-start(f32[61,24,128]{2,1,0:T(8,128)S(1)} %get-tuple-element.16), channel_id=1, source_target_pairs={{16,0},{32,16},{48,32},{64,48},{80,64},{96,80},{112,96},{17,1},{33... | collective-permute-start | bytes 2248712 | tf_op jit(solution)/shard_map/ppermute | solution.py:31
  20.5 25.7 %copy-start.1 = (f32[64,128]{1,0:T(8,128)S(1)}, f32[64,128]{1,0:T(8,128)}, u32[]{:S(2)}) copy-start(f32[64,128]{1,0:T(8,128)} %coef.3) | copy-start | bytes 98308
  20.5 25.7 %copy-start.3 = (s32[64,128]{1,0:T(8,128)S(1)}, s32[64,128]{1,0:T(8,128)}, u32[]{:S(2)}) copy-start(s32[64,128]{1,0:T(8,128)} %refs_5_.1) | copy-start | bytes 98308
  21.7 24.4 %all-to-all-start = ((f32[8,8,16,128]{3,2,1,0:T(8,128)}), f32[8,8,16,128]{3,2,1,0:T(8,128)S(1)}, u32[]{:S(2)}, u32[]{:S(2)}) async-start(f32[8,8,16,128]{3,2,1,0:T(8,128)} %pad_maximum_fusion), calls=%async_computation | async-start | bytes 1048576 | tf_op jit(solution)/shard_map/all_to_all | solution.py:48
  26.4 19.2 %collective-permute-start.1 = (f32[8,8,128]{2,1,0:T(8,128)S(1)}, f32[8,8,128]{2,1,0:T(8,128)S(1)}, u32[]{:S(2)}, u32[]{:S(2)}) collective-permute-start(f32[8,8,128]{2,1,0:T(8,128)S(1)} %get-tuple-element.26), channel_id=1, source_target_pairs={{16,0},{32,16},{48,32},{64,48},{80,64},{96,80},{112,96},{17,1},{33... | collective-permute-start | bytes 98312 | tf_op jit(solution)/shard_map/ppermute | solution.py:31
  28.9 16.8 %collective-permute-start = (f32[8,8,128]{2,1,0:T(8,128)S(1)}, f32[8,8,128]{2,1,0:T(8,128)S(1)}, u32[]{:S(2)}, u32[]{:S(2)}) collective-permute-start(f32[8,8,128]{2,1,0:T(8,128)S(1)} %get-tuple-element.27), channel_id=1, source_target_pairs={{0,16},{16,32},{32,48},{48,64},{64,80},{80,96},{96,112},{1,17},{17... | collective-permute-start | bytes 98312 | tf_op jit(solution)/shard_map/ppermute | solution.py:31
  53.8 14.6 %collective-permute-start.4 = (f32[61,24,128]{2,1,0:T(8,128)S(1)}, f32[61,24,128]{2,1,0:T(8,128)S(1)}, u32[]{:S(2)}, u32[]{:S(2)}) collective-permute-start(f32[61,24,128]{2,1,0:T(8,128)S(1)} %get-tuple-element.24), channel_id=1, source_target_pairs={{0,1},{1,2},{2,3},{3,4},{4,5},{5,6},{6,7},{7,8},{8,9},{9,10},{10,1... | collective-permute-start | bytes 2248712 | tf_op jit(solution)/shard_map/ppermute | solution.py:31
  59.9 16.5 %collective-permute-start.5 = (f32[61,24,128]{2,1,0:T(8,128)S(1)}, f32[61,24,128]{2,1,0:T(8,128)S(1)}, u32[]{:S(2)}, u32[]{:S(2)}) collective-permute-start(f32[61,24,128]{2,1,0:T(8,128)S(1)} %get-tuple-element.25), channel_id=1, source_target_pairs={{1,0},{2,1},{3,2},{4,3},{5,4},{6,5},{7,6},{8,7},{9,8},{10,9},{11,1... | collective-permute-start | bytes 2248712 | tf_op jit(solution)/shard_map/ppermute | solution.py:31

commit v4 on v3

--- a/solution.py
+++ b/solution.py
@@ -19,6 +19,8 @@
 NROW = 24
 SROWS = 48
 MU = 10
+FU = 6
+MB = 10
 SU = 12
 
 VMEM = pl.BlockSpec(memory_space=pltpu.VMEM)
@@ -76,9 +78,9 @@
     loop(count, unroll, step, 0)
 
 
-def side_bands(sn_w, sng, sn_e, bs, bt):
+def side_bands(sn_w, sng, sn_e, bs, shift):
     zero = jnp.zeros((8, LANES), jnp.float32)
-    spare = jnp.zeros((LANES - 16 - sng.shape[1], LANES), jnp.float32)
+    spare = jnp.zeros((LANES - 24 - sng.shape[1], LANES), jnp.float32)
 
     def clear(i):
         for k in range(3):
@@ -86,14 +88,53 @@
 
     each(64, 4, clear)
     for s in range(8):
-        b = jnp.concatenate([sn_w[s], sng[s], sn_e[s], spare], axis=0).T
+        b = jnp.concatenate([zero, sn_w[s], sng[s], sn_e[s], spare], axis=0).T
         for half in range(2):
             kj = s + 8 * half
             if kj < 15:
-                bs[kj // 5, pl.ds(kj % 5, 64, stride=8), :] = b[64 * half : 64 * half + 64]
-    for k in range(3):
-        for g in range(4):
-            bt[k, g] = bs[k, g * LANES : (g + 1) * LANES, :].T
+                bs[kj // 5, pl.ds(kj % 5 + shift, 64, stride=8), :] = b[64 * half : 64 * half + 64]
+
+
+def on_sides(body):
+    for north, is_edge in enumerate(axis_ends("gy")):
+
+        @pl.when(is_edge)
+        def _():
+            body(north)
+
+
+def turned(parts):
+    zero = jnp.zeros((8, LANES), jnp.float32)
+    rows = [zero] + parts + [zero] * (LANES // 8 - 1 - len(parts))
+    return jnp.concatenate(rows, axis=0).T
+
+
+def fill_rates(rate_, width, from_w, from_e):
+    levels, size_x = from_w.shape[0] - 1, width.shape[0]
+    rate_[2:8, :] = from_w[levels, HALO : 2 * HALO, :]
+    rate_[8 : 8 + size_x, :] = width[...].astype(jnp.float32)
+    rate_[8 + size_x : 14 + size_x, :] = from_e[levels, HALO : 2 * HALO, :]
+
+
+def factors(coefs, dst, at):
+    def body(z, prev):
+        new = []
+        for s, m in zip(at, prev):
+            r = coefs[s : s + 8, :]
+            m = 1.0 / (1.0 + 2.0 * r - r * r * m)
+            dst[z, s : s + 8, :] = m
+            new.append(m)
+        return tuple(new)
+
+    zero = jnp.zeros((8, LANES), jnp.float32)
+    lax.fori_loop(0, dst.shape[0], body, tuple(zero for _ in at))
+
+
+def fill_coefs(R_, coef, halo_r):
+    size_x = coef.shape[0]
+    R_[OFF : OFF + size_x, :] = coef[...]
+    R_[OFF - 8 : OFF, :] = halo_r[0:8, :]
+    R_[OFF + size_x : OFF + size_x + 8, :] = halo_r[8:16, :]
 
 
 def end_bands(weg, cw, ce):
@@ -116,22 +157,25 @@
                 ce[k, pl.ds(3 + j, 64, stride=8), :] = a[64 * half : 64 * half + 64]
 
 
-def rim_kernel(p, u, v, w, coef, width, east, west, held, sems):
+def rim_kernel(p, u, v, w, coef, width, east, west, held, held_c, held_w, sems):
     levels, size_x, _ = u.shape
     zero = jnp.zeros((8, LANES), jnp.float32)
     copies = []
     for f, src in enumerate((p, u, v, w)):
         for side, lo in enumerate((size_x - 8, 0)):
             copies.append(pltpu.make_async_copy(src.at[:, lo : lo + 8, :], held.at[side, f], sems.at[side, f]))
+    for side, lo in enumerate((size_x - 8, 0)):
+        copies.append(pltpu.make_async_copy(coef.at[lo : lo + 8, :], held_c.at[side], sems.at[side, 4]))
+        copies.append(pltpu.make_async_copy(width.at[lo : lo + 8, :], held_w.at[side], sems.at[side, 5]))
     for copy in copies:
         copy.start()
-    for msg, lo in ((east, size_x - HALO), (west, 0)):
+    for copy in copies:
+        copy.wait()
+    for side, (msg, at) in enumerate(((east, slice(8 - HALO, 8)), (west, slice(0, HALO)))):
         for b in range(3):
             msg[levels, 8 * b : 8 * b + 8, :] = zero
-        msg[levels, 0:HALO, :] = coef[lo : lo + HALO, :]
-        msg[levels, HALO : 2 * HALO, :] = width[lo : lo + HALO, :].astype(jnp.float32)
-    for copy in copies:
-        copy.wait()
+        msg[levels, 0:HALO, :] = held_c[side, at, :]
+        msg[levels, HALO : 2 * HALO, :] = held_w[side, at, :].astype(jnp.float32)
 
     def pack(z):
         for f in range(4):
@@ -142,9 +186,9 @@
 
 
 def strip_kernel(
-    nx, ny, p, u, v, w, coef, width, weg, sn_w, sng, sn_e, from_w, from_e,
+    nx, p, u, v, w, coef, width, weg, sn_w, sng, sn_e, from_w, from_e,
     px, ux, vx, wx, halo_r, own, own_r, north, south,
-    cw, ce, bs, bt, rate_, sems,
+    cw, ce, bs, rate_, sems,
 ):
     levels, size_x, _ = u.shape
     blocks = size_x // 8
@@ -152,7 +196,6 @@
     ends_at = (OFF, OFF + size_x - 8)
     zero = jnp.zeros((8, LANES), jnp.float32)
     is_west, is_east = axis_ends("gx")
-    is_south, is_north = axis_ends("gy")
     fields = ((p, px, 2), (u, ux, 0), (v, vx, 1), (w, wx, None))
     copies = [
         pltpu.make_async_copy(src, dst.at[:, OFF : OFF + size_x, :], sems.at[f])
@@ -175,12 +218,8 @@
     def _():
         end_bands(weg, cw, ce)
 
-    @pl.when(is_south | is_north)
-    def _():
-        side_bands(sn_w, sng, sn_e, bs, bt)
-        rate_[2:8, :] = from_w[levels, HALO : 2 * HALO, :]
-        rate_[8 : 8 + size_x, :] = width[...].astype(jnp.float32)
-        rate_[8 + size_x : 14 + size_x, :] = from_e[levels, HALO : 2 * HALO, :]
+    on_sides(lambda north: side_bands(sn_w, sng, sn_e, bs, 3 * north))
+    fill_rates(rate_, width, from_w, from_e)
 
     def ends(dst, k):
         x = iota8(0).astype(jnp.float32) + (lax.axis_index("gx") * size_x).astype(jnp.float32)
@@ -197,38 +236,7 @@
 
         each(levels, 6, body)
 
-    def sides(dst, k):
-        y = iota8(1).astype(jnp.float32) + (lax.axis_index("gy") * LANES).astype(jnp.float32)
-        dist = jnp.where(is_north, (ny - 1.0) - y, y)
-        base = jnp.where(is_north, 123 + LANES, LANES)
-        for first in range(0, blocks + 2, SB):
-            some = range(first, min(first + SB, blocks + 2))
-            weights = []
-            for b in some:
-                rate = jnp.maximum(rate_[8 * b : 8 * b + 8, :], 1.0)
-                weights.append(jnp.maximum(rate - dist, 0.0) / rate)
-
-            def trip(g, _):
-                new = []
-                for i in range(ZS):
-                    z = g * ZS + i
-                    shift = lax.rem(base - 8 * lax.rem(z, 16), LANES)
-                    for b, weight in zip(some, weights):
-                        band = pltpu.roll(bt[k, z // 16, 8 * b : 8 * b + 8, :], shift, 1)
-                        val = dst[z, starts[b] : starts[b] + 8, :]
-                        new.append(val + weight * (band - val))
-                for i in range(ZS):
-                    for j, b in enumerate(some):
-                        dst[g * ZS + i, starts[b] : starts[b] + 8, :] = new[i * len(some) + j]
-                return 0
-
-            lax.fori_loop(0, levels // ZS, trip, 0)
-
     lane_group = iota8(1) // 16
-
-    def turned(parts):
-        rows = [zero] + parts + [zero] * (LANES // 8 - 1 - len(parts))
-        return jnp.concatenate(rows, axis=0).T
 
     for f, (_, dst, k) in enumerate(fields):
         copies[f].wait()
@@ -237,10 +245,6 @@
             @pl.when(is_west | is_east)
             def _():
                 ends(dst, k)
-
-            @pl.when(is_south | is_north)
-            def _():
-                sides(dst, k)
 
         def group(g, _):
             acc = None
@@ -267,6 +271,23 @@
 
         lax.fori_loop(0, levels // ZG, group, 0, unroll=2)
 
+    def blend(north):
+        rate = turned([pltpu.roll(rate_[8 * b : 8 * b + 8, :], 8, 1) for b in range(blocks + 2)])
+        at = slice(0, 8) if north else slice(8, 16)
+        y = iota8(0).astype(jnp.float32)
+        rate = jnp.maximum(rate[at], 1.0)
+        weight = jnp.maximum(rate - (7.0 - y if north else y), 0.0) / rate
+
+        def body(z):
+            rows = pl.ds(pl.multiple_of(z * 8, 8), 8)
+            for f, (_, _, k) in enumerate(fields[:3]):
+                val = own[f, z, at, :]
+                own[f, z, at, :] = val + weight * (bs[k, rows, :] - val)
+
+        each(levels, 6, body)
+
+    on_sides(blend)
+
     parts = [halo_r[0:8, :]]
     parts += [coef[8 * b : 8 * b + 8, :] for b in range(blocks)]
     parts += [halo_r[8:16, :]]
@@ -279,15 +300,78 @@
     south[levels, 0:HALO, :] = t[8:14]
 
 
+def prep_kernel(
+    px, ux, vx, coef, halo_r, width, from_w, from_e, sn_w, sng, sn_e,
+    pb, ub, vb, E_, M_,
+    bs, bt, rate_, R_,
+):
+    levels, _, _ = px.shape
+    blocks = width.shape[0] // 8
+    starts = [OFF - 8 + 8 * b for b in range(blocks + 2)]
+    fields = ((px, pb, 2), (ux, ub, 0), (vx, vb, 1))
+
+    def take(z):
+        for src, dst, _ in fields:
+            for s in starts:
+                dst[z, s : s + 8, :] = src[z, s : s + 8, :]
+
+    each(levels, 2, take)
+
+    def blend(north):
+        side_bands(sn_w, sng, sn_e, bs, 3 * north)
+        for k in range(3):
+            for g in range(4):
+                bt[k, g] = bs[k, g * LANES : (g + 1) * LANES, :].T
+        fill_rates(rate_, width, from_w, from_e)
+        y = iota8(1).astype(jnp.float32)
+        dist = 127.0 - y if north else y
+        for first in range(0, blocks + 2, SB):
+            some = range(first, min(first + SB, blocks + 2))
+            weights = []
+            for b in some:
+                rate = jnp.maximum(rate_[8 * b : 8 * b + 8, :], 1.0)
+                weights.append(jnp.maximum(rate - dist, 0.0) / rate)
+
+            def trip(g, _):
+                for _, dst, k in fields:
+                    for i in range(ZS):
+                        z = g * ZS + i
+                        shift = lax.rem(LANES + 120 * north - 8 * lax.rem(z, 16), LANES)
+                        for b, weight in zip(some, weights):
+                            s = starts[b]
+                            band = pltpu.roll(bt[k, z // 16, s : s + 8, :], shift, 1)
+                            val = dst[z, s : s + 8, :]
+                            dst[z, s : s + 8, :] = val + weight * (band - val)
+                return 0
+
+            lax.fori_loop(0, levels // ZS, trip, 0)
+
+    on_sides(blend)
+    lane0 = iota8(1) == 0
+
+    def diverge(z):
+        for s in starts:
+            u = ub[z, s : s + 8, :]
+            u_w = ub[z, s - 1 : s + 7, :]
+            v = vb[z, s : s + 8, :]
+            v_s = jnp.where(lane0, 0.0, pltpu.roll(v, 1, 1))
+            E_[z, s : s + 8, :] = SPREAD * ((u - u_w) + (v - v_s))
+
+    each(levels, 6, diverge)
+    fill_coefs(R_, coef, halo_r)
+    factors(R_, M_, starts)
+
+
 def step_kernel(
-    px, ux, vx, wx, coef, halo_r, own, own_r, from_s, from_n,
+    p0, u0, v0, w0, e0, M_, coef, halo_r, own, own_r, from_s, from_n,
     u_out, v_out, w_out, p_out,
-    P_, E_, W_, S_, M_, Q_, R_, sP, sE, sW, sQ, sM, sR, rows, T_, sems,
+    P_, E_, W_, S_, Q_, D_, R_, sP, sE, sW, sQ, sM, sR, rows, T_, sems,
 ):
     levels, size_x, _ = u_out.shape
     blocks = size_x // 8
     starts = [8 * b for b in range(1, blocks + 3)]
     main = [OFF + 8 * b for b in range(blocks)]
+    ahead = starts[::2]
     sstarts = [SROW, SROW + 8, NROW, NROW + 8]
     zero = jnp.zeros((8, LANES), jnp.float32)
     sub = iota8(0)
@@ -313,9 +397,7 @@
             dst[z, NROW + 8 : NROW + 8 + HALO, :] = from_n[z, lo : lo + HALO, :]
 
     each(levels, 2, unpack)
-    R_[OFF : OFF + size_x, :] = coef[...]
-    R_[OFF - 8 : OFF, :] = halo_r[0:8, :]
-    R_[OFF + size_x : OFF + size_x + 8, :] = halo_r[8:16, :]
+    fill_coefs(R_, coef, halo_r)
     sR[SROW + 8 : SROW + 16, :] = own_r[8:16, :]
     sR[NROW : NROW + 8, :] = own_r[0:8, :]
     sR[SROW + 8 - HALO : SROW + 8, :] = from_s[levels, 0:HALO, :]
@@ -331,26 +413,16 @@
 
     each(levels, 6, strip_init)
 
-    def factors(coefs, dst, at):
-        def body(z, prev):
-            new = []
-            for s, m in zip(at, prev):
-                r = coefs[s : s + 8, :]
-                m = 1.0 / (1.0 + 2.0 * r - r * r * m)
-                dst[z, s : s + 8, :] = m
-                new.append(m)
-            return tuple(new)
-
-        lax.fori_loop(0, levels, body, tuple(zero for _ in at))
-
     factors(sR, sM, sstarts)
 
-    def descend(qq, ww, mm, rr, at, sectioned, size):
+    def descend(qq, ww, mm, rr, at, sectioned, size, old=None):
+        given = ww if old is None else old
+
         def down(z, qs, ds, last=False):
             new = []
             qn = None if last else [qq[z + 1, s : s + 8, :] for s in at]
             for i, s in enumerate(at):
-                rhs = ww[z, s : s + 8, :] + (qs[i] if last else qs[i] - qn[i])
+                rhs = given[z, s : s + 8, :] + (qs[i] if last else qs[i] - qn[i])
                 if ds is not None:
                     rhs = rhs + rr[s : s + 8, :] * ds[i]
                 d = mm[z, s : s + 8, :] * rhs
@@ -381,9 +453,11 @@
             qs, ds = down(first + i, qs, ds)
         return down(levels - 1, qs, ds, last=True)[1]
 
-    def ascend(pp, qq, ww, mm, rr, at, ws, size, scale=1.0, done=None):
+    def ascend(pp, qq, ww, mm, rr, at, ws, size, scale=1.0, done=None, also=None):
         def up(z, ws):
             new = []
+            if also:
+                also(z)
             for j, s in enumerate(at):
                 w = ww[z, s : s + 8, :] + mm[z, s : s + 8, :] * (rr[s : s + 8, :] * ws[j])
                 ww[z, s : s + 8, :] = w if scale == 1.0 else scale * w
@@ -392,6 +466,8 @@
             return tuple(new)
 
         chunk = levels // 4 if done else levels
+        if also:
+            also(levels - 1)
         if scale != 1.0:
             for j, s in enumerate(at):
                 ww[levels - 1, s : s + 8, :] = scale * ws[j]
@@ -448,48 +524,45 @@
     def edges(k, z, s):
         return pltpu.roll(T_[k, s : s + 8, :], lax.rem(2 * LANES - 2 * z, LANES), 1)
 
-    def main_init(z):
-        for s in starts:
-            u = ux[z, s : s + 8, :]
-            u_w = ux[z, s - 1 : s + 7, :]
-            v = vx[z, s : s + 8, :]
-            v_s = jnp.where(lane0, edges(SUBSTEPS, z, s), pltpu.roll(v, 1, 1))
-            E_[z, s : s + 8, :] = SPREAD * ((u - u_w) + (v - v_s))
-            P_[z, s : s + 8, :] = px[z, s : s + 8, :]
-            W_[z, s : s + 8, :] = wx[z, s : s + 8, :]
-            if s != starts[0]:
-                S_[z, s : s + 8, :] = zero
-
-    each(levels, 6, main_init)
-    factors(R_, M_, starts)
-
-    def main_down(k):
+    def main_down(k, first=False):
         def sectioned(z):
+            pp = p0 if first else P_
             for s in starts:
-                p = P_[z, s : s + 8, :]
-                p_w = P_[z, s - 1 : s + 7, :]
-                p_e = P_[z, s + 1 : s + 9, :]
+                p = pp[z, s : s + 8, :]
+                p_w = pp[z, s - 1 : s + 7, :]
+                p_e = pp[z, s + 1 : s + 9, :]
                 if s == main[0]:
                     p_w = jnp.where(mask_w, p, p_w)
                 if s == main[-1]:
                     p_e = jnp.where(mask_e, 0.0, p_e)
-                edge = edges(k, z, s)
+                edge = edges(0, z, s) if first else D_[z, s : s + 8, :] if s in ahead else edges(k, z, s)
                 p_s = jnp.where(lane0, edge, pltpu.roll(p, 1, 1))
                 p_n = jnp.where(lane127, edge, pltpu.roll(p, LANES - 1, 1))
-                e = E_[z, s : s + 8, :] - AB * (((p_w + p_e) + (p_s + p_n)) - 4.0 * p)
+                if first:
+                    e = e0[z, s : s + 8, :] - jnp.where(lane0, SPREAD * edges(SUBSTEPS, z, s), 0.0)
+                else:
+                    e = E_[z, s : s + 8, :]
+                e = e - AB * (((p_w + p_e) + (p_s + p_n)) - 4.0 * p)
                 E_[z, s : s + 8, :] = e
                 if s != starts[0]:
-                    S_[z, s : s + 8, :] = S_[z, s : s + 8, :] + p
+                    S_[z, s : s + 8, :] = p if first else S_[z, s : s + 8, :] + p
                 Q_[z, s : s + 8, :] = p - e
 
-        return descend(Q_, W_, M_, R_, starts, sectioned, MU)
+        return descend(Q_, W_, M_, R_, starts, sectioned, FU if first else MU, w0 if first else None)
+
+    def main_up(k, ws):
+        def also(z):
+            for s in ahead:
+                D_[z, s : s + 8, :] = edges(k + 1, z, s)
+
+        ascend(P_, Q_, W_, M_, R_, starts, ws, MB, also=also)
 
     def main_step(k, _):
-        ws = main_down(k)
-        ascend(P_, Q_, W_, M_, R_, starts, ws, 3)
+        main_up(k, main_down(k))
         return 0
 
-    lax.fori_loop(0, SUBSTEPS - 1, main_step, 0)
+    main_up(0, main_down(0, True))
+    lax.fori_loop(1, SUBSTEPS - 1, main_step, 0)
     ws = main_down(SUBSTEPS - 1)
 
     total = T_[0]
@@ -513,8 +586,8 @@
             if s == main[-1]:
                 east = jnp.where(mask_e, 0.0, east)
             north = jnp.where(lane127, edges(0, z, s), pltpu.roll(total, LANES - 1, 1))
-            E_[z, s : s + 8, :] = ux[z, s : s + 8, :] - ACCEL * (east - total)
-            S_[z, s : s + 8, :] = vx[z, s : s + 8, :] - ACCEL * (north - total)
+            E_[z, s : s + 8, :] = u0[z, s : s + 8, :] - ACCEL * (east - total)
+            S_[z, s : s + 8, :] = v0[z, s : s + 8, :] - ACCEL * (north - total)
 
     for c in range(4):
         each(chunk, chunk if chunk < 5 else 5, lambda i: finish(c * chunk + i))
@@ -531,10 +604,9 @@
 
 
 def whole(u_wind, v_wind, w_wind, pressure, vert_coef, we_slab, sn_slab, relax_width):
-    levels, size_x, size_y = pressure.shape
-    stay = [pltpu.with_memory_space_constraint(x, pltpu.HBM) for x in (pressure, u_wind, v_wind, w_wind)]
+    levels, size_x, _ = pressure.shape
+    stay = [pltpu.with_memory_space_constraint(x, pltpu.HBM) for x in (pressure, u_wind, v_wind, w_wind, vert_coef, relax_width)]
     nx = float(size_x * lax.axis_size("gx"))
-    ny = float(size_y * lax.axis_size("gy"))
     f32 = jnp.float32
     block = jax.ShapeDtypeStruct(pressure.shape, f32)
     message = jax.ShapeDtypeStruct((levels + 1, 4 * HALO, LANES), f32)
@@ -544,15 +616,18 @@
     east, west = pl.pallas_call(
         rim_kernel,
         out_shape=(message, message),
-        in_specs=[HBM] * 4 + [VMEM] * 2,
+        in_specs=[HBM] * 6,
         out_specs=[VMEM] * 2,
         scratch_shapes=[
             pltpu.VMEM((2, 4, levels, 8, LANES), f32),
-            pltpu.SemaphoreType.DMA((2, 4)),
+            pltpu.VMEM((2, 8, LANES), f32),
+            pltpu.VMEM((2, 8, LANES), jnp.int32),
+            pltpu.SemaphoreType.DMA((2, 6)),
         ],
         compiler_params=pltpu.CompilerParams(vmem_limit_bytes=24 << 20),
         name="rims",
-    )(*stay, vert_coef, relax_width)
+    )(*stay)
+    sn_slab, we_slab, east, west = lax.optimization_barrier((sn_slab, we_slab, east, west))
     from_w = passed_along(east, "gx", 1)
     from_e = passed_along(west, "gx", -1)
 
@@ -564,7 +639,7 @@
 
     bands = pltpu.VMEM((3, 512, LANES), f32)
     px, ux, vx, wx, halo_r, own, own_r, north, south = pl.pallas_call(
-        lambda *refs: strip_kernel(nx, ny, *refs),
+        lambda *refs: strip_kernel(nx, *refs),
         out_shape=(
             extended,
             extended,
@@ -582,22 +657,36 @@
             bands,
             bands,
             bands,
-            pltpu.VMEM((3, 4, LANES, LANES), f32),
             pltpu.VMEM((size_x + 16, LANES), f32),
             pltpu.SemaphoreType.DMA((4,)),
         ],
-        compiler_params=pltpu.CompilerParams(vmem_limit_bytes=24 << 20),
+        compiler_params=pltpu.CompilerParams(vmem_limit_bytes=8 << 20),
         name="strips",
-    )(*stay, vert_coef, relax_width, weg, sn_w, sng, sn_e, from_w, from_e)
+    )(*stay[:4], vert_coef, relax_width, weg, sn_w, sng, sn_e, from_w, from_e)
     from_s = passed_along(north, "gy", 1)
     from_n = passed_along(south, "gy", -1)
+    pb, ub, vb, e0, m0 = pl.pallas_call(
+        prep_kernel,
+        out_shape=(extended,) * 5,
+        in_specs=[VMEM] * 11,
+        out_specs=[VMEM] * 5,
+        scratch_shapes=[
+            bands,
+            pltpu.VMEM((3, 4, LANES, LANES), f32),
+            pltpu.VMEM((size_x + 16, LANES), f32),
+            pltpu.VMEM((ext, LANES), f32),
+        ],
+        compiler_params=pltpu.CompilerParams(vmem_limit_bytes=6 << 20),
+        cost_estimate=pl.CostEstimate(flops=20_000_000, bytes_accessed=20_000_000, transcendentals=0),
+        name="prep",
+    )(px, ux, vx, vert_coef, halo_r, relax_width, from_w, from_e, sn_w, sng, sn_e)
 
     big = pltpu.VMEM((levels, ext, LANES), f32)
     strip = pltpu.VMEM((levels, SROWS, LANES), f32)
     return pl.pallas_call(
         step_kernel,
         out_shape=(block, block, block, block),
-        in_specs=[VMEM] * 10,
+        in_specs=[VMEM] * 12,
         out_specs=[HBM] * 4,
         scratch_shapes=[big] * 6
         + [pltpu.VMEM((ext, LANES), f32)]
@@ -608,9 +697,9 @@
             pltpu.VMEM((SUBSTEPS + 1, LANES, LANES), f32),
             pltpu.SemaphoreType.DMA((16,)),
         ],
-        compiler_params=pltpu.CompilerParams(vmem_limit_bytes=32 << 20),
+        compiler_params=pltpu.CompilerParams(vmem_limit_bytes=30 << 20),
         name="substeps",
-    )(px, ux, vx, wx, vert_coef, halo_r, own, own_r, from_s, from_n)
+    )(pb, ub, vb, wx, e0, m0, vert_coef, halo_r, own, own_r, from_s, from_n)
 
 
 def solution(mesh):

time: 112 us -> 108 us (0.964)
  waiting for transfers between devices: 27 us -> 24.1 us
  local copies, waits for them, and re-layouts: 2.58 us -> 0.31 us
    ppermute x6, waiting for transfers between devices: 26.4 us -> 22.7 us  [passed_along(): return lax.ppermute(block, axis, route)]
    pallas_call x1 -> x2, Pallas kernels: 7.61 us -> 10.5 us  [the longest x1 7.66 us: whole(): pl.pallas_call(lambda *refs: strip_kernel(nx, *refs), out_shape=(extended...]
    pallas_call x1, Pallas kernels: 35.2 us -> 33.2 us  [whole(): pl.pallas_call(step_kernel, out_shape=(block, block, block, block), in_sp...]
    unnamed x10 -> x8, local copies, waits for them, and re-layouts: 1.53 us -> 0.02 us
  transfers between devices with their start and end apart: 8 -> 8, of which waited for: 4 -> 5; matrix products, arithmetic and copies ran while one was open for 1% -> 1% of each run, Pallas kernels for 3% -> 3%
where the time goes in v4:
time: 108 us; the launch traced here: 107 us
  Pallas kernels  46.6 us (43%)
  starting transfers between devices  33.6 us (31%)
  waiting for transfers between devices  24.1 us (22%)
  other arithmetic  1.88 us (2%)
    pallas_call x1, Pallas kernels, whole(): pl.pallas_call(step_kernel, out_shape=(block, block, block, block), in_sp...  33.2 us
    ppermute x6, waiting for transfers between devices, passed_along(): return lax.ppermute(block, axis, route)  22.7 us
    ppermute x6, starting transfers between devices, passed_along(): return lax.ppermute(block, axis, route)  20.7 us
    all_to_all x2, starting transfers between devices, to_edges(): return lax.all_to_all(sent, axis, 0, 0, tiled=True)  13 us
    pallas_call x1, Pallas kernels, whole(): pl.pallas_call(lambda *refs: strip_kernel(nx, *refs), out_shape=(extended...  7.66 us
    pallas_call x1, Pallas kernels, whole(): pl.pallas_call(rim_kernel, out_shape=(message, message), in_specs=[HBM] *...  2.88 us
    pallas_call x1, Pallas kernels, whole(): pl.pallas_call(prep_kernel, out_shape=(extended,) * 5, in_specs=[VMEM] *...  2.88 us
  transfers between devices with their start and end apart: 8, of which 5 were waited for; matrix products, arithmetic and copies ran while one was open for 1% of the time, Pallas kernels for 3%

profile of v4, /device:TPU:31, one launch (start us, length us, event | category | flops | bytes accessed | tf_op | source)
XLA Modules:
  0.0 107.5 jit_solution(668922202721627879)
XLA Ops:
  0.6 0.0 copy-start.3
  0.6 0.0 copy-start.2
  0.7 2.9 %rims.1 = (f32[61,24,128]{2,1,0:T(8,128)}, f32[61,24,128]{2,1,0:T(8,128)S(1)}) custom-call(f32[60,64,128]{2,1,0:T(8,128)} %refs_0_.1, f32[60,64,128]{2,1,0:T(8,128)} %refs_1_.1, f32[60,64,128]{2,1,0:T(8,128)} %refs_2_.1, f32[60,64,128]{2,1,0:T(8,128)} %refs_3_.1, f32[64,128]{1,0:T(8,128)} %coef.5, s32[64,128]{1,0:T(8,128)} %width.3), custom_call_target="tpu_custom_call" | custom-call | tf_op jit(solution)/shard_map/rims/pallas_call | solution.py:616
  3.5 0.0 copy-start
  3.6 0.0 copy-start.1
  3.6 0.0 copy-done.3
  3.7 0.1 pad.37.clone
  3.7 0.1 add_bitcast_fusion.2
  3.8 0.8 pad_maximum_fusion.1
  4.6 8.4 %all-to-all-start.1 = ((f32[16,8,4,128]{3,2,1,0:T(4,128)}), f32[16,8,4,128]{3,2,1,0:T(4,128)S(1)}, u32[]{:S(2)}, u32[]{:S(2)}) async-start(f32[16,8,4,128]{3,2,1,0:T(4,128)} %pad_maximum_fusion.1), calls=%async_computation.1 | async-start | bytes 524288 | tf_op jit(solution)/shard_map/all_to_all | solution.py:50
  13.0 2.3 %collective-permute-start.2 = (f32[61,24,128]{2,1,0:T(8,128)}, f32[61,24,128]{2,1,0:T(8,128)S(1)}, u32[]{:S(2)}, u32[]{:S(2)}) collective-permute-start(f32[61,24,128]{2,1,0:T(8,128)} %get-tuple-element.28), channel_id=1, source_target_pairs={{0,16},{16,32},{32,48},{48,64},{64,80},{80,96},{96,112},{1,17},{17... | collective-permute-start | bytes 2248712 | tf_op jit(solution)/shard_map/ppermute | solution.py:33
  15.3 3.0 %collective-permute-start.3 = (f32[61,24,128]{2,1,0:T(8,128)S(1)}, f32[61,24,128]{2,1,0:T(8,128)S(1)}, u32[]{:S(2)}, u32[]{:S(2)}) collective-permute-start(f32[61,24,128]{2,1,0:T(8,128)S(1)} %get-tuple-element.29), channel_id=1, source_target_pairs={{16,0},{32,16},{48,32},{64,48},{80,64},{96,80},{112,96},{17,1},{33... | collective-permute-start | bytes 2248712 | tf_op jit(solution)/shard_map/ppermute | solution.py:33
  18.4 0.1 add_bitcast_fusion
  18.5 0.1 pad.40.clone
  18.6 0.9 pad_maximum_fusion
  19.5 0.9 all-to-all-done.1
  20.4 4.6 %all-to-all-start = ((f32[8,8,16,128]{3,2,1,0:T(8,128)}), f32[8,8,16,128]{3,2,1,0:T(8,128)S(1)}, u32[]{:S(2)}, u32[]{:S(2)}) async-start(f32[8,8,16,128]{3,2,1,0:T(8,128)} %pad_maximum_fusion), calls=%async_computation | async-start | bytes 1048576 | tf_op jit(solution)/shard_map/all_to_all | solution.py:50
  25.0 2.5 %collective-permute-start.1 = (f32[8,8,128]{2,1,0:T(8,128)S(1)}, f32[8,8,128]{2,1,0:T(8,128)S(1)}, u32[]{:S(2)}, u32[]{:S(2)}) collective-permute-start(f32[8,8,128]{2,1,0:T(8,128)S(1)} %get-tuple-element.44), channel_id=1, source_target_pairs={{16,0},{32,16},{48,32},{64,48},{80,64},{96,80},{112,96},{17,1},{33... | collective-permute-start | bytes 98312 | tf_op jit(solution)/shard_map/ppermute | solution.py:33
  27.5 4.9 %collective-permute-start = (f32[8,8,128]{2,1,0:T(8,128)S(1)}, f32[8,8,128]{2,1,0:T(8,128)S(1)}, u32[]{:S(2)}, u32[]{:S(2)}) collective-permute-start(f32[8,8,128]{2,1,0:T(8,128)S(1)} %get-tuple-element.45), channel_id=1, source_target_pairs={{0,16},{16,32},{32,48},{48,64},{64,80},{80,96},{96,112},{1,17},{17... | collective-permute-start | bytes 98312 | tf_op jit(solution)/shard_map/ppermute | solution.py:33
  32.4 11.0 %collective-permute-done.1.refs_9_.sn_e = f32[8,8,128]{2,1,0:T(8,128)S(1)} collective-permute-done((f32[8,8,128]{2,1,0:T(8,128)S(1)}, f32[8,8,128]{2,1,0:T(8,128)S(1)}, u32[]{:S(2)}, u32[]{:S(2)}) %collective-permute-start.1) | collective-permute-done | bytes 32800 | tf_op jit(solution)/shard_map/ppermute | solution.py:33
  43.4 0.0 collective-permute-done.refs_7_.sn_w
  43.4 0.6 all-to-all-done.refs_6_
  44.0 0.0 collective-permute-done.2.refs_10_.from_w
  44.0 0.0 collective-permute-done.3.refs_11_.from_e
  44.0 0.0 copy-done.1
  44.0 7.7 %strips.1 = (f32[60,96,128]{2,1,0:T(8,128)S(1)}, f32[60,96,128]{2,1,0:T(8,128)S(1)}, f32[60,96,128]{2,1,0:T(8,128)S(1)}, f32[60,96,128]{2,1,0:T(8,128)S(1)}, f32...) custom-call(f32[60,64,128]{2,1,0:T(8,128)} %refs_0_.1, ...), custom_call_target="tpu_custom_call" | custom-call | tf_op jit(solution)/shard_map/strips/pallas_call | solution.py:641
  51.7 6.1 %collective-permute-start.4 = (f32[61,24,128]{2,1,0:T(8,128)S(1)}, f32[61,24,128]{2,1,0:T(8,128)S(1)}, u32[]{:S(2)}, u32[]{:S(2)}) collective-permute-start(f32[61,24,128]{2,1,0:T(8,128)S(1)} %get-tuple-element.42), channel_id=1, source_target_pairs={{0,1},{1,2},{2,3},{3,4},{4,5},{5,6},{6,7},{7,8},{8,9},{9,10},{10,1... | collective-permute-start | bytes 2248712 | tf_op jit(solution)/shard_map/ppermute | solution.py:33
  57.8 1.9 %collective-permute-start.5 = (f32[61,24,128]{2,1,0:T(8,128)S(1)}, f32[61,24,128]{2,1,0:T(8,128)S(1)}, u32[]{:S(2)}, u32[]{:S(2)}) collective-permute-start(f32[61,24,128]{2,1,0:T(8,128)S(1)} %get-tuple-element.43), channel_id=1, source_target_pairs={{1,0},{2,1},{3,2},{4,3},{5,4},{6,5},{7,6},{8,7},{9,8},{10,9},{11,1... | collective-permute-start | bytes 2248712 | tf_op jit(solution)/shard_map/ppermute | solution.py:33
  59.7 2.9 %prep.1 = (f32[60,96,128]{2,1,0:T(8,128)S(1)}, f32[60,96,128]{2,1,0:T(8,128)S(1)}, f32[60,96,128]{2,1,0:T(8,128)S(1)}, f32[60,96,128]{2,1,0:T(8,128)S(1)}, f32[60,96,128]{2,1,0:T(8,128)S(1)}) custom-call(f32[60,96,128]{2,1,0:T(8,128)S(1)} %get-tuple-element.30.px, f32[60,96,128]{2,1,0:T(8,128)S(1)} %get-tuple-element.31.ux, ...), custom_call_target="tpu_custom_call" | custom-call | flops 20000000 | bytes 20000000 | tf_op jit(solution)/shard_map/prep/pallas_call | solution.py:668
  62.6 3.7 %collective-permute-done.4.from_s = f32[61,24,128]{2,1,0:T(8,128)S(1)} collective-permute-done((f32[61,24,128]{2,1,0:T(8,128)S(1)}, f32[61,24,128]{2,1,0:T(8,128)S(1)}, u32[]{:S(2)}, u32[]{:S(2)}) %collective-permute-start.4) | collective-permute-done | bytes 749600 | tf_op jit(solution)/shard_map/ppermute | solution.py:33
  66.3 8.0 %collective-permute-done.5.from_n = f32[61,24,128]{2,1,0:T(8,128)S(1)} collective-permute-done((f32[61,24,128]{2,1,0:T(8,128)S(1)}, f32[61,24,128]{2,1,0:T(8,128)S(1)}, u32[]{:S(2)}, u32[]{:S(2)}) %collective-permute-start.5) | collective-permute-done | bytes 749600 | tf_op jit(solution)/shard_map/ppermute | solution.py:33
  74.3 33.2 %substeps.1 = (f32[60,64,128]{2,1,0:T(8,128)}, f32[60,64,128]{2,1,0:T(8,128)}, f32[60,64,128]{2,1,0:T(8,128)}, f32[60,64,128]{2,1,0:T(8,128)}) custom-call(f32[60,96,128]{2,1,0:T(8,128)S(1)} %get-tuple-element.34.p0, f32[60,96,128]{2,1,0:T(8,128)S(1)} %get-tuple-element.35.u0, f32[60,96,128]{2,1,0:T(8,128)S(1)} %get-tuple-element.36.v0, ...), custom_call_target="tpu_custom_call" | custom-call | tf_op jit(solution)/shard_map/substeps/pallas_call | solution.py:686
  (18 shorter events, 0.1 us)
Async XLA Ops:
  0.6 2.9 %copy-start.3 = (f32[2,3,60,5,4]{2,4,3,1,0:T(4,128)S(1)}, f32[2,3,60,5,4]{2,4,3,1,0:T(4,128)}, u32[]{:S(2)}) copy-start(f32[2,3,60,5,4]{2,4,3,1,0:T(4,128)} %param.14) | copy-start | bytes 86404
  0.6 17.7 %copy-start.2 = (f32[2,3,60,5,16]{2,4,3,1,0:T(8,128)S(1)}, f32[2,3,60,5,16]{2,4,3,1,0:T(8,128)}, u32[]{:S(2)}) copy-start(f32[2,3,60,5,16]{2,4,3,1,0:T(8,128)} %param.13) | copy-start | bytes 345604
  3.5 40.5 %copy-start = (f32[64,128]{1,0:T(8,128)S(1)}, f32[64,128]{1,0:T(8,128)}, u32[]{:S(2)}) copy-start(f32[64,128]{1,0:T(8,128)} %coef.5) | copy-start | bytes 98308
  3.6 40.4 %copy-start.1 = (s32[64,128]{1,0:T(8,128)S(1)}, s32[64,128]{1,0:T(8,128)}, u32[]{:S(2)}) copy-start(s32[64,128]{1,0:T(8,128)} %width.3) | copy-start | bytes 98308
  4.6 15.8 %all-to-all-start.1 = ((f32[16,8,4,128]{3,2,1,0:T(4,128)}), f32[16,8,4,128]{3,2,1,0:T(4,128)S(1)}, u32[]{:S(2)}, u32[]{:S(2)}) async-start(f32[16,8,4,128]{3,2,1,0:T(4,128)} %pad_maximum_fusion.1), calls=%async_computation.1 | async-start | bytes 524288 | tf_op jit(solution)/shard_map/all_to_all | solution.py:50
  13.0 31.0 %collective-permute-start.2 = (f32[61,24,128]{2,1,0:T(8,128)}, f32[61,24,128]{2,1,0:T(8,128)S(1)}, u32[]{:S(2)}, u32[]{:S(2)}) collective-permute-start(f32[61,24,128]{2,1,0:T(8,128)} %get-tuple-element.28), channel_id=1, source_target_pairs={{0,16},{16,32},{32,48},{48,64},{64,80},{80,96},{96,112},{1,17},{17... | collective-permute-start | bytes 2248712 | tf_op jit(solution)/shard_map/ppermute | solution.py:33
  15.3 28.7 %collective-permute-start.3 = (f32[61,24,128]{2,1,0:T(8,128)S(1)}, f32[61,24,128]{2,1,0:T(8,128)S(1)}, u32[]{:S(2)}, u32[]{:S(2)}) collective-permute-start(f32[61,24,128]{2,1,0:T(8,128)S(1)} %get-tuple-element.29), channel_id=1, source_target_pairs={{16,0},{32,16},{48,32},{64,48},{80,64},{96,80},{112,96},{17,1},{33... | collective-permute-start | bytes 2248712 | tf_op jit(solution)/shard_map/ppermute | solution.py:33
  20.4 23.6 %all-to-all-start = ((f32[8,8,16,128]{3,2,1,0:T(8,128)}), f32[8,8,16,128]{3,2,1,0:T(8,128)S(1)}, u32[]{:S(2)}, u32[]{:S(2)}) async-start(f32[8,8,16,128]{3,2,1,0:T(8,128)} %pad_maximum_fusion), calls=%async_computation | async-start | bytes 1048576 | tf_op jit(solution)/shard_map/all_to_all | solution.py:50
  25.0 18.4 %collective-permute-start.1 = (f32[8,8,128]{2,1,0:T(8,128)S(1)}, f32[8,8,128]{2,1,0:T(8,128)S(1)}, u32[]{:S(2)}, u32[]{:S(2)}) collective-permute-start(f32[8,8,128]{2,1,0:T(8,128)S(1)} %get-tuple-element.44), channel_id=1, source_target_pairs={{16,0},{32,16},{48,32},{64,48},{80,64},{96,80},{112,96},{17,1},{33... | collective-permute-start | bytes 98312 | tf_op jit(solution)/shard_map/ppermute | solution.py:33
  27.5 15.9 %collective-permute-start = (f32[8,8,128]{2,1,0:T(8,128)S(1)}, f32[8,8,128]{2,1,0:T(8,128)S(1)}, u32[]{:S(2)}, u32[]{:S(2)}) collective-permute-start(f32[8,8,128]{2,1,0:T(8,128)S(1)} %get-tuple-element.45), channel_id=1, source_target_pairs={{0,16},{16,32},{32,48},{48,64},{64,80},{80,96},{96,112},{1,17},{17... | collective-permute-start | bytes 98312 | tf_op jit(solution)/shard_map/ppermute | solution.py:33
  51.7 14.6 %collective-permute-start.4 = (f32[61,24,128]{2,1,0:T(8,128)S(1)}, f32[61,24,128]{2,1,0:T(8,128)S(1)}, u32[]{:S(2)}, u32[]{:S(2)}) collective-permute-start(f32[61,24,128]{2,1,0:T(8,128)S(1)} %get-tuple-element.42), channel_id=1, source_target_pairs={{0,1},{1,2},{2,3},{3,4},{4,5},{5,6},{6,7},{7,8},{8,9},{9,10},{10,1... | collective-permute-start | bytes 2248712 | tf_op jit(solution)/shard_map/ppermute | solution.py:33
  57.8 16.5 %collective-permute-start.5 = (f32[61,24,128]{2,1,0:T(8,128)S(1)}, f32[61,24,128]{2,1,0:T(8,128)S(1)}, u32[]{:S(2)}, u32[]{:S(2)}) collective-permute-start(f32[61,24,128]{2,1,0:T(8,128)S(1)} %get-tuple-element.43), channel_id=1, source_target_pairs={{1,0},{2,1},{3,2},{4,3},{5,4},{6,5},{7,6},{8,7},{9,8},{10,9},{11,1... | collective-permute-start | bytes 2248712 | tf_op jit(solution)/shard_map/ppermute | solution.py:33

commit v5 on v4

--- a/solution.py
+++ b/solution.py
@@ -18,10 +18,10 @@
 SROW = 8
 NROW = 24
 SROWS = 48
-MU = 10
-FU = 6
-MB = 10
-SU = 12
+MU = 15
+FU = 10
+MB = 20
+SU = 20
 
 VMEM = pl.BlockSpec(memory_space=pltpu.VMEM)
 HBM = pl.BlockSpec(memory_space=pltpu.HBM)

time: 108 us -> 105 us (0.972)
  Pallas kernels: 46.6 us -> 43.5 us
    pallas_call x1, Pallas kernels: 33.2 us -> 29.9 us  [whole(): pl.pallas_call(step_kernel, out_shape=(block, block, block, block), in_sp...]
where the time goes in v5:
time: 105 us; the launch traced here: 104 us
  Pallas kernels  43.5 us (41%)
  starting transfers between devices  33.6 us (32%)
  waiting for transfers between devices  24 us (23%)
  other arithmetic  1.88 us (2%)
  between operations  1.07 us (1%)
    pallas_call x1, Pallas kernels, whole(): pl.pallas_call(step_kernel, out_shape=(block, block, block, block), in_sp...  29.9 us
    ppermute x6, waiting for transfers between devices, passed_along(): return lax.ppermute(block, axis, route)  22.5 us
    ppermute x6, starting transfers between devices, passed_along(): return lax.ppermute(block, axis, route)  20.7 us
    all_to_all x2, starting transfers between devices, to_edges(): return lax.all_to_all(sent, axis, 0, 0, tiled=True)  13 us
    pallas_call x1, Pallas kernels, whole(): pl.pallas_call(lambda *refs: strip_kernel(nx, *refs), out_shape=(extended...  7.66 us
    pallas_call x1, Pallas kernels, whole(): pl.pallas_call(prep_kernel, out_shape=(extended,) * 5, in_specs=[VMEM] *...  3.06 us
    pallas_call x1, Pallas kernels, whole(): pl.pallas_call(rim_kernel, out_shape=(message, message), in_specs=[HBM] *...  2.88 us
  transfers between devices with their start and end apart: 8, of which 5 were waited for; matrix products, arithmetic and copies ran while one was open for 1% of the time, Pallas kernels for 3%

profile of v5, /device:TPU:31, one launch (start us, length us, event | category | flops | bytes accessed | tf_op | source)
XLA Modules:
  0.0 104.4 jit_solution(3313238320209709192)
XLA Ops:
  0.6 0.0 copy-start.3
  0.6 0.0 copy-start.2
  0.7 2.9 %rims.1 = (f32[61,24,128]{2,1,0:T(8,128)}, f32[61,24,128]{2,1,0:T(8,128)S(1)}) custom-call(f32[60,64,128]{2,1,0:T(8,128)} %refs_0_.1, f32[60,64,128]{2,1,0:T(8,128)} %refs_1_.1, f32[60,64,128]{2,1,0:T(8,128)} %refs_2_.1, f32[60,64,128]{2,1,0:T(8,128)} %refs_3_.1, f32[64,128]{1,0:T(8,128)} %coef.5, s32[64,128]{1,0:T(8,128)} %width.3), custom_call_target="tpu_custom_call" | custom-call | tf_op jit(solution)/shard_map/rims/pallas_call | solution.py:616
  3.5 0.0 copy-start
  3.6 0.0 copy-start.1
  3.7 0.1 pad.37.clone
  3.7 0.1 add_bitcast_fusion.2
  3.8 0.8 pad_maximum_fusion.1
  4.6 8.4 %all-to-all-start.1 = ((f32[16,8,4,128]{3,2,1,0:T(4,128)}), f32[16,8,4,128]{3,2,1,0:T(4,128)S(1)}, u32[]{:S(2)}, u32[]{:S(2)}) async-start(f32[16,8,4,128]{3,2,1,0:T(4,128)} %pad_maximum_fusion.1), calls=%async_computation.1 | async-start | bytes 524288 | tf_op jit(solution)/shard_map/all_to_all | solution.py:50
  13.0 2.3 %collective-permute-start.2 = (f32[61,24,128]{2,1,0:T(8,128)}, f32[61,24,128]{2,1,0:T(8,128)S(1)}, u32[]{:S(2)}, u32[]{:S(2)}) collective-permute-start(f32[61,24,128]{2,1,0:T(8,128)} %get-tuple-element.28), channel_id=1, source_target_pairs={{0,16},{16,32},{32,48},{48,64},{64,80},{80,96},{96,112},{1,17},{17... | collective-permute-start | bytes 2248712 | tf_op jit(solution)/shard_map/ppermute | solution.py:33
  15.3 3.0 %collective-permute-start.3 = (f32[61,24,128]{2,1,0:T(8,128)S(1)}, f32[61,24,128]{2,1,0:T(8,128)S(1)}, u32[]{:S(2)}, u32[]{:S(2)}) collective-permute-start(f32[61,24,128]{2,1,0:T(8,128)S(1)} %get-tuple-element.29), channel_id=1, source_target_pairs={{16,0},{32,16},{48,32},{64,48},{80,64},{96,80},{112,96},{17,1},{33... | collective-permute-start | bytes 2248712 | tf_op jit(solution)/shard_map/ppermute | solution.py:33
  18.3 0.0 copy-done.2
  18.4 0.1 add_bitcast_fusion
  18.5 0.1 pad.40.clone
  18.6 0.9 pad_maximum_fusion
  19.5 0.9 all-to-all-done.1
  20.4 4.6 %all-to-all-start = ((f32[8,8,16,128]{3,2,1,0:T(8,128)}), f32[8,8,16,128]{3,2,1,0:T(8,128)S(1)}, u32[]{:S(2)}, u32[]{:S(2)}) async-start(f32[8,8,16,128]{3,2,1,0:T(8,128)} %pad_maximum_fusion), calls=%async_computation | async-start | bytes 1048576 | tf_op jit(solution)/shard_map/all_to_all | solution.py:50
  25.0 2.5 %collective-permute-start.1 = (f32[8,8,128]{2,1,0:T(8,128)S(1)}, f32[8,8,128]{2,1,0:T(8,128)S(1)}, u32[]{:S(2)}, u32[]{:S(2)}) collective-permute-start(f32[8,8,128]{2,1,0:T(8,128)S(1)} %get-tuple-element.44), channel_id=1, source_target_pairs={{16,0},{32,16},{48,32},{64,48},{80,64},{96,80},{112,96},{17,1},{33... | collective-permute-start | bytes 98312 | tf_op jit(solution)/shard_map/ppermute | solution.py:33
  27.5 4.9 %collective-permute-start = (f32[8,8,128]{2,1,0:T(8,128)S(1)}, f32[8,8,128]{2,1,0:T(8,128)S(1)}, u32[]{:S(2)}, u32[]{:S(2)}) collective-permute-start(f32[8,8,128]{2,1,0:T(8,128)S(1)} %get-tuple-element.45), channel_id=1, source_target_pairs={{0,16},{16,32},{32,48},{48,64},{64,80},{80,96},{96,112},{1,17},{17... | collective-permute-start | bytes 98312 | tf_op jit(solution)/shard_map/ppermute | solution.py:33
  32.4 11.0 %collective-permute-done.1.refs_9_.sn_e = f32[8,8,128]{2,1,0:T(8,128)S(1)} collective-permute-done((f32[8,8,128]{2,1,0:T(8,128)S(1)}, f32[8,8,128]{2,1,0:T(8,128)S(1)}, u32[]{:S(2)}, u32[]{:S(2)}) %collective-permute-start.1) | collective-permute-done | bytes 32800 | tf_op jit(solution)/shard_map/ppermute | solution.py:33
  43.4 0.0 collective-permute-done.refs_7_.sn_w
  43.4 0.6 all-to-all-done.refs_6_
  44.0 0.0 collective-permute-done.2.refs_10_.from_w
  44.0 0.0 collective-permute-done.3.refs_11_.from_e
  44.0 0.0 copy-done.1
  44.0 7.7 %strips.1 = (f32[60,96,128]{2,1,0:T(8,128)S(1)}, f32[60,96,128]{2,1,0:T(8,128)S(1)}, f32[60,96,128]{2,1,0:T(8,128)S(1)}, f32[60,96,128]{2,1,0:T(8,128)S(1)}, f32...) custom-call(f32[60,64,128]{2,1,0:T(8,128)} %refs_0_.1, ...), custom_call_target="tpu_custom_call" | custom-call | tf_op jit(solution)/shard_map/strips/pallas_call | solution.py:641
  51.7 6.1 %collective-permute-start.4 = (f32[61,24,128]{2,1,0:T(8,128)S(1)}, f32[61,24,128]{2,1,0:T(8,128)S(1)}, u32[]{:S(2)}, u32[]{:S(2)}) collective-permute-start(f32[61,24,128]{2,1,0:T(8,128)S(1)} %get-tuple-element.42), channel_id=1, source_target_pairs={{0,1},{1,2},{2,3},{3,4},{4,5},{5,6},{6,7},{7,8},{8,9},{9,10},{10,1... | collective-permute-start | bytes 2248712 | tf_op jit(solution)/shard_map/ppermute | solution.py:33
  57.8 1.9 %collective-permute-start.5 = (f32[61,24,128]{2,1,0:T(8,128)S(1)}, f32[61,24,128]{2,1,0:T(8,128)S(1)}, u32[]{:S(2)}, u32[]{:S(2)}) collective-permute-start(f32[61,24,128]{2,1,0:T(8,128)S(1)} %get-tuple-element.43), channel_id=1, source_target_pairs={{1,0},{2,1},{3,2},{4,3},{5,4},{6,5},{7,6},{8,7},{9,8},{10,9},{11,1... | collective-permute-start | bytes 2248712 | tf_op jit(solution)/shard_map/ppermute | solution.py:33
  59.7 3.1 %prep.1 = (f32[60,96,128]{2,1,0:T(8,128)S(1)}, f32[60,96,128]{2,1,0:T(8,128)S(1)}, f32[60,96,128]{2,1,0:T(8,128)S(1)}, f32[60,96,128]{2,1,0:T(8,128)S(1)}, f32[60,96,128]{2,1,0:T(8,128)S(1)}) custom-call(f32[60,96,128]{2,1,0:T(8,128)S(1)} %get-tuple-element.30.px, f32[60,96,128]{2,1,0:T(8,128)S(1)} %get-tuple-element.31.ux, ...), custom_call_target="tpu_custom_call" | custom-call | flops 20000000 | bytes 20000000 | tf_op jit(solution)/shard_map/prep/pallas_call | solution.py:668
  62.7 3.5 %collective-permute-done.4.from_s = f32[61,24,128]{2,1,0:T(8,128)S(1)} collective-permute-done((f32[61,24,128]{2,1,0:T(8,128)S(1)}, f32[61,24,128]{2,1,0:T(8,128)S(1)}, u32[]{:S(2)}, u32[]{:S(2)}) %collective-permute-start.4) | collective-permute-done | bytes 749600 | tf_op jit(solution)/shard_map/ppermute | solution.py:33
  66.3 8.0 %collective-permute-done.5.from_n = f32[61,24,128]{2,1,0:T(8,128)S(1)} collective-permute-done((f32[61,24,128]{2,1,0:T(8,128)S(1)}, f32[61,24,128]{2,1,0:T(8,128)S(1)}, u32[]{:S(2)}, u32[]{:S(2)}) %collective-permute-start.5) | collective-permute-done | bytes 749600 | tf_op jit(solution)/shard_map/ppermute | solution.py:33
  74.3 29.9 %substeps.1 = (f32[60,64,128]{2,1,0:T(8,128)}, f32[60,64,128]{2,1,0:T(8,128)}, f32[60,64,128]{2,1,0:T(8,128)}, f32[60,64,128]{2,1,0:T(8,128)}) custom-call(f32[60,96,128]{2,1,0:T(8,128)S(1)} %get-tuple-element.34.p0, f32[60,96,128]{2,1,0:T(8,128)S(1)} %get-tuple-element.35.u0, f32[60,96,128]{2,1,0:T(8,128)S(1)} %get-tuple-element.36.v0, ...), custom_call_target="tpu_custom_call" | custom-call | tf_op jit(solution)/shard_map/substeps/pallas_call | solution.py:686
  (18 shorter events, 0.1 us)
Async XLA Ops:
  0.6 2.9 %copy-start.3 = (f32[2,3,60,5,4]{2,4,3,1,0:T(4,128)S(1)}, f32[2,3,60,5,4]{2,4,3,1,0:T(4,128)}, u32[]{:S(2)}) copy-start(f32[2,3,60,5,4]{2,4,3,1,0:T(4,128)} %param.14) | copy-start | bytes 86404
  0.6 17.7 %copy-start.2 = (f32[2,3,60,5,16]{2,4,3,1,0:T(8,128)S(1)}, f32[2,3,60,5,16]{2,4,3,1,0:T(8,128)}, u32[]{:S(2)}) copy-start(f32[2,3,60,5,16]{2,4,3,1,0:T(8,128)} %param.13) | copy-start | bytes 345604
  3.5 40.5 %copy-start = (f32[64,128]{1,0:T(8,128)S(1)}, f32[64,128]{1,0:T(8,128)}, u32[]{:S(2)}) copy-start(f32[64,128]{1,0:T(8,128)} %coef.5) | copy-start | bytes 98308
  3.6 40.4 %copy-start.1 = (s32[64,128]{1,0:T(8,128)S(1)}, s32[64,128]{1,0:T(8,128)}, u32[]{:S(2)}) copy-start(s32[64,128]{1,0:T(8,128)} %width.3) | copy-start | bytes 98308
  4.6 15.8 %all-to-all-start.1 = ((f32[16,8,4,128]{3,2,1,0:T(4,128)}), f32[16,8,4,128]{3,2,1,0:T(4,128)S(1)}, u32[]{:S(2)}, u32[]{:S(2)}) async-start(f32[16,8,4,128]{3,2,1,0:T(4,128)} %pad_maximum_fusion.1), calls=%async_computation.1 | async-start | bytes 524288 | tf_op jit(solution)/shard_map/all_to_all | solution.py:50
  13.0 31.0 %collective-permute-start.2 = (f32[61,24,128]{2,1,0:T(8,128)}, f32[61,24,128]{2,1,0:T(8,128)S(1)}, u32[]{:S(2)}, u32[]{:S(2)}) collective-permute-start(f32[61,24,128]{2,1,0:T(8,128)} %get-tuple-element.28), channel_id=1, source_target_pairs={{0,16},{16,32},{32,48},{48,64},{64,80},{80,96},{96,112},{1,17},{17... | collective-permute-start | bytes 2248712 | tf_op jit(solution)/shard_map/ppermute | solution.py:33
  15.3 28.7 %collective-permute-start.3 = (f32[61,24,128]{2,1,0:T(8,128)S(1)}, f32[61,24,128]{2,1,0:T(8,128)S(1)}, u32[]{:S(2)}, u32[]{:S(2)}) collective-permute-start(f32[61,24,128]{2,1,0:T(8,128)S(1)} %get-tuple-element.29), channel_id=1, source_target_pairs={{16,0},{32,16},{48,32},{64,48},{80,64},{96,80},{112,96},{17,1},{33... | collective-permute-start | bytes 2248712 | tf_op jit(solution)/shard_map/ppermute | solution.py:33
  20.4 23.6 %all-to-all-start = ((f32[8,8,16,128]{3,2,1,0:T(8,128)}), f32[8,8,16,128]{3,2,1,0:T(8,128)S(1)}, u32[]{:S(2)}, u32[]{:S(2)}) async-start(f32[8,8,16,128]{3,2,1,0:T(8,128)} %pad_maximum_fusion), calls=%async_computation | async-start | bytes 1048576 | tf_op jit(solution)/shard_map/all_to_all | solution.py:50
  25.0 18.4 %collective-permute-start.1 = (f32[8,8,128]{2,1,0:T(8,128)S(1)}, f32[8,8,128]{2,1,0:T(8,128)S(1)}, u32[]{:S(2)}, u32[]{:S(2)}) collective-permute-start(f32[8,8,128]{2,1,0:T(8,128)S(1)} %get-tuple-element.44), channel_id=1, source_target_pairs={{16,0},{32,16},{48,32},{64,48},{80,64},{96,80},{112,96},{17,1},{33... | collective-permute-start | bytes 98312 | tf_op jit(solution)/shard_map/ppermute | solution.py:33
  27.5 15.9 %collective-permute-start = (f32[8,8,128]{2,1,0:T(8,128)S(1)}, f32[8,8,128]{2,1,0:T(8,128)S(1)}, u32[]{:S(2)}, u32[]{:S(2)}) collective-permute-start(f32[8,8,128]{2,1,0:T(8,128)S(1)} %get-tuple-element.45), channel_id=1, source_target_pairs={{0,16},{16,32},{32,48},{48,64},{64,80},{80,96},{96,112},{1,17},{17... | collective-permute-start | bytes 98312 | tf_op jit(solution)/shard_map/ppermute | solution.py:33
  51.7 14.6 %collective-permute-start.4 = (f32[61,24,128]{2,1,0:T(8,128)S(1)}, f32[61,24,128]{2,1,0:T(8,128)S(1)}, u32[]{:S(2)}, u32[]{:S(2)}) collective-permute-start(f32[61,24,128]{2,1,0:T(8,128)S(1)} %get-tuple-element.42), channel_id=1, source_target_pairs={{0,1},{1,2},{2,3},{3,4},{4,5},{5,6},{6,7},{7,8},{8,9},{9,10},{10,1... | collective-permute-start | bytes 2248712 | tf_op jit(solution)/shard_map/ppermute | solution.py:33
  57.8 16.5 %collective-permute-start.5 = (f32[61,24,128]{2,1,0:T(8,128)S(1)}, f32[61,24,128]{2,1,0:T(8,128)S(1)}, u32[]{:S(2)}, u32[]{:S(2)}) collective-permute-start(f32[61,24,128]{2,1,0:T(8,128)S(1)} %get-tuple-element.43), channel_id=1, source_target_pairs={{1,0},{2,1},{3,2},{4,3},{5,4},{6,5},{7,6},{8,7},{9,8},{10,9},{11,1... | collective-permute-start | bytes 2248712 | tf_op jit(solution)/shard_map/ppermute | solution.py:33
